TPU v7x, 8 devices: a whole 2x2x1 slice. The times are simulated.
8 devices in a mesh: batch: 1 (over z), dap: 8 (over y, x, core).
Axes of the slice: x: 2, y: 2, z: 1, core: 2. Of those that a mesh axis runs over, the one named last changes fastest.
Arguments:
- z_pair: bfloat16 [512, 512, 128], P(('batch', 'dap'))
- pair_mask: int32 [512, 512], P(('batch', 'dap'))
- dz_out: bfloat16 [512, 512, 128], P(('batch', 'dap'))
- ln_in_scale: bfloat16 [128], replicated
- ln_in_offset: bfloat16 [128], replicated
- w_in: bfloat16 [128, 512], replicated
- b_in: bfloat16 [512], replicated
- ln_out_scale: bfloat16 [128], replicated
- ln_out_offset: bfloat16 [128], replicated
- w_out: bfloat16 [128, 128], replicated
- b_out: bfloat16 [128], replicated
- w_gate: bfloat16 [128, 128], replicated
- b_gate: bfloat16 [128], replicated
Outputs:
- output 1: bfloat16 [512, 512, 128], P(('batch', 'dap'))
- output 2: bfloat16 [128], P('batch')
- output 3: bfloat16 [128], P('batch')
- output 4: bfloat16 [128, 512], P('batch')
- output 5: bfloat16 [512], P('batch')
- output 6: bfloat16 [128], P('batch')
- output 7: bfloat16 [128], P('batch')
- output 8: bfloat16 [128, 128], P('batch')
- output 9: bfloat16 [128], P('batch')
- output 10: bfloat16 [128, 128], P('batch')
- output 11: bfloat16 [128], P('batch')
All inputs are finite; a program needn't handle non-finite values.
Results may differ from a plain program's by a relative error of at most 0.0125153.
Values are sent between devices in bfloat16 or wider.
A program may use at most 1 GiB of HBM per device.

v0:
```python
import jax
import jax.numpy as jnp
from jax import lax
from jax.sharding import PartitionSpec as P

LN_EPS = 1e-5


def norm_forward(x_val, ln_scale, ln_offset, axis_id):
    mean_val = jnp.mean(x_val, axis=axis_id, keepdims=True)
    centered = x_val - mean_val
    inv_std = lax.rsqrt(jnp.mean(centered * centered, axis=axis_id, keepdims=True) + LN_EPS)
    x_hat = centered * inv_std
    return x_hat, inv_std, x_hat * ln_scale + ln_offset


def norm_backward(grad_out, x_hat, inv_std, ln_scale, axis_id):
    grad_hat = grad_out * ln_scale
    mean_grad = jnp.mean(grad_hat, axis=axis_id, keepdims=True)
    mean_proj = jnp.mean(grad_hat * x_hat, axis=axis_id, keepdims=True)
    return inv_std * (grad_hat - mean_grad - x_hat * mean_proj)


def input_side(z_part, mask_part, ln_in_scale, ln_in_offset, w_in, b_in):
    hidden = w_in.shape[1] // 4
    in_hat, in_inv, in_aff = norm_forward(z_part.astype(jnp.float32), ln_in_scale.astype(jnp.float32), ln_in_offset.astype(jnp.float32), -1)
    z_norm = in_aff.astype(jnp.bfloat16)
    proj_t = jnp.einsum('de,rnd->ern', w_in, z_norm, preferred_element_type=jnp.float32) + b_in.astype(jnp.float32)[:, None, None]
    proj_a = proj_t[:hidden]
    proj_b = proj_t[hidden:2 * hidden]
    sig_a = jax.nn.sigmoid(proj_t[2 * hidden:3 * hidden])
    sig_b = jax.nn.sigmoid(proj_t[3 * hidden:])
    mask_f = mask_part.astype(jnp.float32)[None]
    act_a = (mask_f * sig_a * proj_a).astype(jnp.bfloat16)
    act_b = (mask_f * sig_b * proj_b).astype(jnp.bfloat16)
    return in_hat, in_inv, z_norm, proj_a, proj_b, sig_a, sig_b, mask_f, act_a, act_b


def output_chain(tri_out, gate_lin, dy_part, ln_out_scale, ln_out_offset, w_out, b_out):
    out_scale = ln_out_scale.astype(jnp.float32)[:, None, None]
    out_offset = ln_out_offset.astype(jnp.float32)[:, None, None]
    out_hat, out_inv, out_aff = norm_forward(tri_out, out_scale, out_offset, 0)
    o_norm = out_aff.astype(jnp.bfloat16)
    update = (jnp.einsum('crn,cd->rnd', o_norm, w_out, preferred_element_type=jnp.float32) + b_out.astype(jnp.float32)).astype(jnp.bfloat16)
    sig_g = jax.nn.sigmoid(gate_lin)
    dy_f = dy_part.astype(jnp.float32)
    d_update = (sig_g * dy_f).astype(jnp.bfloat16)
    d_gate_lin = dy_f * update.astype(jnp.float32) * sig_g * (1.0 - sig_g)
    d_onorm = jnp.einsum('cd,rnd->crn', w_out, d_update, preferred_element_type=jnp.float32).astype(jnp.bfloat16).astype(jnp.float32)
    d_tri = norm_backward(d_onorm, out_hat, out_inv, out_scale, 0).astype(jnp.bfloat16)
    return d_tri, o_norm, out_hat, d_onorm, d_update, d_gate_lin


def input_backward(d_act_a, d_act_b, proj_a, proj_b, sig_a, sig_b, mask_f, z_norm, in_hat, in_inv, dy_part, d_gate_lin, ln_in_scale, w_in, w_gate):
    grad_a = d_act_a.astype(jnp.bfloat16).astype(jnp.float32) * mask_f
    grad_b = d_act_b.astype(jnp.bfloat16).astype(jnp.float32) * mask_f
    d_proj = jnp.concatenate([grad_a * sig_a, grad_b * sig_b, grad_a * proj_a * sig_a * (1.0 - sig_a), grad_b * proj_b * sig_b * (1.0 - sig_b)], axis=0)
    d_b_in = jnp.sum(d_proj, axis=(1, 2))
    d_b_gate = jnp.sum(d_gate_lin, axis=(0, 1))
    proj_grad16 = d_proj.astype(jnp.bfloat16)
    gate_grad16 = d_gate_lin.astype(jnp.bfloat16)
    d_w_in = jnp.einsum('rnd,ern->de', z_norm, proj_grad16, preferred_element_type=jnp.float32)
    d_w_gate = jnp.einsum('rnd,rne->de', z_norm, gate_grad16, preferred_element_type=jnp.float32)
    d_znorm = (jnp.einsum('ern,de->rnd', proj_grad16, w_in, preferred_element_type=jnp.float32) + jnp.einsum('rne,de->rnd', gate_grad16, w_gate, preferred_element_type=jnp.float32)).astype(jnp.bfloat16).astype(jnp.float32)
    d_in_scale = jnp.sum(d_znorm * in_hat, axis=(0, 1))
    d_in_offset = jnp.sum(d_znorm, axis=(0, 1))
    d_z = (dy_part.astype(jnp.float32) + norm_backward(d_znorm, in_hat, in_inv, ln_in_scale.astype(jnp.float32), -1)).astype(jnp.bfloat16)
    return d_z, d_in_scale, d_in_offset, d_w_in, d_b_in, d_w_gate, d_b_gate


def local_grads(z_loc, mask_loc, dy_loc, ln_in_scale, ln_in_offset, w_in, b_in, ln_out_scale, ln_out_offset, w_out, b_out, w_gate, b_gate):
    in_hat, in_inv, z_norm, proj_a, proj_b, sig_a, sig_b, mask_f, act_a, act_b = input_side(z_loc, mask_loc, ln_in_scale, ln_in_offset, w_in, b_in)
    gate_lin = jnp.einsum('rnd,de->rne', z_norm, w_gate, preferred_element_type=jnp.float32) + b_gate.astype(jnp.float32)
    b_full = lax.all_gather(act_b, 'dap', axis=1, tiled=True)
    tri_out = jnp.einsum('cik,cjk->cij', act_a, b_full, preferred_element_type=jnp.float32)
    d_tri, o_norm, out_hat, d_onorm, d_update, d_gate_lin = output_chain(tri_out, gate_lin, dy_loc, ln_out_scale, ln_out_offset, w_out, b_out)
    d_w_out = jnp.einsum('crn,rnd->cd', o_norm, d_update, preferred_element_type=jnp.float32)
    d_b_out = jnp.sum(d_update.astype(jnp.float32), axis=(0, 1))
    d_out_scale = jnp.sum(d_onorm * out_hat, axis=(1, 2))
    d_out_offset = jnp.sum(d_onorm, axis=(1, 2))
    d_act_a = jnp.einsum('cij,cjk->cik', d_tri, b_full, preferred_element_type=jnp.float32)
    d_b_part = jnp.einsum('cij,cik->cjk', d_tri, act_a, preferred_element_type=jnp.float32)
    d_act_b = lax.psum_scatter(d_b_part, 'dap', scatter_dimension=1, tiled=True)
    d_z, d_in_scale, d_in_offset, d_w_in, d_b_in, d_w_gate, d_b_gate = input_backward(d_act_a, d_act_b, proj_a, proj_b, sig_a, sig_b, mask_f, z_norm, in_hat, in_inv, dy_loc, d_gate_lin, ln_in_scale, w_in, w_gate)
    summed = lax.psum((d_in_scale, d_in_offset, d_w_in, d_b_in, d_out_scale, d_out_offset, d_w_out, d_b_out, d_w_gate, d_b_gate), 'dap')
    return (d_z,) + tuple(grad_piece.astype(jnp.bfloat16) for grad_piece in summed)


def solution(mesh):
    pair_spec = P(('batch', 'dap'), None, None)
    mask_spec = P(('batch', 'dap'), None)
    vec_rep = P(None)
    mat_rep = P(None, None)
    vec_part = P('batch')
    mat_part = P('batch', None)
    in_specs = (pair_spec, mask_spec, pair_spec, vec_rep, vec_rep, mat_rep, vec_rep, vec_rep, vec_rep, mat_rep, vec_rep, mat_rep, vec_rep)
    out_specs = (pair_spec, vec_part, vec_part, mat_part, vec_part, vec_part, vec_part, mat_part, vec_part, mat_part, vec_part)
    return jax.shard_map(local_grads, mesh=mesh, in_specs=in_specs, out_specs=out_specs, check_vma=False)
```

profile of v0, /device:TPU:0, one launch (start us, length us, event | category | flops | bytes accessed | tf_op | source)
XLA Modules:
  0.0 1603.3 jit_solution(11455289628336885861)
XLA Ops:
  7.2 0.0 copy-start
  7.2 0.0 all-gather.2.cloned.1.call-start
  7.2 0.7 convert_element_type.129
  7.9 0.7 convert_element_type.130
  8.6 0.7 convert_element_type.132
  9.3 0.9 convert_element_type.128
  10.2 5.7 convert_reduce_fusion.2
  15.9 10.8 fusion.22
  26.8 0.0 copy-start.7
  26.8 26.1 %add_bitcast_fusion = f32[512,64,512]{2,0,1:T(8,128)} fusion(f32[512]{0:T(512)S(1)} %convert_element_type.132, bf16[128,512]{1,0:T(8,128)(2,1)S(1)} %copy-done, bf16[64,512,128]{2,1,0:T(8,128)(2,1)} %param.13, f32[128]{0:T(128)S(1)} %convert_element_type.130, f32[128]{0:T(128)S(1)} %convert_element_type.129, f32[64,512]{1,0:T(8,128)S(1)} %add_rsqrt_fusion.1, ...), kind=kOutput, calls=%fused_computation.1 | convolution fusion | flops 4336910336 | bytes 75893760 | tf_op jit(solution)/shard_map/de,rnd->ern/dot_general | solution.py:28
  52.9 0.0 copy-start.27
  52.9 0.0 copy-start.23
  52.9 29.7 %multiply_convert_fusion.1 = (bf16[128,64,512]{2,0,1:T(8,128)(2,1)}, bf16[128,64,512]{2,0,1:T(8,128)(2,1)}) fusion(f32[512,64,512]{2,0,1:T(8,128)} %add_bitcast_fusion, f32[64,512]{1,0:T(8,128)S(1)} %convert_element_type.128), kind=kLoop, calls=%fused_computation.68 | loop fusion | flops 50331648 | bytes 84017152 | tf_op jit(solution)/shard_map/convert_element_type | solution.py:34
  82.6 0.0 all-gather.2.cloned.1.call-update
  82.6 0.0 reduce-scatter.2.cloned.1.call-start
  82.7 0.0 copy-start.11
  82.8 14.4 convert_reduce_fusion.3
  97.1 3.2 copy-done.4
  100.4 4.7 fusion.61
  105.0 12.5 copy.40
  117.6 265.2 %all-gather.2.cloned.1.call-done = bf16[128,512,512]{2,0,1:T(8,128)(2,1)} async-done(((bf16[128,64,512]{2,0,1:T(8,128)(2,1)}), bf16[128,512,512]{2,0,1:T(8,128)(2,1)}) %all-gather.2.cloned.1.call-update) | async-done | bytes 67108880 | tf_op jit(solution)/shard_map/all_gather | solution.py:74
  382.8 85.2 %fusion.72 = (f32[64,512]{1,0:T(8,128)S(1)}, f32[128,64,512]{2,1,0:T(8,128)}) fusion(bf16[128,512,512]{2,0,1:T(8,128)(2,1)} %all-gather.2.cloned.1.call-done, bf16[128,64,512]{2,0,1:T(8,128)(2,1)} %get-tuple-element.36), kind=kOutput, calls=%fused_computation.98 | convolution fusion | flops 4299128832 | bytes 92405760 | tf_op jit(solution)/shard_map/cik,cjk->cij/dot_general | solution.py:75
  468.0 8.1 multiply_reduce_fusion
  476.2 19.4 %fusion.27 = (f32[128]{0:T(128)}, f32[64,512]{1,0:T(8,128)S(1)}, f32[64,512]{1,0:T(8,128)S(1)}, bf16[128,64,512]{2,1,0:T(8,128)(2,1)}) fusion(bf16[64,512,128]{1,0,2:T(8,128)(2,1)} %copy.40, f32[128,64,512]{2,1,0:T(8,128)} %get-tuple-element.41, f32[64,512]{1,0:T(8,128)S(1)} %add_rsqrt_fusion, f32[64,512]{1,0:T(8,128)S(1)} %broadcast_multiply_fusion.4, ...), kind=kLoop, calls=%fused_computation.39 | loop fusion | flops 50265984 | bytes 34080256 | tf_op jit(solution)/shard_map/reduce_sum | solution.py:79
  495.6 6.8 fusion.25
  502.4 51.8 %fusion.45 = f32[128,512,512]{2,1,0:T(8,128)} fusion(bf16[128,64,512]{2,1,0:T(8,128)(2,1)} %fusion.25, bf16[128,64,512]{2,0,1:T(8,128)(2,1)} %get-tuple-element.36), kind=kOutput, calls=%fused_computation.73 | convolution fusion | flops 4294967296 | bytes 150994944 | tf_op jit(solution)/shard_map/cij,cik->cjk/dot_general | solution.py:82
  554.2 109.2 %copy.44 = f32[128,512,512]{2,0,1:T(8,128)} copy(f32[128,512,512]{2,1,0:T(8,128)} %fusion.45) | data formatting | bytes 268435456 | tf_op jit(solution)/shard_map/cij,cik->cjk/dot_general | solution.py:82
  663.5 0.0 reduce-scatter.2.cloned.1.call-update
  663.5 0.6 copy-done.28
  664.1 5.4 convert_reduce_fusion.1
  669.5 24.7 %fusion.73 = (f32[128]{0:T(128)}, bf16[64,512,128]{2,1,0:T(8,128)(2,1)}) fusion(f32[64,512,128]{2,1,0:T(8,128)} %get-tuple-element.39, f32[128]{0:T(128)S(1)} %convert_element_type.149, bf16[128,128]{1,0:T(8,128)(2,1)S(1)} %copy-done.12, bf16[128,64,512]{2,1,0:T(8,128)(2,1)} %get-tuple-element.38, bf16[64,512,128]{2,1,0:T(8,128)(2,1)} %param.15), kind=kOutput, calls=%fused_computation.99 | convolution fusion | flops 1115684736 | bytes 41976832 | tf_op jit(solution)/shard_map/crn,cd->rnd/dot_general | solution.py:44
  694.2 0.0 copy-start.18
  694.2 0.0 slice-start.1
  694.3 16.1 %fusion.54 = f32[128,128]{1,0:T(8,128)} fusion(bf16[64,512,128]{2,1,0:T(8,128)(2,1)} %copy-done.4, bf16[128,64,512]{2,1,0:T(8,128)(2,1)} %get-tuple-element.38), kind=kOutput, calls=%fused_computation.81 | convolution fusion | flops 1073741824 | bytes 16842752 | tf_op jit(solution)/shard_map/crn,rnd->cd/dot_general | solution.py:77
  710.5 15.8 fusion.51
  726.3 104.6 %fusion = bf16[128,64,512]{2,1,0:T(8,128)(2,1)} fusion(bf16[128,64,512]{2,1,0:T(8,128)(2,1)S(1)} %bitcast.66, bf16[128,512,512]{2,0,1:T(8,128)(2,1)} %all-gather.2.cloned.1.call-done), kind=kOutput, calls=%fused_computation.2 | convolution fusion | flops 4294967296 | bytes 83886080 | tf_op jit(solution)/shard_map/cij,cjk->cik/dot_general | solution.py:81
  831.0 564.5 %reduce-scatter.2.cloned.1.call-done = f32[128,64,512]{2,0,1:T(8,128)} async-done(((f32[128,512,512]{2,0,1:T(8,128)}), f32[128,64,512]{2,0,1:T(8,128)}) %reduce-scatter.2.cloned.1.call-update) | async-done | bytes 16777232 | tf_op jit(solution)/shard_map/reduce_scatter | solution.py:83
  1395.5 52.5 %fusion.41 = (f32[128,64,512]{2,0,1:T(8,128)}, f32[128,64,512]{2,0,1:T(8,128)}, f32[128,64,512]{2,0,1:T(8,128)}, f32[128,64,512]{2,0,1:T(8,128)}) fusion(f32[64,512]{1,0:T(8,128)S(1)} %copy-done.10, bf16[128,64,512]{2,1,0:T(8,128)(2,1)} %fusion, f32[512,64,512]{2,0,1:T(8,128)} %add_bitcast_fusion, f32[128,64,512]{2,0,1:T(8,128)} %reduce-scatter.2.cloned.1.call-done), kind=kLoop, calls=%fused_computation.64 | loop fusion | flops 88080384 | bytes 159514624 | tf_op jit(solution)/shard_map/mul | solution.py:57
  1448.0 20.7 %fusion.4 = f32[512]{0:T(512)S(1)} fusion(f32[128,64,512]{2,0,1:T(8,128)} %get-tuple-element.34, f32[128,64,512]{2,0,1:T(8,128)} %get-tuple-element.33, f32[128,64,512]{2,0,1:T(8,128)} %get-tuple-element.35, f32[128,64,512]{2,0,1:T(8,128)} %get-tuple-element.32), kind=kLoop, calls=%fused_computation.6 | loop fusion | flops 67108352 | bytes 67110912 | tf_op jit(solution)/shard_map/reduce_sum | solution.py:58
  1468.6 28.5 %convolution_bitcast_fusion = f32[128,512]{1,0:T(8,128)S(1)} fusion(bf16[64,512,128]{2,1,0:T(8,128)(2,1)} %param.13, f32[128]{0:T(128)S(1)} %copy-done.18, f32[128]{0:T(128)S(1)} %copy-done.16, f32[64,512]{1,0:T(8,128)S(1)} %copy-done.8, f32[64,512]{1,0:T(8,128)S(1)} %copy-done.6, f32[128,64,512]{2,0,1:T(8,128)} %get-tuple-element.34, ...), kind=kOutput, calls=%fused_computation.79 | convolution fusion | flops 4454350848 | bytes 76022784 | tf_op jit(solution)/shard_map/rnd,ern->de/dot_general | solution.py:62
  1497.2 28.3 %fusion.57 = f32[64,512,128]{2,1,0:T(8,128)} fusion(bf16[128,512]{1,0:T(8,128)(2,1)S(1)} %copy-done, f32[128,64,512]{2,0,1:T(8,128)} %get-tuple-element.34, f32[128,64,512]{2,0,1:T(8,128)} %get-tuple-element.33, f32[128,64,512]{2,0,1:T(8,128)} %get-tuple-element.35, f32[128,64,512]{2,0,1:T(8,128)} %get-tuple-element.32), kind=kOutput, calls=%fused_computation.82 | convolution fusion | flops 4429185024 | bytes 84017152 | tf_op jit(solution)/shard_map/ern,de->rnd/dot_general | solution.py:64
  1525.5 0.0 copy-start.3
  1525.5 21.7 %fusion.33 = (f32[128]{0:T(128)S(1)}, f32[64,512]{1,0:T(8,128)S(1)}, f32[64,512]{1,0:T(8,128)S(1)}, f32[128]{0:T(128)S(1)}, bf16[64,512,128]{2,1,0:T(8,128)(2,1)S(1)}) fusion(bf16[64,512,128]{2,1,0:T(8,128)(2,1)} %param.13, f32[64,512]{1,0:T(8,128)S(1)} %copy-done.8, f32[64,512]{1,0:T(8,128)S(1)} %copy-done.6, f32[128]{0:T(128)S(1)} %copy-done.16, ...), kind=kOutput, calls=%fused_computation.45 | convolution fusion | flops 1128201984 | bytes 42501632 | tf_op jit(solution)/shard_map/rne,de->rnd/dot_general | solution.py:64
  1547.3 0.0 copy-start.19
  1547.3 0.0 copy-start.20
  1547.3 0.0 copy-start.22
  1547.3 20.8 %fusion.32 = bf16[64,512,128]{2,1,0:T(8,128)(2,1)} fusion(bf16[64,512,128]{2,1,0:T(8,128)(2,1)S(1)} %copy-done.1, bf16[64,512,128]{2,1,0:T(8,128)(2,1)S(1)} %get-tuple-element.42, bf16[64,512,128]{2,1,0:T(8,128)(2,1)S(1)} %copy-done.3, f32[64,512]{1,0:T(8,128)S(1)} %broadcast_multiply_fusion, f32[64,512]{1,0:T(8,128)S(1)} %broadcast_multiply_fusion.1, ...), kind=kLoop, calls=%fused_computation.44 | loop fusion | flops 50331648 | bytes 34079232 | tf_op jit(solution)/shard_map/convert_element_type | solution.py:67
  1568.2 27.8 %all-reduce.2 = (bf16[128]{0:T(256)(128)(2,1)}, bf16[128]{0:T(256)(128)(2,1)}, bf16[128,512]{1,0:T(8,128)(2,1)}, bf16[512]{0:T(512)(128)(2,1)}, bf16[128]{0:T(25...) all-reduce(f32[128]{0:T(128)S(1)} %get-tuple-element.13, ...), channel_id=1, replica_groups=mesh['batch'=1,'dap'=8] {'dap'}, use_global_device_ids=true, to_apply=%region_10.0 | all-reduce | flops 99584 | bytes 597504 | tf_op jit(solution)/shard_map/psum | solution.py:85
  (76 shorter events, 0.3 us)
Async XLA Ops:
  7.2 19.6 %copy-start = (bf16[128,512]{1,0:T(8,128)(2,1)S(1)}, bf16[128,512]{1,0:T(8,128)(2,1)}, u32[]{:S(2)}) copy-start(bf16[128,512]{1,0:T(8,128)(2,1)} %param.18) | copy-start | bytes 393220
  7.2 375.6 %all-gather.2.cloned.1.call-start = ((), (), s32[]{:S(2)}) async-start(), calls=%async_computation.1 | async-start | bytes 75497472 | tf_op jit(solution)/shard_map/all_gather | solution.py:74
  7.9 74.8 %copy-start.15 = (f32[128]{0:T(128)}, f32[128]{0:T(128)S(1)}, u32[]{:S(2)}) copy-start(f32[128]{0:T(128)S(1)} %convert_element_type.129) | copy-start | bytes 1540
  8.6 74.1 %copy-start.17 = (f32[128]{0:T(128)}, f32[128]{0:T(128)S(1)}, u32[]{:S(2)}) copy-start(f32[128]{0:T(128)S(1)} %convert_element_type.130) | copy-start | bytes 1540
  10.2 42.7 %copy-start.9 = (f32[64,512]{1,0:T(8,128)}, f32[64,512]{1,0:T(8,128)S(1)}, u32[]{:S(2)}) copy-start(f32[64,512]{1,0:T(8,128)S(1)} %convert_element_type.128) | copy-start | bytes 393220
  15.9 66.8 %copy-start.5 = (f32[64,512]{1,0:T(8,128)}, f32[64,512]{1,0:T(8,128)S(1)}, u32[]{:S(2)}) copy-start(f32[64,512]{1,0:T(8,128)S(1)} %broadcast_multiply_fusion.5) | copy-start | bytes 393220
  26.8 56.0 %copy-start.7 = (f32[64,512]{1,0:T(8,128)}, f32[64,512]{1,0:T(8,128)S(1)}, u32[]{:S(2)}) copy-start(f32[64,512]{1,0:T(8,128)S(1)} %add_rsqrt_fusion.1) | copy-start | bytes 393220
  52.9 29.8 %copy-start.25 = (bf16[128]{0:T(256)(128)(2,1)S(1)}, bf16[128]{0:T(256)(128)(2,1)}, u32[]{:S(2)}) copy-start(bf16[128]{0:T(256)(128)(2,1)} %param.20) | copy-start | bytes 772
  52.9 29.8 %copy-start.26 = (bf16[128]{0:T(256)(128)(2,1)S(1)}, bf16[128]{0:T(256)(128)(2,1)}, u32[]{:S(2)}) copy-start(bf16[128]{0:T(256)(128)(2,1)} %param.21) | copy-start | bytes 772
  52.9 29.8 %copy-start.27 = (bf16[128]{0:T(256)(128)(2,1)S(1)}, bf16[128]{0:T(256)(128)(2,1)}, u32[]{:S(2)}) copy-start(bf16[128]{0:T(256)(128)(2,1)} %param.25) | copy-start | bytes 772
  52.9 29.8 %copy-start.23 = (bf16[128,128]{1,0:T(8,128)(2,1)S(1)}, bf16[128,128]{1,0:T(8,128)(2,1)}, u32[]{:S(2)}) copy-start(bf16[128,128]{1,0:T(8,128)(2,1)} %param.24) | copy-start | bytes 98308
  82.6 1312.9 %reduce-scatter.2.cloned.1.call-start = ((), (), s32[]{:S(2)}) async-start(), calls=%async_computation.2 | async-start | bytes 150994944 | tf_op jit(solution)/shard_map/reduce_scatter | solution.py:83
  82.7 17.6 %copy-start.11 = (bf16[128,128]{1,0:T(8,128)(2,1)S(1)}, bf16[128,128]{1,0:T(8,128)(2,1)}, u32[]{:S(2)}) copy-start(bf16[128,128]{1,0:T(8,128)(2,1)} %param.22) | copy-start | bytes 98308
  97.1 3.2 copy-start.4
  468.0 27.6 %slice-start.2 = ((s8[8388608]{0:T(1024)(128)(4,1)}), s8[4194304]{0:T(1024)(128)(4,1)S(1)}, s32[]{:S(2)}) async-start(s8[8388608]{0:T(1024)(128)(4,1)} %bitcast.63), calls=%async_computation.5 | async-start | bytes 8388608
  476.2 19.4 %copy-start.2 = (f32[128,64,512]{2,1,0:T(8,128)S(1)}, f32[128,64,512]{2,1,0:T(8,128)}, u32[]{:S(2)}) copy-start(f32[128,64,512]{2,1,0:T(8,128)} %get-tuple-element.41) | copy-start | bytes 50331652
  476.2 19.4 %slice-start.3 = ((s8[8388608]{0:T(1024)(128)(4,1)}), s8[4194304]{0:T(1024)(128)(4,1)S(1)}, s32[]{:S(2)}) async-start(s8[8388608]{0:T(1024)(128)(4,1)} %bitcast.63), calls=%async_computation.6 | async-start | bytes 8388608
  663.4 0.7 copy-start.28
  663.4 6.0 copy-start.12
  694.2 16.2 %slice-start = ((s8[8388608]{0:T(1024)(128)(4,1)}), s8[4194304]{0:T(1024)(128)(4,1)S(1)}, s32[]{:S(2)}) async-start(s8[8388608]{0:T(1024)(128)(4,1)} %bitcast.61), calls=%async_computation.3 | async-start | bytes 8388608
  694.2 16.2 %slice-start.6 = ((s8[8388608]{0:T(1024)(128)(4,1)}), s8[4194304]{0:T(1024)(128)(4,1)S(1)}, s32[]{:S(2)}) async-start(s8[8388608]{0:T(1024)(128)(4,1)} %bitcast.67), calls=%async_computation.9 | async-start | bytes 8388608
  694.2 16.2 %copy-start.6 = (f32[64,512]{1,0:T(8,128)S(1)}, f32[64,512]{1,0:T(8,128)}, u32[]{:S(2)}) copy-start(f32[64,512]{1,0:T(8,128)} %copy-done.5) | copy-start | bytes 393220
  694.2 16.2 %copy-start.8 = (f32[64,512]{1,0:T(8,128)S(1)}, f32[64,512]{1,0:T(8,128)}, u32[]{:S(2)}) copy-start(f32[64,512]{1,0:T(8,128)} %copy-done.7) | copy-start | bytes 393220
  694.2 16.2 %copy-start.16 = (f32[128]{0:T(128)S(1)}, f32[128]{0:T(128)}, u32[]{:S(2)}) copy-start(f32[128]{0:T(128)} %copy-done.15) | copy-start | bytes 1540
  694.2 16.2 %copy-start.18 = (f32[128]{0:T(128)S(1)}, f32[128]{0:T(128)}, u32[]{:S(2)}) copy-start(f32[128]{0:T(128)} %copy-done.17) | copy-start | bytes 1540
  694.2 16.2 %slice-start.1 = ((s8[8388608]{0:T(1024)(128)(4,1)}), s8[4194304]{0:T(1024)(128)(4,1)S(1)}, s32[]{:S(2)}) async-start(s8[8388608]{0:T(1024)(128)(4,1)} %bitcast.61), calls=%async_computation.4 | async-start | bytes 8388608
  694.2 16.2 %slice-start.7 = ((s8[8388608]{0:T(1024)(128)(4,1)}), s8[4194304]{0:T(1024)(128)(4,1)S(1)}, s32[]{:S(2)}) async-start(s8[8388608]{0:T(1024)(128)(4,1)} %bitcast.67), calls=%async_computation.10 | async-start | bytes 8388608
  694.2 32.1 %slice-start.4 = ((s8[8388608]{0:T(1024)(128)(4,1)}), s8[4194304]{0:T(1024)(128)(4,1)S(1)}, s32[]{:S(2)}) async-start(s8[8388608]{0:T(1024)(128)(4,1)} %bitcast.65), calls=%async_computation.7 | async-start | bytes 8388608
  710.5 15.8 slice-start.5
  726.3 669.1 %copy-start.10 = (f32[64,512]{1,0:T(8,128)S(1)}, f32[64,512]{1,0:T(8,128)}, u32[]{:S(2)}) copy-start(f32[64,512]{1,0:T(8,128)} %copy-done.9) | copy-start | bytes 393220
  1497.2 28.3 %copy-start.24 = (bf16[128,128]{1,0:T(8,128)(2,1)S(1)}, bf16[128,128]{1,0:T(8,128)(2,1)}, u32[]{:S(2)}) copy-start(bf16[128,128]{1,0:T(8,128)(2,1)} %param.24) | copy-start | bytes 98308
  1525.5 21.8 %copy-start.1 = (bf16[64,512,128]{2,1,0:T(8,128)(2,1)S(1)}, bf16[64,512,128]{2,1,0:T(8,128)(2,1)}, u32[]{:S(2)}) copy-start(bf16[64,512,128]{2,1,0:T(8,128)(2,1)} %param.13) | copy-start | bytes 25165828
  1525.5 21.8 %copy-start.3 = (bf16[64,512,128]{2,1,0:T(8,128)(2,1)S(1)}, bf16[64,512,128]{2,1,0:T(8,128)(2,1)}, u32[]{:S(2)}) copy-start(bf16[64,512,128]{2,1,0:T(8,128)(2,1)} %param.15) | copy-start | bytes 25165828
  1547.2 20.9 %copy-start.13 = (f32[128,128]{1,0:T(8,128)S(1)}, f32[128,128]{1,0:T(8,128)}, u32[]{:S(2)}) copy-start(f32[128,128]{1,0:T(8,128)} %fusion.54) | copy-start | bytes 196612
  1547.2 20.9 %copy-start.14 = (f32[128,128]{1,0:T(8,128)S(1)}, f32[128,128]{1,0:T(8,128)}, u32[]{:S(2)}) copy-start(f32[128,128]{1,0:T(8,128)} %fusion.51) | copy-start | bytes 196612
  1547.3 20.9 %copy-start.19 = (f32[128]{0:T(128)S(1)}, f32[128]{0:T(128)}, u32[]{:S(2)}) copy-start(f32[128]{0:T(128)} %convert_reduce_fusion.1) | copy-start | bytes 1540
  1547.3 20.9 %copy-start.20 = (f32[128]{0:T(128)S(1)}, f32[128]{0:T(128)}, u32[]{:S(2)}) copy-start(f32[128]{0:T(128)} %get-tuple-element.11) | copy-start | bytes 1540
  1547.3 20.9 %copy-start.21 = (f32[128]{0:T(128)S(1)}, f32[128]{0:T(128)}, u32[]{:S(2)}) copy-start(f32[128]{0:T(128)} %get-tuple-element.43) | copy-start | bytes 1540
  1547.3 20.9 %copy-start.22 = (f32[128]{0:T(128)S(1)}, f32[128]{0:T(128)}, u32[]{:S(2)}) copy-start(f32[128]{0:T(128)} %get-tuple-element.28) | copy-start | bytes 1540
Sparse Core Ops, SparseCore 0:
  82.7 300.0 all-gather.1
  663.6 731.8 reduce-scatter.1
where the time goes:
time: 1610 us; the launch traced here: 1600 us
  waiting for transfers between devices  830 us (52%)
  matrix products  422 us (26%)
  other arithmetic  183 us (11%)
  local copies, waits for them, and re-layouts  126 us (8%)
  blocking collectives  27.8 us (2%)
    reduce_scatter x1, waiting for transfers between devices, local_grads(): d_act_b = lax.psum_scatter(d_b_part, 'dap', scatter_dimension=1, tiled=True)  565 us
    all_gather x1, waiting for transfers between devices, local_grads(): b_full = lax.all_gather(act_b, 'dap', axis=1, tiled=True)  265 us
    dot_general x1, local copies, waits for them, and re-layouts, local_grads(): jnp.einsum('cij,cik->cjk', d_tri, act_a, preferred_element_type=jnp.float32)  109 us
    dot_general x1, matrix products, local_grads(): jnp.einsum('cij,cjk->cik', d_tri, b_full, preferred_element_type=jnp.floa...  105 us
    dot_general x1, matrix products, local_grads(): jnp.einsum('cik,cjk->cij', act_a, b_full, preferred_element_type=jnp.floa...  85.2 us
    mul x1, other arithmetic, input_backward(): grad_a * sig_a  52.5 us
    dot_general x1, matrix products, local_grads(): jnp.einsum('cij,cik->cjk', d_tri, act_a, preferred_element_type=jnp.float32)  51.8 us
  transfers between devices with their start and end apart: 2, of which 2 were waited for; matrix products, arithmetic and copies ran while one was open for 12% of the time, Pallas kernels for 0%

commit v1 on v0

v1 whole, which is shorter than its diff:
```python
import jax
import jax.numpy as jnp
from jax import lax
from jax.experimental import pallas as pl
from jax.experimental.pallas import tpu as pltpu
from jax.sharding import PartitionSpec as P

LN_EPS = 1e-5
N = 512
C = 128
NR = 64
NB = 16
NQ = NR // NB
HALF = NR // 2
HOPS = ((0, 0), (2, 4), (6, 6), (4, 2))
SB = NB + 8
SO = NR + 8
F32 = jnp.float32
BF16 = jnp.bfloat16
VMEM_LIMIT = 60 * 1024 * 1024


def sds(shape, dtype):
    return jax.ShapeDtypeStruct(shape, dtype)


def full_spec(shape):
    return pl.BlockSpec(shape, lambda *ids: (0,) * len(shape))


def sigmoid(x_val):
    return 1.0 / (1.0 + jnp.exp(-x_val))


def nt_dot(lhs, rhs):
    return lax.dot_general(lhs, rhs, (((1,), (1,)), ((), ())), preferred_element_type=F32)


def nn_dot(lhs, rhs):
    return lax.dot_general(lhs, rhs, (((1,), (0,)), ((), ())), preferred_element_type=F32)


def ones_rows(width):
    return jnp.where(lax.broadcasted_iota(jnp.int32, (16, width), 0) == 0, 1.0, 0.0).astype(BF16)


def norm_rows(x_val):
    mean_val = jnp.mean(x_val, axis=0, keepdims=True)
    centered = x_val - mean_val
    inv_std = lax.rsqrt(jnp.mean(centered * centered, axis=0, keepdims=True) + LN_EPS)
    return centered * inv_std, inv_std


def put_row(scr, row, pitch, val):
    for lane in range(val.shape[1] // 128):
        scr[lane, pl.ds(row, C, stride=pitch), :] = val[:, 128 * lane:128 * (lane + 1)]


def get_row(scr, row, pitch):
    return jnp.concatenate([scr[lane, pl.ds(row, C, stride=pitch), :] for lane in range(scr.shape[0])], axis=1)


def flush_rows(scr, out_ref, pitch):
    rows = out_ref.shape[1]

    def body(ch, carry):
        base = pl.multiple_of(ch * pitch, 8)
        for lane in range(scr.shape[0]):
            out_ref[ch, :, 128 * lane:128 * (lane + 1)] = scr[lane, pl.ds(base, rows), :].astype(BF16)
        return carry

    lax.fori_loop(0, C, body, 0, unroll=8)


def pair_row(ref, row, ids_ref):
    return jnp.concatenate([ref[row, pl.ds(pl.multiple_of(ids_ref[p], HALF), HALF), :] for p in range(16)], axis=0)


def normed_row(z_row, scale, offset):
    z_t = z_row.T.astype(F32)
    x_hat, inv_std = norm_rows(z_t)
    z_norm = (x_hat * scale + offset).astype(BF16)
    return x_hat, inv_std, z_norm


def pass_ids(ids_ref, tok_ref):
    for p in range(17):
        tok_ref[p] = ids_ref[p]


TOKEN = sds((17,), jnp.int32)
TOKEN_SPEC = pl.BlockSpec(memory_space=pltpu.SMEM)


def load_mask(m_ref, m_scr, ids_ref):
    m_scr[...] = pair_row(m_ref, 0, ids_ref).astype(F32).T


def gated_kernel(ids_ref, z_ref, m_ref, w_ref, scale_ref, offset_ref, a_ref, b_ref, tok_ref, a_scr, b_scr, m_scr):
    pass_ids(ids_ref, tok_ref)
    load_mask(m_ref, m_scr, ids_ref)
    first = pl.program_id(0) * NB

    def body(row, carry):
        _, _, z_norm = normed_row(pair_row(z_ref, row, ids_ref), scale_ref[...], offset_ref[...])
        aug = jnp.concatenate([z_norm, ones_rows(N)], axis=0)
        mask_f = m_scr[pl.ds(first + row, 1), :]
        for side, scr in ((0, a_scr), (1, b_scr)):
            proj = nn_dot(w_ref[side * C:(side + 1) * C], aug)
            sig = sigmoid(nn_dot(w_ref[(2 + side) * C:(3 + side) * C], aug))
            put_row(scr, row, SB, mask_f * sig * proj)
        return carry

    lax.fori_loop(0, NB, body, 0, unroll=4)
    flush_rows(a_scr, a_ref, SB)
    flush_rows(b_scr, b_ref, SB)


def gated_call(ids, piece, w_t, scale, offset):
    out_spec = pl.BlockSpec((C, NB, N), lambda r, ids: (0, r, 0))
    return pl.pallas_call(
        gated_kernel,
        grid_spec=pltpu.PrefetchScalarGridSpec(
            num_scalar_prefetch=1,
            grid=(HALF // NB,),
            in_specs=[
                pl.BlockSpec((NB, N, C), lambda r, ids: (r, 0, 0)),
                pl.BlockSpec((1, N, C), lambda r, ids: (HALF, 0, 0)),
                full_spec((4 * C, C + 16)), full_spec((C, N)), full_spec((C, N)),
            ],
            out_specs=[out_spec, out_spec, TOKEN_SPEC],
            scratch_shapes=[pltpu.VMEM((4, C * SB, 128), F32)] * 2 + [pltpu.VMEM((C, N), F32)],
        ),
        out_shape=[sds((C, HALF, N), BF16)] * 2 + [TOKEN],
        compiler_params=pltpu.CompilerParams(vmem_limit_bytes=VMEM_LIMIT),
        cost_estimate=pl.CostEstimate(flops=2 * 32 * 512 * 144 * 512, bytes_accessed=12 << 20, transcendentals=1 << 22),
        name="gated_rows",
    )(ids, piece, piece, w_t, scale, offset)


def lanes(val):
    return val[:, :128] + val[:, 128:256] + (val[:, 256:384] + val[:, 384:])


def own_kernel(ids_ref, z_ref, dy_ref, m_ref, w_ref, scale_ref, offset_ref, w_out_ref,
               a_ref, b_ref, dup_ref, don_ref, g1_ref, dbout_ref, dooff_ref, tok_ref, a_scr, b_scr, m_scr):
    pass_ids(ids_ref, tok_ref)

    @pl.when(pl.program_id(0) == 0)
    def _():
        dbout_ref[...] = jnp.zeros_like(dbout_ref)
        dooff_ref[...] = jnp.zeros_like(dooff_ref)

    load_mask(m_ref, m_scr, ids_ref)
    first = pl.program_id(0) % 2 * NB

    def body(row, carry):
        _, _, z_norm = normed_row(pair_row(z_ref, row, ids_ref), scale_ref[...], offset_ref[...])
        aug = jnp.concatenate([z_norm, ones_rows(N)], axis=0)
        mask_f = m_scr[pl.ds(first + row, 1), :]
        for side, scr in ((0, a_scr), (1, b_scr)):
            proj = nn_dot(w_ref[side * C:(side + 1) * C], aug)
            sig = sigmoid(nn_dot(w_ref[(2 + side) * C:(3 + side) * C], aug))
            put_row(scr, row, SB, mask_f * sig * proj)
        sig_g = sigmoid(nn_dot(w_ref[4 * C:5 * C], aug))
        dy_t = pair_row(dy_ref, row, ids_ref).T.astype(F32)
        d_upd = sig_g * dy_t
        g1_ref[row] = d_upd * (1.0 - sig_g)
        d_upd16 = d_upd.astype(BF16)
        dup_ref[row] = d_upd16
        d_onorm = nn_dot(w_out_ref[...], d_upd16).astype(BF16)
        don_ref[row] = d_onorm
        dbout_ref[...] += lanes(d_upd16.astype(F32))
        dooff_ref[...] += lanes(d_onorm.astype(F32))
        return carry

    lax.fori_loop(0, NB, body, 0, unroll=2)
    flush_rows(a_scr, a_ref, SB)
    flush_rows(b_scr, b_ref, SB)


def own_call(ids, z_loc, dy_loc, m_loc, w_t, scale, offset, w_out):
    row_spec = pl.BlockSpec((NB, N, C), lambda r, ids: (r, 0, 0))
    t_spec = pl.BlockSpec((NB, C, N), lambda r, ids: (r, 0, 0))
    act_spec = pl.BlockSpec((C, NB, N), lambda r, ids: (0, r, 0))
    return pl.pallas_call(
        own_kernel,
        grid_spec=pltpu.PrefetchScalarGridSpec(
            num_scalar_prefetch=1,
            grid=(NQ,),
            in_specs=[row_spec, row_spec, pl.BlockSpec((1, N, C), lambda r, ids: (r // 2, 0, 0)),
                      full_spec((5 * C, C + 16)), full_spec((C, N)), full_spec((C, N)), full_spec((C, C))],
            out_specs=[act_spec, act_spec, t_spec, t_spec, t_spec, full_spec((C, 128)), full_spec((C, 128)), TOKEN_SPEC],
            scratch_shapes=[pltpu.VMEM((4, C * SB, 128), F32)] * 2 + [pltpu.VMEM((C, N), F32)],
        ),
        out_shape=[sds((C, NR, N), BF16), sds((C, NR, N), BF16), sds((NR, C, N), BF16), sds((NR, C, N), BF16), sds((NR, C, N), F32), sds((C, 128), F32), sds((C, 128), F32), TOKEN],
        compiler_params=pltpu.CompilerParams(vmem_limit_bytes=VMEM_LIMIT),
        cost_estimate=pl.CostEstimate(flops=2 * 64 * 512 * 144 * 512, bytes_accessed=64 << 20, transcendentals=1 << 23),
        name="own_rows",
    )(ids, z_loc, dy_loc, m_loc, w_t, scale, offset, w_out)


CB = 16


def out_kernel(ids_ref, a_ref, b_own0, b_own1, b_par0, b_par1, don_ref, dup_ref, g1_ref, w_out_ref, scale_ref, offset_ref,
               do_ref, dg_ref, same0, same1, cross0, cross1, dwout_ref, dosc_ref, dbg_ref, tok_ref, o_scr):
    pass_ids(ids_ref, tok_ref)
    step = pl.program_id(0)
    first_core = ids_ref[16] == 0

    def prod(ch, carry):
        base = pl.multiple_of((step * CB + ch) * SO, 8)
        own = jnp.concatenate([b_own0[ch], b_own1[ch]], axis=0)
        par = jnp.concatenate([b_par0[ch], b_par1[ch]], axis=0)
        val = nt_dot(a_ref[ch], jnp.concatenate([own, par], axis=0))
        o_scr[0, pl.ds(base, NR), :] = jnp.where(first_core, val, pltpu.roll(val, 64, 1))
        return carry

    lax.fori_loop(0, CB, prod, 0, unroll=8)

    @pl.when(step == C // CB - 1)
    def _():
        dwout_ref[...] = jnp.zeros_like(dwout_ref)
        dosc_ref[...] = jnp.zeros_like(dosc_ref)
        dbg_ref[...] = jnp.zeros_like(dbg_ref)

        def chain(row, carry):
            o_hat, inv_std = norm_rows(get_row(o_scr, row, SO))
            o_norm = (o_hat * scale_ref[...] + offset_ref[...]).astype(BF16)
            aug = jnp.concatenate([o_norm, ones_rows(128)], axis=0)
            upd = nn_dot(w_out_ref[...], aug).astype(BF16).astype(F32)
            d_gate = g1_ref[row] * upd
            dbg_ref[...] += d_gate
            dg_ref[row] = d_gate.astype(BF16)
            d_onorm = don_ref[row].astype(F32)
            dosc_ref[...] += d_onorm * o_hat
            grad_hat = d_onorm * scale_ref[...]
            mean_grad = jnp.mean(grad_hat, axis=0, keepdims=True)
            mean_proj = jnp.mean(grad_hat * o_hat, axis=0, keepdims=True)
            put_row(o_scr, row, SO, inv_std * (grad_hat - mean_grad - o_hat * mean_proj))
            dwout_ref[...] += nt_dot(o_norm, dup_ref[row])
            return carry

        lax.fori_loop(0, NR, chain, 0, unroll=4)
        lane = lax.broadcasted_iota(jnp.int32, (NB, 128), 1)
        low = lane < 64
        even = lane % 64 < 32

        def pack(ch, carry):
            base = pl.multiple_of(ch * SO, 8)
            val = o_scr[0, pl.ds(base, NR), :]
            do_ref[ch] = jnp.where(first_core, val, pltpu.roll(val, 64, 1)).astype(BF16)
            g0, g1, g2, g3 = (val[NB * g:NB * (g + 1)] for g in range(4))
            r0, r1, r2, r3 = (pltpu.roll(g, 64, 1) for g in (g0, g1, g2, g3))
            a0, a1 = jnp.where(low, g0, r2), jnp.where(low, g1, r3)
            a2, a3 = jnp.where(low, r0, g2), jnp.where(low, r1, g3)
            p0 = jnp.where(even, a0, pltpu.roll(a1, 32, 1))
            p1 = jnp.where(even, pltpu.roll(a0, 96, 1), a1)
            p2 = jnp.where(even, a2, pltpu.roll(a3, 32, 1))
            p3 = jnp.where(even, pltpu.roll(a2, 96, 1), a3)
            same0[ch] = jnp.where(first_core, p0, p2).astype(BF16)
            same1[ch] = jnp.where(first_core, p1, p3).astype(BF16)
            cross0[ch] = jnp.where(first_core, p2, p0).astype(BF16)
            cross1[ch] = jnp.where(first_core, p3, p1).astype(BF16)
            return carry

        lax.fori_loop(0, C, pack, 0, unroll=4)


def piece_spec(width, blk):
    return pl.BlockSpec((width, HALF, N), lambda s, *ids: (s, blk, 0))


def out_call(chunk, ids, a_own, b_pieces, don, dup, g1, w_out_t, scale, offset):
    lane_spec = pl.BlockSpec((NR, C, 128), lambda s, ids: (0, 0, chunk))
    acc_spec = full_spec((C, 128))
    pack_spec = full_spec((C, NB, 128))
    return pl.pallas_call(
        out_kernel,
        grid_spec=pltpu.PrefetchScalarGridSpec(
            num_scalar_prefetch=1,
            grid=(C // CB,),
            in_specs=[pl.BlockSpec((CB, NR, N), lambda s, ids: (s, 0, 0))] + [piece_spec(CB, blk) for _, blk in b_pieces]
            + [lane_spec, lane_spec, lane_spec, full_spec((C, C + 16)), full_spec((C, 128)), full_spec((C, 128))],
            out_specs=[full_spec((C, NR, 128)), full_spec((NR, C, 128))] + [pack_spec] * 4 + [acc_spec] * 3 + [TOKEN_SPEC],
            scratch_shapes=[pltpu.VMEM((1, C * SO, 128), F32)],
        ),
        out_shape=[sds((C, NR, 128), BF16), sds((NR, C, 128), BF16)] + [sds((C, NB, 128), BF16)] * 4 + [sds((C, 128), F32)] * 3 + [TOKEN],
        compiler_params=pltpu.CompilerParams(vmem_limit_bytes=VMEM_LIMIT),
        cost_estimate=pl.CostEstimate(flops=2 * 128 * 64 * 128 * 512, bytes_accessed=48 << 20, transcendentals=0),
        name="out_chain",
    )(ids, a_own, *(arr for arr, _ in b_pieces), don, dup, g1, w_out_t, scale, offset)


CK = 8


def da_kernel(*refs):
    do_refs, b_refs, da_ref = refs[:4], refs[4:20], refs[20]
    for ch in range(CK):
        do_row = jnp.concatenate([ref[ch] for ref in do_refs], axis=1)
        b_rows = jnp.concatenate([ref[ch] for ref in b_refs], axis=0)
        da_ref[ch] = nn_dot(do_row, b_rows).astype(BF16)


def da_call(do_chunks, b_pieces):
    return pl.pallas_call(
        da_kernel,
        grid=(C // CK,),
        in_specs=[pl.BlockSpec((CK, NR, 128), lambda s: (s, 0, 0))] * 4 + [piece_spec(CK, blk) for _, blk in b_pieces],
        out_specs=pl.BlockSpec((CK, NR, N), lambda s: (s, 0, 0)),
        out_shape=sds((C, NR, N), BF16),
        compiler_params=pltpu.CompilerParams(vmem_limit_bytes=VMEM_LIMIT),
        cost_estimate=pl.CostEstimate(flops=2 * 128 * 64 * 512 * 512, bytes_accessed=80 << 20, transcendentals=0),
        name="grad_a",
    )(*do_chunks, *(arr for arr, _ in b_pieces))


def db_kernel(*refs):
    do_refs, a_refs, db_ref = refs[:16], refs[16:32], refs[32]
    for ch in range(CK):
        x_t = [jnp.concatenate([ref[ch] for ref in do_refs[8 * h:8 * h + 8]], axis=0).T for h in range(2)]
        total = None
        for g in range(4):
            lhs = jnp.concatenate([x[32 * g:32 * g + 32] for x in x_t], axis=0)
            half, sub = divmod(g, 2)
            rhs = jnp.concatenate([ref[ch, NB * sub:NB * (sub + 1), :] for ref in a_refs[8 * half:8 * half + 8]], axis=0)
            term = nn_dot(lhs, rhs)
            total = term if total is None else total + term
        db_ref[ch] = total.astype(BF16)


def db_call(do_pieces, a_pieces):
    return pl.pallas_call(
        db_kernel,
        grid=(C // CK,),
        in_specs=[pl.BlockSpec((CK, NB, 128), lambda s: (s, 0, 0))] * 16 + [piece_spec(CK, blk) for _, blk in a_pieces],
        out_specs=pl.BlockSpec((CK, NR, N), lambda s: (s, 0, 0)),
        out_shape=sds((C, NR, N), BF16),
        compiler_params=pltpu.CompilerParams(vmem_limit_bytes=VMEM_LIMIT),
        cost_estimate=pl.CostEstimate(flops=2 * 128 * 64 * 512 * 512, bytes_accessed=80 << 20, transcendentals=0),
        name="grad_b",
    )(*do_pieces, *(arr for arr, _ in a_pieces))


def in_kernel(ids_ref, z_ref, dy_ref, m_ref, da_ref, db_ref, dg0, dg1, dg2, dg3, w_ref, scale_ref, offset_ref, w_cat_ref,
              dz_ref, dw_ref, dbin_ref, dsc_ref, doff_ref, a_scr, b_scr, m_scr):
    @pl.when(pl.program_id(0) == 0)
    def _():
        dw_ref[...] = jnp.zeros_like(dw_ref)
        dbin_ref[...] = jnp.zeros_like(dbin_ref)
        dsc_ref[...] = jnp.zeros_like(dsc_ref)
        doff_ref[...] = jnp.zeros_like(doff_ref)

    def unpack(ch, carry):
        base = pl.multiple_of(ch * SB, 8)
        for src, scr in ((da_ref, a_scr), (db_ref, b_scr)):
            for lane in range(4):
                scr[lane, pl.ds(base, NB), :] = src[ch, :, 128 * lane:128 * (lane + 1)].astype(F32)
        return carry

    lax.fori_loop(0, C, unpack, 0, unroll=4)

    load_mask(m_ref, m_scr, ids_ref)
    first = pl.program_id(0) % 2 * NB

    def body(row, carry):
        x_hat, inv_std, z_norm = normed_row(pair_row(z_ref, row, ids_ref), scale_ref[...], offset_ref[...])
        aug = jnp.concatenate([z_norm, ones_rows(N)], axis=0)
        mask_f = m_scr[pl.ds(first + row, 1), :]
        parts = []
        for side, scr in ((0, a_scr), (1, b_scr)):
            proj = nn_dot(w_ref[side * C:(side + 1) * C], aug)
            sig = sigmoid(nn_dot(w_ref[(2 + side) * C:(3 + side) * C], aug))
            d_proj = get_row(scr, row, SB) * mask_f * sig
            d_lin = d_proj * proj * (1.0 - sig)
            dbin_ref[side * C:(side + 1) * C] += lanes(d_proj)
            dbin_ref[(2 + side) * C:(3 + side) * C] += lanes(d_lin)
            parts.append((d_proj.astype(BF16), d_lin.astype(BF16)))
        cat = jnp.concatenate([parts[0][0], parts[1][0], parts[0][1], parts[1][1], jnp.concatenate([dg[row] for dg in (dg0, dg1, dg2, dg3)], axis=1)], axis=0)
        dw_ref[...] += nt_dot(cat, z_norm)
        d_znorm = nn_dot(w_cat_ref[...], cat).astype(BF16).astype(F32)
        dsc_ref[...] += lanes(d_znorm * x_hat)
        doff_ref[...] += lanes(d_znorm)
        grad_hat = d_znorm * scale_ref[...]
        mean_grad = jnp.mean(grad_hat, axis=0, keepdims=True)
        mean_proj = jnp.mean(grad_hat * x_hat, axis=0, keepdims=True)
        d_zt = inv_std * (grad_hat - mean_grad - x_hat * mean_proj)
        d_row = (pair_row(dy_ref, row, ids_ref).astype(F32) + d_zt.T).astype(BF16)
        for p in range(16):
            dz_ref[row, pl.ds(pl.multiple_of(ids_ref[p], HALF), HALF), :] = d_row[HALF * p:HALF * (p + 1)]
        return carry

    lax.fori_loop(0, NB, body, 0, unroll=2)


def in_call(ids, z_loc, dy_loc, m_loc, d_a, d_b, dg_chunks, w_t, scale, offset, w_cat):
    row_spec = pl.BlockSpec((NB, N, C), lambda r, ids: (r, 0, 0))
    act_spec = pl.BlockSpec((C, NB, N), lambda r, ids: (0, r, 0))
    return pl.pallas_call(
        in_kernel,
        grid_spec=pltpu.PrefetchScalarGridSpec(
            num_scalar_prefetch=1,
            grid=(NQ,),
            in_specs=[row_spec, row_spec, pl.BlockSpec((1, N, C), lambda r, ids: (r // 2, 0, 0)), act_spec, act_spec]
            + [pl.BlockSpec((NB, C, 128), lambda r, ids: (r, 0, 0))] * 4
            + [full_spec((4 * C, C + 16)), full_spec((C, N)), full_spec((C, N)), full_spec((C, 5 * C))],
            out_specs=[row_spec, full_spec((5 * C, C)), full_spec((4 * C, 128)), full_spec((C, 128)), full_spec((C, 128))],
            scratch_shapes=[pltpu.VMEM((4, C * SB, 128), F32)] * 2 + [pltpu.VMEM((C, N), F32)],
        ),
        out_shape=[sds((NR, N, C), BF16), sds((5 * C, C), F32), sds((4 * C, 128), F32), sds((C, 128), F32), sds((C, 128), F32)],
        compiler_params=pltpu.CompilerParams(vmem_limit_bytes=VMEM_LIMIT),
        cost_estimate=pl.CostEstimate(flops=2 * 64 * 512 * 640 * 128 * 3, bytes_accessed=64 << 20, transcendentals=1 << 23),
        name="in_backward",
    )(ids, z_loc, dy_loc, m_loc, d_a, d_b, *dg_chunks, w_t, scale, offset, w_cat)


def aug_weight(w_mat, bias):
    wide = jnp.zeros((w_mat.shape[1], 16), BF16).at[:, 0].set(bias)
    return jnp.concatenate([w_mat.T, wide], axis=1)


def column(vec, width):
    return jnp.broadcast_to(vec.astype(F32)[:, None], (C, width))


def local_grads(z_loc, mask_loc, dy_loc, ln_in_scale, ln_in_offset, w_in, b_in, ln_out_scale, ln_out_offset, w_out, b_out, w_gate, b_gate):
    me = lax.axis_index('dap')
    chip, core = me // 2, me % 2
    w_cat = jnp.concatenate([w_in, w_gate], axis=1)
    w_t = aug_weight(w_cat, jnp.concatenate([b_in, b_gate]))
    w_out_t = aug_weight(w_out, b_out)
    in_scale, in_offset = column(ln_in_scale, N), column(ln_in_offset, N)
    out_scale, out_offset = column(ln_out_scale, 128), column(ln_out_offset, 128)

    order = [((chip * 2) ^ HOPS[q][h]) * NR + core_of * NR + h * HALF for q in range(4) for core_of in range(2) for h in range(2)]
    ids = jnp.stack(order + [core]).astype(jnp.int32)
    mask_t = jnp.transpose(mask_loc.reshape(2, HALF, N), (0, 2, 1)).astype(BF16)
    mask_t = jnp.pad(mask_t, ((0, 0), (0, 0), (0, C - HALF)))

    def move(val, flips):
        return lax.ppermute(val, 'dap', [(d, d ^ flips) for d in range(8)])

    top, bottom = (jnp.concatenate([z_loc[HALF * h:HALF * (h + 1)], mask_t[h:h + 1]], axis=0) for h in range(2))
    gathered = {}
    gathered[1, 0], gathered[1, 1] = move(top, HOPS[1][0]), move(bottom, HOPS[1][1])
    gathered[2, 0], gathered[2, 1] = move(gathered[1, 0], HOPS[1][1]), move(gathered[1, 1], HOPS[1][0])
    gathered[3, 0], gathered[3, 1] = move(top, HOPS[3][0]), move(bottom, HOPS[3][1])

    a_own, b_own, dup, don, g1, acc_bout, acc_ooff, ids = own_call(ids, z_loc, dy_loc, mask_t, w_t, in_scale, in_offset, w_out)
    b_par, a_par = move(b_own, 1), move(a_own, 1)
    a_at = {(0, h, f): (val, h) for h in range(2) for f, val in ((0, a_own), (1, a_par))}
    b_at = {(0, h, f): (val, h) for h in range(2) for f, val in ((0, b_own), (1, b_par))}
    do_at, do_chunks, dg_chunks, sums = {}, [], [], []
    for q in range(4):
        for h in range(2):
            if q:
                act_a, act_b, ids = gated_call(ids, gathered[q, h], w_t[:4 * C], in_scale, in_offset)
                a_at[q, h, 0], b_at[q, h, 0] = (act_a, 0), (act_b, 0)
                b_at[q, h, 1] = move(act_b, 1), 0
                a_at[q, h, 1] = move(act_a, 1), 0
        b_pieces = [b_at[q, h, f] for f in range(2) for h in range(2)]
        do_own, dg, same0, same1, cross0, cross1, *acc, ids = out_call(q, ids, a_own, b_pieces, don, dup, g1, w_out_t, out_scale, out_offset)
        do_chunks.append(do_own)
        dg_chunks.append(dg)
        sums.append(acc)
        for flip, h, val in ((0, 0, same0), (0, 1, same1), (1, 0, cross0), (1, 1, cross1)):
            flips = HOPS[q][h] ^ flip
            do_at[h, flips] = move(val, flips) if flips else val
    d_a = da_call(do_chunks, [b_at[q, h, f] for q in range(4) for f in range(2) for h in range(2)])
    chunk_of = {(HOPS[q][h], h): q for q in range(4) for h in range(2)}
    d_b = db_call([do_at[h, s] for h in range(2) for s in range(8)],
                  [a_at[chunk_of[s & 6, h], h, s & 1] for h in range(2) for s in range(8)])
    d_z, acc_w, acc_bin, acc_isc, acc_ioff = in_call(ids, z_loc, dy_loc, mask_t, d_a, d_b, dg_chunks, w_t[:4 * C], in_scale, in_offset, w_cat)

    acc_wout, acc_osc, acc_bg = (sum(s[n] for s in sums) for n in range(3))
    vecs = [jnp.sum(v, axis=1) for v in (acc_isc, acc_ioff, acc_bin, acc_osc, acc_ooff, acc_bout, acc_bg)]
    vecs, acc_w, acc_wout = lax.psum((jnp.concatenate(vecs), acc_w, acc_wout), 'dap')
    vecs = vecs.astype(BF16)
    d_isc, d_ioff, d_bin, d_osc, d_ooff, d_bout, d_bg = jnp.split(vecs, [C, 2 * C, 6 * C, 7 * C, 8 * C, 9 * C])
    acc_w = acc_w.T.astype(BF16)
    return d_z, d_isc, d_ioff, acc_w[:, :4 * C], d_bin, d_osc, d_ooff, acc_wout.astype(BF16), d_bout, acc_w[:, 4 * C:], d_bg


def solution(mesh):
    pair_spec = P(('batch', 'dap'), None, None)
    mask_spec = P(('batch', 'dap'), None)
    vec_rep = P(None)
    mat_rep = P(None, None)
    vec_part = P('batch')
    mat_part = P('batch', None)
    in_specs = (pair_spec, mask_spec, pair_spec, vec_rep, vec_rep, mat_rep, vec_rep, vec_rep, vec_rep, mat_rep, vec_rep, mat_rep, vec_rep)
    out_specs = (pair_spec, vec_part, vec_part, mat_part, vec_part, vec_part, vec_part, mat_part, vec_part, mat_part, vec_part)
    return jax.shard_map(local_grads, mesh=mesh, in_specs=in_specs, out_specs=out_specs, check_vma=False)
```

time: 1610 us -> 715 us (0.44)
  waiting for transfers between devices: 830 us -> 212 us
  matrix products: 422 us -> 0 us
  Pallas kernels: 0 us -> 416 us
  other arithmetic: 183 us -> 14.2 us
  local copies, waits for them, and re-layouts: 126 us -> 18.3 us
  starting transfers between devices: 0.08 us -> 25.9 us
    reduce_scatter x1 -> x0, waiting for transfers between devices: 565 us -> none  [local_grads(): d_act_b = lax.psum_scatter(d_b_part, 'dap', scatter_dimension=1, tiled=True)]
    dot_general x12 -> x0, matrix products: 422 us -> none  [the longest x1 105 us: local_grads(): jnp.einsum('cij,cjk->cik', d_tri, b_full, preferred_element_type=jnp.floa...]
    pallas_call x0 -> x14, Pallas kernels: none -> 416 us  [the longest x4 129 us: out_call(): pl.pallas_call(out_kernel, grid_spec=pltpu.PrefetchScalarGridSpec(num_sca...]
    all_gather x1 -> x0, waiting for transfers between devices: 265 us -> none  [local_grads(): b_full = lax.all_gather(act_b, 'dap', axis=1, tiled=True)]
    ppermute x0 -> x34, waiting for transfers between devices: none -> 212 us  [move(): return lax.ppermute(val, 'dap', [(d, d ^ flips) for d in range(8)])]
    dot_general x2 -> x0, local copies, waits for them, and re-layouts: 122 us -> none  [the longest x1 109 us: local_grads(): jnp.einsum('cij,cik->cjk', d_tri, act_a, preferred_element_type=jnp.float32)]
    reduce_sum x6, other arithmetic: 70 us -> 4.14 us  [local_grads(): jnp.sum(v, axis=1)]
    convert_element_type x11 -> x1, other arithmetic: 60.3 us -> 0.91 us  [local_grads(): mask_t = jnp.transpose(mask_loc.reshape(2, HALF, N), (0, 2, 1)).astype(BF16)]
  transfers between devices with their start and end apart: 2 -> 34, of which waited for: 2 -> 9; matrix products, arithmetic and copies ran while one was open for 12% -> 2% of each run, Pallas kernels for 0% -> 38%
where the time goes in v1:
time: 715 us; the launch traced here: 714 us
  Pallas kernels  416 us (58%)
  waiting for transfers between devices  212 us (30%)
  blocking collectives  27.3 us (4%)
  starting transfers between devices  25.9 us (4%)
  local copies, waits for them, and re-layouts  18.3 us (3%)
  other arithmetic  14.2 us (2%)
    ppermute x34, waiting for transfers between devices, move(): return lax.ppermute(val, 'dap', [(d, d ^ flips) for d in range(8)])  212 us
    pallas_call x4, Pallas kernels, out_call(): pl.pallas_call(out_kernel, grid_spec=pltpu.PrefetchScalarGridSpec(num_sca...  129 us
    pallas_call x6, Pallas kernels, gated_call(): pl.pallas_call(gated_kernel, grid_spec=pltpu.PrefetchScalarGridSpec(num_s...  109 us
    pallas_call x1, Pallas kernels, in_call(): pl.pallas_call(in_kernel, grid_spec=pltpu.PrefetchScalarGridSpec(num_scal...  60.9 us
    pallas_call x1, Pallas kernels, own_call(): pl.pallas_call(own_kernel, grid_spec=pltpu.PrefetchScalarGridSpec(num_sca...  55.5 us
    pallas_call x1, Pallas kernels, da_call(): pl.pallas_call(da_kernel, grid=(C // CK,), in_specs=[pl.BlockSpec((CK, NR...  31 us
    pallas_call x1, Pallas kernels, db_call(): pl.pallas_call(db_kernel, grid=(C // CK,), in_specs=[pl.BlockSpec((CK, NB...  30.7 us
    psum x1, blocking collectives, local_grads(): lax.psum((jnp.concatenate(vecs), acc_w, acc_wout), 'dap')  27.3 us
  transfers between devices with their start and end apart: 34, of which 9 were waited for; matrix products, arithmetic and copies ran while one was open for 2% of the time, Pallas kernels for 38%

profile of v1, /device:TPU:0, one launch (start us, length us, event | category | flops | bytes accessed | tf_op | source)
XLA Modules:
  0.0 714.4 jit_solution(16292181245003714378)
XLA Ops:
  1.4 0.9 convert_element_type.35
  4.8 1.3 broadcast_select_fusion
  8.5 1.5 broadcast_in_dim.8.scale_ref
  10.0 1.4 broadcast_in_dim.9.offset_ref
  11.4 55.5 %own_rows.1 = (bf16[128,64,512]{2,1,0:T(8,128)(2,1)}, bf16[128,64,512]{2,1,0:T(8,128)(2,1)}, bf16[64,128,512]{2,1,0:T(8,128)(2,1)}, bf16[64,128,512]{2,1,0:T(8,1...) custom-call(s32[17]{0:T(128)} %stack.71.ids_ref, ...), custom_call_target="tpu_custom_call" | custom-call | flops 4831838208 | bytes 67108864 | tf_op jit(solution)/shard_map/own_rows/pallas_call | solution.py:186
  67.8 4.0 fusion.5
  71.8 2.4 pad_maximum_fusion
  74.2 2.5 collective-permute-start.1
  76.8 2.4 pad_maximum_fusion.1
  79.2 1.5 collective-permute-start.2
  84.5 32.0 %out_chain.4 = (bf16[128,64,128]{2,1,0:T(8,128)(2,1)}, bf16[64,128,128]{2,1,0:T(8,128)(2,1)}, bf16[128,16,128]{2,1,0:T(8,128)(2,1)}, bf16[128,16,128]{2,1,0:T(8,...) custom-call(s32[17]{0:T(128)} %get-tuple-element.106.ids_ref, ...), custom_call_target="tpu_custom_call" | custom-call | flops 1073741824 | bytes 50331648 | tf_op jit(solution)/shard_map/out_chain/pallas_call | solution.py:279
  116.5 54.6 %collective-permute-done.1.z_ref.m_ref = bf16[33,512,128]{2,1,0:T(8,128)(2,1)} collective-permute-done((bf16[33,512,128]{2,1,0:T(8,128)(2,1)}, bf16[33,512,128]{2,1,0:T(8,128)(2,1)}, u32[]{:S(2)}, u32[]{:S(2)}) %collective-permute-start.1) | collective-permute-done | bytes 4325408 | tf_op jit(solution)/shard_map/ppermute | solution.py:443
  171.1 18.2 %gated_rows.6 = (bf16[128,32,512]{2,1,0:T(8,128)(2,1)}, bf16[128,32,512]{2,1,0:T(8,128)(2,1)}, s32[17]{0:T(128)}) custom-call(s32[17]{0:T(128)} %get-tuple-element.112.ids_ref, bf16[33,512,128]{2,1,0:T(8,128)(2,1)} %collective-permute-done.1.z_ref.m_ref, bf16[33,512,128]{2,1,0:T(8,128)(2,1)} %collective-permute-done.1.z_ref.m_ref, ...), custom_call_target="tpu_custom_call" | custom-call | flops 2415919104 | bytes 12582912 | tf_op jit(solution)/shard_map/gated_rows/pallas_call | solution.py:121
  189.3 18.0 %gated_rows.7 = (bf16[128,32,512]{2,1,0:T(8,128)(2,1)}, bf16[128,32,512]{2,1,0:T(8,128)(2,1)}, s32[17]{0:T(128)}) custom-call(s32[17]{0:T(128)} %get-tuple-element.113.ids_ref, bf16[33,512,128]{2,1,0:T(8,128)(2,1)} %collective-permute-done.2.z_ref.m_ref, bf16[33,512,128]{2,1,0:T(8,128)(2,1)} %collective-permute-done.2.z_ref.m_ref, ...), custom_call_target="tpu_custom_call" | custom-call | flops 2415919104 | bytes 12582912 | tf_op jit(solution)/shard_map/gated_rows/pallas_call | solution.py:121
  207.8 1.8 collective-permute-start.5
  209.6 1.5 collective-permute-start.6
  211.6 3.3 collective-permute-done.4.b_par1.refs_11_
  214.9 1.7 collective-permute-start.10
  216.6 32.2 %out_chain.5 = (bf16[128,64,128]{2,1,0:T(8,128)(2,1)}, bf16[64,128,128]{2,1,0:T(8,128)(2,1)}, bf16[128,16,128]{2,1,0:T(8,128)(2,1)}, bf16[128,16,128]{2,1,0:T(8,...) custom-call(s32[17]{0:T(128)} %get-tuple-element.114.ids_ref, ...), custom_call_target="tpu_custom_call" | custom-call | flops 1073741824 | bytes 50331648 | tf_op jit(solution)/shard_map/out_chain/pallas_call | solution.py:279
  248.9 55.5 %collective-permute-done.5.z_ref.m_ref = bf16[33,512,128]{2,1,0:T(8,128)(2,1)} collective-permute-done((bf16[33,512,128]{2,1,0:T(8,128)(2,1)}, bf16[33,512,128]{2,1,0:T(8,128)(2,1)}, u32[]{:S(2)}, u32[]{:S(2)}) %collective-permute-start.5) | collective-permute-done | bytes 4325408 | tf_op jit(solution)/shard_map/ppermute | solution.py:443
  304.4 18.0 %gated_rows.8 = (bf16[128,32,512]{2,1,0:T(8,128)(2,1)}, bf16[128,32,512]{2,1,0:T(8,128)(2,1)}, s32[17]{0:T(128)}) custom-call(s32[17]{0:T(128)} %get-tuple-element.117.ids_ref, bf16[33,512,128]{2,1,0:T(8,128)(2,1)} %collective-permute-done.5.z_ref.m_ref, bf16[33,512,128]{2,1,0:T(8,128)(2,1)} %collective-permute-done.5.z_ref.m_ref, ...), custom_call_target="tpu_custom_call" | custom-call | flops 2415919104 | bytes 12582912 | tf_op jit(solution)/shard_map/gated_rows/pallas_call | solution.py:121
  323.0 18.2 %gated_rows.9 = (bf16[128,32,512]{2,1,0:T(8,128)(2,1)}, bf16[128,32,512]{2,1,0:T(8,128)(2,1)}, s32[17]{0:T(128)}) custom-call(s32[17]{0:T(128)} %get-tuple-element.118.ids_ref, bf16[33,512,128]{2,1,0:T(8,128)(2,1)} %collective-permute-done.6.z_ref.m_ref, bf16[33,512,128]{2,1,0:T(8,128)(2,1)} %collective-permute-done.6.z_ref.m_ref, ...), custom_call_target="tpu_custom_call" | custom-call | flops 2415919104 | bytes 12582912 | tf_op jit(solution)/shard_map/gated_rows/pallas_call | solution.py:121
  341.2 55.4 %collective-permute-done.9.z_ref.m_ref = bf16[33,512,128]{2,1,0:T(8,128)(2,1)} collective-permute-done((bf16[33,512,128]{2,1,0:T(8,128)(2,1)}, bf16[33,512,128]{2,1,0:T(8,128)(2,1)}, u32[]{:S(2)}, u32[]{:S(2)}) %collective-permute-start.9) | collective-permute-done | bytes 4325408 | tf_op jit(solution)/shard_map/ppermute | solution.py:443
  396.6 1.5 collective-permute-done.10.z_ref.m_ref
  398.6 12.1 %collective-permute-done.13.refs_1_ = bf16[128,16,128]{2,1,0:T(8,128)(2,1)S(1)} collective-permute-done((bf16[128,16,128]{2,1,0:T(8,128)(2,1)S(1)}, bf16[128,16,128]{2,1,0:T(8,128)(2,1)S(1)}, u32[]{:S(2)}, u32[]{:S(2)}) %collective-permute-start.13) | collective-permute-done | bytes 524320 | tf_op jit(solution)/shard_map/ppermute | solution.py:443
  410.9 1.8 collective-permute-done.20.refs_9_
  412.8 1.7 collective-permute-start.14
  414.5 1.7 collective-permute-start.23
  416.4 32.6 %out_chain.6 = (bf16[128,64,128]{2,1,0:T(8,128)(2,1)}, bf16[64,128,128]{2,1,0:T(8,128)(2,1)}, bf16[128,16,128]{2,1,0:T(8,128)(2,1)}, bf16[128,16,128]{2,1,0:T(8,...) custom-call(s32[17]{0:T(128)} %get-tuple-element.119.ids_ref, ...), custom_call_target="tpu_custom_call" | custom-call | flops 1073741824 | bytes 50331648 | tf_op jit(solution)/shard_map/out_chain/pallas_call | solution.py:279
  449.0 18.1 %gated_rows.10 = (bf16[128,32,512]{2,1,0:T(8,128)(2,1)}, bf16[128,32,512]{2,1,0:T(8,128)(2,1)}, s32[17]{0:T(128)}) custom-call(s32[17]{0:T(128)} %get-tuple-element.122.ids_ref, bf16[33,512,128]{2,1,0:T(8,128)(2,1)} %collective-permute-done.9.z_ref.m_ref, bf16[33,512,128]{2,1,0:T(8,128)(2,1)} %collective-permute-done.9.z_ref.m_ref, ...), custom_call_target="tpu_custom_call" | custom-call | flops 2415919104 | bytes 12582912 | tf_op jit(solution)/shard_map/gated_rows/pallas_call | solution.py:121
  467.1 18.1 %gated_rows.11 = (bf16[128,32,512]{2,1,0:T(8,128)(2,1)}, bf16[128,32,512]{2,1,0:T(8,128)(2,1)}, s32[17]{0:T(128)}) custom-call(s32[17]{0:T(128)} %get-tuple-element.123.ids_ref, bf16[33,512,128]{2,1,0:T(8,128)(2,1)} %collective-permute-done.10.z_ref.m_ref, bf16[33,512,128]{2,1,0:T(8,128)(2,1)} %collective-permute-done.10.z_ref.m_ref, ...), custom_call_target="tpu_custom_call" | custom-call | flops 2415919104 | bytes 12582912 | tf_op jit(solution)/shard_map/gated_rows/pallas_call | solution.py:121
  486.0 13.4 %collective-permute-done.24.refs_13_ = bf16[128,16,128]{2,1,0:T(8,128)(2,1)S(1)} collective-permute-done((bf16[128,16,128]{2,1,0:T(8,128)(2,1)S(1)}, bf16[128,16,128]{2,1,0:T(8,128)(2,1)S(1)}, u32[]{:S(2)}, u32[]{:S(2)}) %collective-permute-start.24) | collective-permute-done | bytes 524320 | tf_op jit(solution)/shard_map/ppermute | solution.py:443
  499.9 1.4 collective-permute-start.18
  501.4 13.9 %collective-permute-done.18.refs_6_ = bf16[128,16,128]{2,1,0:T(8,128)(2,1)S(1)} collective-permute-done((bf16[128,16,128]{2,1,0:T(8,128)(2,1)}, bf16[128,16,128]{2,1,0:T(8,128)(2,1)S(1)}, u32[]{:S(2)}, u32[]{:S(2)}) %collective-permute-start.18) | collective-permute-done | bytes 524320 | tf_op jit(solution)/shard_map/ppermute | solution.py:443
  515.8 1.5 collective-permute-start.25
  517.3 1.7 collective-permute-start.26
  519.4 32.4 %out_chain.7 = (bf16[128,64,128]{2,1,0:T(8,128)(2,1)}, bf16[64,128,128]{2,1,0:T(8,128)(2,1)}, bf16[128,16,128]{2,1,0:T(8,128)(2,1)}, bf16[128,16,128]{2,1,0:T(8,...) custom-call(s32[17]{0:T(128)} %get-tuple-element.124.ids_ref, ...), custom_call_target="tpu_custom_call" | custom-call | flops 1073741824 | bytes 50331648 | tf_op jit(solution)/shard_map/out_chain/pallas_call | solution.py:279
  551.9 1.0 add_add_fusion
  552.9 1.5 collective-permute-start.16
  555.1 1.4 collective-permute-start.22
  556.5 0.9 add_reduce_fusion
  557.4 31.0 %grad_a.1.da_ref = bf16[128,64,512]{2,1,0:T(8,128)(2,1)} custom-call(bf16[128,64,128]{2,1,0:T(8,128)(2,1)} %get-tuple-element.128.refs_0_, bf16[128,64,128]{2,1,0:T(8,128)(2,1)} %get-tuple-element.129.refs_1_, bf16[128,64,128]{2,1,0:T(8,128)(2,1)} %get-tuple-element.130.refs_2_, bf16[128,64,128]{2,1,0:T(8,128)(2,1)} %get-tuple-element.131.refs_3_, ...), custom_call_target="tpu_custom_call" | custom-call | flops 4294967296 | bytes 83886080 | tf_op jit(solution)/shard_map/grad_a/pallas_call | solution.py:308
  589.8 30.7 %grad_b.1.db_ref = bf16[128,64,512]{2,1,0:T(8,128)(2,1)} custom-call(bf16[128,16,128]{2,1,0:T(8,128)(2,1)} %get-tuple-element.132.refs_0_, bf16[128,16,128]{2,1,0:T(8,128)(2,1)} %copy-done.1, bf16[128,16,128]{2,1,0:T(8,128)(2,1)} %copy-done.3, bf16[128,16,128]{2,1,0:T(8,128)(2,1)} %copy-done.4, bf16[128,16,128]{2,1,0:T(8,128)(2,1)} %copy-done.9, ...), custom_call_target="tpu_custom_call" | custom-call | flops 4294967296 | bytes 83886080 | tf_op jit(solution)/shard_map/grad_b/pallas_call | solution.py:335
  620.5 60.9 %in_backward.1 = (bf16[64,512,128]{2,1,0:T(8,128)(2,1)}, f32[640,128]{1,0:T(8,128)}, f32[512,128]{1,0:T(8,128)}, f32[128,128]{1,0:T(8,128)}, f32[128,128]{1,0:T(8,128)}) custom-call(s32[17]{0:T(128)} %get-tuple-element.127.ids_ref, bf16[64,512,128]{2,1,0:T(8,128)(2,1)} %z_ref.3, bf16[64,512,128]{2,1,0:T(8,128)(2,1)} %dy_ref.3, ...), custom_call_target="tpu_custom_call" | custom-call | flops 16106127360 | bytes 67108864 | tf_op jit(solution)/shard_map/in_backward/pallas_call | solution.py:401
  681.4 0.9 reduce_sum.63
  682.3 0.9 reduce_sum.64
  683.3 1.1 reduce_sum.65
  684.5 27.3 %all-reduce.5 = (bf16[1280]{0:T(1024)(128)(2,1)S(1)}, bf16[640,128]{1,0:T(8,128)(2,1)S(1)}, bf16[128,128]{1,0:T(8,128)(2,1)}) all-reduce(f32[1280]{0:T(1024)S(1)} %constant_dynamic-update-slice_fusion.3, f32[640,128]{1,0:T(8,128)} %get-tuple-element.172, f32[128,128]{1,0:T(8,128)S(1)} %get-tuple-element.212), channel_id=1, replica_groups=mesh['batch'=1,'dap'=8] {'dap'}, use_global_device_ids=true, to_apply=%region_8.9 | all-reduce | flops 99584 | bytes 597504 | tf_op jit(solution)/shard_map/psum | solution.py:479
  (147 shorter events, 19.6 us)
Async XLA Ops:
  66.9 16.2 %collective-permute-start = (bf16[128,64,512]{2,1,0:T(8,128)(2,1)}, bf16[128,64,512]{2,1,0:T(8,128)(2,1)}, u32[]{:S(2)}, u32[]{:S(2)}) collective-permute-start(bf16[128,64,512]{2,1,0:T(8,128)(2,1)} %get-tuple-element.108.b_own0.b_own1.refs_4_.refs_5_), channel_id=1, source_target_pairs={{0,1},{1,0},{2,3},{3,2},{4,5},{5,4},{6,7},{7,6}} | collective-permute-start | bytes 25165832 | tf_op jit(solution)/shard_map/ppermute | solution.py:443
  74.2 96.8 %collective-permute-start.1 = (bf16[33,512,128]{2,1,0:T(8,128)(2,1)}, bf16[33,512,128]{2,1,0:T(8,128)(2,1)}, u32[]{:S(2)}, u32[]{:S(2)}) collective-permute-start(bf16[33,512,128]{2,1,0:T(8,128)(2,1)} %pad_maximum_fusion), channel_id=1, source_target_pairs={{0,2},{1,3},{2,0},{3,1},{4,6},{5,7},{6,4},{7,5}} | collective-permute-start | bytes 12976136 | tf_op jit(solution)/shard_map/ppermute | solution.py:443
  79.2 110.1 %collective-permute-start.2 = (bf16[33,512,128]{2,1,0:T(8,128)(2,1)}, bf16[33,512,128]{2,1,0:T(8,128)(2,1)}, u32[]{:S(2)}, u32[]{:S(2)}) collective-permute-start(bf16[33,512,128]{2,1,0:T(8,128)(2,1)} %pad_maximum_fusion.1), channel_id=1, source_target_pairs={{0,4},{1,5},{2,6},{3,7},{4,0},{5,1},{6,2},{7,3}} | collective-permute-start | bytes 12976136 | tf_op jit(solution)/shard_map/ppermute | solution.py:443
  189.3 21.8 %collective-permute-start.3 = (bf16[128,32,512]{2,1,0:T(8,128)(2,1)}, bf16[128,32,512]{2,1,0:T(8,128)(2,1)}, u32[]{:S(2)}, u32[]{:S(2)}) collective-permute-start(bf16[128,32,512]{2,1,0:T(8,128)(2,1)} %get-tuple-element.115.b_own0.refs_8_), channel_id=1, source_target_pairs={{0,1},{1,0},{2,3},{3,2},{4,5},{5,4},{6,7},{7,6}} | collective-permute-start | bytes 12582920 | tf_op jit(solution)/shard_map/ppermute | solution.py:443
  207.3 7.6 %collective-permute-start.4 = (bf16[128,32,512]{2,1,0:T(8,128)(2,1)}, bf16[128,32,512]{2,1,0:T(8,128)(2,1)}, u32[]{:S(2)}, u32[]{:S(2)}) collective-permute-start(bf16[128,32,512]{2,1,0:T(8,128)(2,1)} %get-tuple-element.116.b_own1.refs_9_), channel_id=1, source_target_pairs={{0,1},{1,0},{2,3},{3,2},{4,5},{5,4},{6,7},{7,6}} | collective-permute-start | bytes 12582920 | tf_op jit(solution)/shard_map/ppermute | solution.py:443
  207.8 190.3 %collective-permute-start.27 = (bf16[128,64,512]{2,1,0:T(8,128)(2,1)}, bf16[128,64,512]{2,1,0:T(8,128)(2,1)}, u32[]{:S(2)}, u32[]{:S(2)}) collective-permute-start(bf16[128,64,512]{2,1,0:T(8,128)(2,1)} %get-tuple-element.107.a_ref.refs_16_.refs_24_), channel_id=1, source_target_pairs={{0,1},{1,0},{2,3},{3,2},{4,5},{5,4},{6,7},{7,6}} | collective-permute-start | bytes 25165832 | tf_op jit(solution)/shard_map/ppermute | solution.py:443
  207.8 96.6 %collective-permute-start.5 = (bf16[33,512,128]{2,1,0:T(8,128)(2,1)}, bf16[33,512,128]{2,1,0:T(8,128)(2,1)}, u32[]{:S(2)}, u32[]{:S(2)}) collective-permute-start(bf16[33,512,128]{2,1,0:T(8,128)(2,1)} %collective-permute-done.1.z_ref.m_ref), channel_id=1, source_target_pairs={{0,4},{1,5},{2,6},{3,7},{4,0},{5,1},{6,2},{7,3}} | collective-permute-start | bytes 12976136 | tf_op jit(solution)/shard_map/ppermute | solution.py:443
  209.6 112.9 %collective-permute-start.6 = (bf16[33,512,128]{2,1,0:T(8,128)(2,1)}, bf16[33,512,128]{2,1,0:T(8,128)(2,1)}, u32[]{:S(2)}, u32[]{:S(2)}) collective-permute-start(bf16[33,512,128]{2,1,0:T(8,128)(2,1)} %collective-permute-done.2.z_ref.m_ref), channel_id=1, source_target_pairs={{0,2},{1,3},{2,0},{3,1},{4,6},{5,7},{6,4},{7,5}} | collective-permute-start | bytes 12976136 | tf_op jit(solution)/shard_map/ppermute | solution.py:443
  211.1 185.5 %collective-permute-start.9 = (bf16[33,512,128]{2,1,0:T(8,128)(2,1)}, bf16[33,512,128]{2,1,0:T(8,128)(2,1)}, u32[]{:S(2)}, u32[]{:S(2)}) collective-permute-start(bf16[33,512,128]{2,1,0:T(8,128)(2,1)} %pad_maximum_fusion), channel_id=1, source_target_pairs={{0,4},{1,5},{2,6},{3,7},{4,0},{5,1},{6,2},{7,3}} | collective-permute-start | bytes 12976136 | tf_op jit(solution)/shard_map/ppermute | solution.py:443
  214.9 183.2 %collective-permute-start.10 = (bf16[33,512,128]{2,1,0:T(8,128)(2,1)}, bf16[33,512,128]{2,1,0:T(8,128)(2,1)}, u32[]{:S(2)}, u32[]{:S(2)}) collective-permute-start(bf16[33,512,128]{2,1,0:T(8,128)(2,1)} %pad_maximum_fusion.1), channel_id=1, source_target_pairs={{0,2},{1,3},{2,0},{3,1},{4,6},{5,7},{6,4},{7,5}} | collective-permute-start | bytes 12976136 | tf_op jit(solution)/shard_map/ppermute | solution.py:443
  304.4 108.4 %collective-permute-start.28 = (bf16[128,32,512]{2,1,0:T(8,128)(2,1)}, bf16[128,32,512]{2,1,0:T(8,128)(2,1)}, u32[]{:S(2)}, u32[]{:S(2)}) collective-permute-start(bf16[128,32,512]{2,1,0:T(8,128)(2,1)} %get-tuple-element.148.refs_18_), channel_id=1, source_target_pairs={{0,1},{1,0},{2,3},{3,2},{4,5},{5,4},{6,7},{7,6}} | collective-permute-start | bytes 12582920 | tf_op jit(solution)/shard_map/ppermute | solution.py:443
  322.4 92.1 %collective-permute-start.32 = (bf16[128,32,512]{2,1,0:T(8,128)(2,1)}, bf16[128,32,512]{2,1,0:T(8,128)(2,1)}, u32[]{:S(2)}, u32[]{:S(2)}) collective-permute-start(bf16[128,32,512]{2,1,0:T(8,128)(2,1)} %get-tuple-element.152.refs_28_), channel_id=1, source_target_pairs={{0,1},{1,0},{2,3},{3,2},{4,5},{5,4},{6,7},{7,6}} | collective-permute-start | bytes 12582920 | tf_op jit(solution)/shard_map/ppermute | solution.py:443
  323.0 75.1 %copy-start.31 = (bf16[128,16,128]{2,1,0:T(8,128)(2,1)S(1)}, bf16[128,16,128]{2,1,0:T(8,128)(2,1)}, u32[]{:S(2)}) copy-start(bf16[128,16,128]{2,1,0:T(8,128)(2,1)} %get-tuple-element.133) | copy-start | bytes 1572868
  323.0 87.8 %copy-start.30 = (bf16[128,16,128]{2,1,0:T(8,128)(2,1)S(1)}, bf16[128,16,128]{2,1,0:T(8,128)(2,1)}, u32[]{:S(2)}) copy-start(bf16[128,16,128]{2,1,0:T(8,128)(2,1)} %get-tuple-element.141) | copy-start | bytes 1572868
  323.0 91.5 %copy-start.29 = (bf16[128,16,128]{2,1,0:T(8,128)(2,1)S(1)}, bf16[128,16,128]{2,1,0:T(8,128)(2,1)}, u32[]{:S(2)}) copy-start(bf16[128,16,128]{2,1,0:T(8,128)(2,1)} %get-tuple-element.135) | copy-start | bytes 1572868
  323.0 91.5 %copy-start.28 = (bf16[128,16,128]{2,1,0:T(8,128)(2,1)S(1)}, bf16[128,16,128]{2,1,0:T(8,128)(2,1)}, u32[]{:S(2)}) copy-start(bf16[128,16,128]{2,1,0:T(8,128)(2,1)} %get-tuple-element.144) | copy-start | bytes 1572868
  396.6 17.9 %collective-permute-start.7 = (bf16[128,32,512]{2,1,0:T(8,128)(2,1)}, bf16[128,32,512]{2,1,0:T(8,128)(2,1)}, u32[]{:S(2)}, u32[]{:S(2)}) collective-permute-start(bf16[128,32,512]{2,1,0:T(8,128)(2,1)} %get-tuple-element.120.b_own0.refs_12_), channel_id=1, source_target_pairs={{0,1},{1,0},{2,3},{3,2},{4,5},{5,4},{6,7},{7,6}} | collective-permute-start | bytes 12582920 | tf_op jit(solution)/shard_map/ppermute | solution.py:443
  398.1 18.2 %collective-permute-start.8 = (bf16[128,32,512]{2,1,0:T(8,128)(2,1)}, bf16[128,32,512]{2,1,0:T(8,128)(2,1)}, u32[]{:S(2)}, u32[]{:S(2)}) collective-permute-start(bf16[128,32,512]{2,1,0:T(8,128)(2,1)} %get-tuple-element.121.b_own1.refs_13_), channel_id=1, source_target_pairs={{0,1},{1,0},{2,3},{3,2},{4,5},{5,4},{6,7},{7,6}} | collective-permute-start | bytes 12582920 | tf_op jit(solution)/shard_map/ppermute | solution.py:443
  398.1 12.6 %collective-permute-start.13 = (bf16[128,16,128]{2,1,0:T(8,128)(2,1)S(1)}, bf16[128,16,128]{2,1,0:T(8,128)(2,1)S(1)}, u32[]{:S(2)}, u32[]{:S(2)}) collective-permute-start(bf16[128,16,128]{2,1,0:T(8,128)(2,1)S(1)} %copy-done.31), channel_id=1, source_target_pairs={{0,1},{1,0},{2,3},{3,2},{4,5},{5,4},{6,7},{7,6}} | collective-permute-start | bytes 1572872 | tf_op jit(solution)/shard_map/ppermute | solution.py:443
  410.7 38.3 %copy-start.1 = (bf16[128,16,128]{2,1,0:T(8,128)(2,1)}, bf16[128,16,128]{2,1,0:T(8,128)(2,1)S(1)}, u32[]{:S(2)}) copy-start(bf16[128,16,128]{2,1,0:T(8,128)(2,1)S(1)} %collective-permute-done.13.refs_1_) | copy-start | bytes 1572868
  410.7 1.9 collective-permute-start.20
  412.6 87.2 %collective-permute-start.30 = (bf16[128,32,512]{2,1,0:T(8,128)(2,1)}, bf16[128,32,512]{2,1,0:T(8,128)(2,1)}, u32[]{:S(2)}, u32[]{:S(2)}) collective-permute-start(bf16[128,32,512]{2,1,0:T(8,128)(2,1)} %get-tuple-element.150.refs_22_), channel_id=1, source_target_pairs={{0,1},{1,0},{2,3},{3,2},{4,5},{5,4},{6,7},{7,6}} | collective-permute-start | bytes 12582920 | tf_op jit(solution)/shard_map/ppermute | solution.py:443
  412.8 72.4 %collective-permute-start.14 = (bf16[128,16,128]{2,1,0:T(8,128)(2,1)}, bf16[128,16,128]{2,1,0:T(8,128)(2,1)S(1)}, u32[]{:S(2)}, u32[]{:S(2)}) collective-permute-start(bf16[128,16,128]{2,1,0:T(8,128)(2,1)} %get-tuple-element.134), channel_id=1, source_target_pairs={{0,2},{1,3},{2,0},{3,1},{4,6},{5,7},{6,4},{7,5}} | collective-permute-start | bytes 1572872 | tf_op jit(solution)/shard_map/ppermute | solution.py:443
  414.5 71.1 %collective-permute-start.15 = (bf16[128,16,128]{2,1,0:T(8,128)(2,1)S(1)}, bf16[128,16,128]{2,1,0:T(8,128)(2,1)S(1)}, u32[]{:S(2)}, u32[]{:S(2)}) collective-permute-start(bf16[128,16,128]{2,1,0:T(8,128)(2,1)S(1)} %copy-done.29), channel_id=1, source_target_pairs={{0,3},{1,2},{2,1},{3,0},{4,7},{5,6},{6,5},{7,4}} | collective-permute-start | bytes 1572872 | tf_op jit(solution)/shard_map/ppermute | solution.py:443
  414.5 71.2 %collective-permute-start.23 = (bf16[128,16,128]{2,1,0:T(8,128)(2,1)S(1)}, bf16[128,16,128]{2,1,0:T(8,128)(2,1)S(1)}, u32[]{:S(2)}, u32[]{:S(2)}) collective-permute-start(bf16[128,16,128]{2,1,0:T(8,128)(2,1)S(1)} %copy-done.28), channel_id=1, source_target_pairs={{0,4},{1,5},{2,6},{3,7},{4,0},{5,1},{6,2},{7,3}} | collective-permute-start | bytes 1572872 | tf_op jit(solution)/shard_map/ppermute | solution.py:443
  416.3 83.7 %collective-permute-start.33 = (bf16[128,32,512]{2,1,0:T(8,128)(2,1)}, bf16[128,32,512]{2,1,0:T(8,128)(2,1)}, u32[]{:S(2)}, u32[]{:S(2)}) collective-permute-start(bf16[128,32,512]{2,1,0:T(8,128)(2,1)} %get-tuple-element.153.refs_30_), channel_id=1, source_target_pairs={{0,1},{1,0},{2,3},{3,2},{4,5},{5,4},{6,7},{7,6}} | collective-permute-start | bytes 12582920 | tf_op jit(solution)/shard_map/ppermute | solution.py:443
  467.1 52.0 %copy-start.15 = (f32[128,128]{1,0:T(8,128)S(1)}, f32[128,128]{1,0:T(8,128)}, u32[]{:S(2)}) copy-start(f32[128,128]{1,0:T(8,128)} %get-tuple-element.166) | copy-start | bytes 196612
  467.1 52.1 %copy-start.14 = (f32[128,128]{1,0:T(8,128)S(1)}, f32[128,128]{1,0:T(8,128)}, u32[]{:S(2)}) copy-start(f32[128,128]{1,0:T(8,128)} %get-tuple-element.167) | copy-start | bytes 196612
  485.2 66.6 %copy-start.3 = (bf16[128,16,128]{2,1,0:T(8,128)(2,1)}, bf16[128,16,128]{2,1,0:T(8,128)(2,1)S(1)}, u32[]{:S(2)}) copy-start(bf16[128,16,128]{2,1,0:T(8,128)(2,1)S(1)} %collective-permute-done.14.refs_2_) | copy-start | bytes 1572868
  485.2 30.6 %collective-permute-start.11 = (bf16[128,32,512]{2,1,0:T(8,128)(2,1)}, bf16[128,32,512]{2,1,0:T(8,128)(2,1)}, u32[]{:S(2)}, u32[]{:S(2)}) collective-permute-start(bf16[128,32,512]{2,1,0:T(8,128)(2,1)} %get-tuple-element.125.b_own0.refs_16_), channel_id=1, source_target_pairs={{0,1},{1,0},{2,3},{3,2},{4,5},{5,4},{6,7},{7,6}} | collective-permute-start | bytes 12582920 | tf_op jit(solution)/shard_map/ppermute | solution.py:443
  485.6 66.2 %copy-start.4 = (bf16[128,16,128]{2,1,0:T(8,128)(2,1)}, bf16[128,16,128]{2,1,0:T(8,128)(2,1)S(1)}, u32[]{:S(2)}) copy-start(bf16[128,16,128]{2,1,0:T(8,128)(2,1)S(1)} %collective-permute-done.15.refs_3_) | copy-start | bytes 1572868
  485.6 31.7 %collective-permute-start.12 = (bf16[128,32,512]{2,1,0:T(8,128)(2,1)}, bf16[128,32,512]{2,1,0:T(8,128)(2,1)}, u32[]{:S(2)}, u32[]{:S(2)}) collective-permute-start(bf16[128,32,512]{2,1,0:T(8,128)(2,1)} %get-tuple-element.126.b_own1.refs_17_), channel_id=1, source_target_pairs={{0,1},{1,0},{2,3},{3,2},{4,5},{5,4},{6,7},{7,6}} | collective-permute-start | bytes 12582920 | tf_op jit(solution)/shard_map/ppermute | solution.py:443
  485.7 66.1 %copy-start.5 = (bf16[128,16,128]{2,1,0:T(8,128)(2,1)}, bf16[128,16,128]{2,1,0:T(8,128)(2,1)S(1)}, u32[]{:S(2)}) copy-start(bf16[128,16,128]{2,1,0:T(8,128)(2,1)S(1)} %collective-permute-done.23.refs_12_) | copy-start | bytes 1572868
  485.7 13.7 %collective-permute-start.24 = (bf16[128,16,128]{2,1,0:T(8,128)(2,1)S(1)}, bf16[128,16,128]{2,1,0:T(8,128)(2,1)S(1)}, u32[]{:S(2)}, u32[]{:S(2)}) collective-permute-start(bf16[128,16,128]{2,1,0:T(8,128)(2,1)S(1)} %copy-done.27), channel_id=1, source_target_pairs={{0,5},{1,4},{2,7},{3,6},{4,1},{5,0},{6,3},{7,2}} | collective-permute-start | bytes 1572872 | tf_op jit(solution)/shard_map/ppermute | solution.py:443
  499.4 52.4 %copy-start.6 = (bf16[128,16,128]{2,1,0:T(8,128)(2,1)}, bf16[128,16,128]{2,1,0:T(8,128)(2,1)S(1)}, u32[]{:S(2)}) copy-start(bf16[128,16,128]{2,1,0:T(8,128)(2,1)S(1)} %collective-permute-done.24.refs_13_) | copy-start | bytes 1572868
  499.4 55.6 %collective-permute-start.29 = (bf16[128,32,512]{2,1,0:T(8,128)(2,1)}, bf16[128,32,512]{2,1,0:T(8,128)(2,1)}, u32[]{:S(2)}, u32[]{:S(2)}) collective-permute-start(bf16[128,32,512]{2,1,0:T(8,128)(2,1)} %get-tuple-element.149.refs_20_), channel_id=1, source_target_pairs={{0,1},{1,0},{2,3},{3,2},{4,5},{5,4},{6,7},{7,6}} | collective-permute-start | bytes 12582920 | tf_op jit(solution)/shard_map/ppermute | solution.py:443
  499.8 88.6 %collective-permute-start.31 = (bf16[128,32,512]{2,1,0:T(8,128)(2,1)}, bf16[128,32,512]{2,1,0:T(8,128)(2,1)}, u32[]{:S(2)}, u32[]{:S(2)}) collective-permute-start(bf16[128,32,512]{2,1,0:T(8,128)(2,1)} %get-tuple-element.151.refs_26_), channel_id=1, source_target_pairs={{0,1},{1,0},{2,3},{3,2},{4,5},{5,4},{6,7},{7,6}} | collective-permute-start | bytes 12582920 | tf_op jit(solution)/shard_map/ppermute | solution.py:443
  499.9 15.3 %collective-permute-start.18 = (bf16[128,16,128]{2,1,0:T(8,128)(2,1)}, bf16[128,16,128]{2,1,0:T(8,128)(2,1)S(1)}, u32[]{:S(2)}, u32[]{:S(2)}) collective-permute-start(bf16[128,16,128]{2,1,0:T(8,128)(2,1)} %get-tuple-element.138), channel_id=1, source_target_pairs={{0,6},{1,7},{2,4},{3,5},{4,2},{5,3},{6,0},{7,1}} | collective-permute-start | bytes 1572872 | tf_op jit(solution)/shard_map/ppermute | solution.py:443
  515.3 37.6 %collective-permute-start.19 = (bf16[128,16,128]{2,1,0:T(8,128)(2,1)}, bf16[128,16,128]{2,1,0:T(8,128)(2,1)S(1)}, u32[]{:S(2)}, u32[]{:S(2)}) collective-permute-start(bf16[128,16,128]{2,1,0:T(8,128)(2,1)} %get-tuple-element.139), channel_id=1, source_target_pairs={{0,7},{1,6},{2,5},{3,4},{4,3},{5,2},{6,1},{7,0}} | collective-permute-start | bytes 1572872 | tf_op jit(solution)/shard_map/ppermute | solution.py:443
  515.8 38.6 %collective-permute-start.25 = (bf16[128,16,128]{2,1,0:T(8,128)(2,1)}, bf16[128,16,128]{2,1,0:T(8,128)(2,1)}, u32[]{:S(2)}, u32[]{:S(2)}) collective-permute-start(bf16[128,16,128]{2,1,0:T(8,128)(2,1)} %get-tuple-element.146), channel_id=1, source_target_pairs={{0,6},{1,7},{2,4},{3,5},{4,2},{5,3},{6,0},{7,1}} | collective-permute-start | bytes 1572872 | tf_op jit(solution)/shard_map/ppermute | solution.py:443
  517.3 37.2 %collective-permute-start.26 = (bf16[128,16,128]{2,1,0:T(8,128)(2,1)}, bf16[128,16,128]{2,1,0:T(8,128)(2,1)}, u32[]{:S(2)}, u32[]{:S(2)}) collective-permute-start(bf16[128,16,128]{2,1,0:T(8,128)(2,1)} %get-tuple-element.147), channel_id=1, source_target_pairs={{0,7},{1,6},{2,5},{3,4},{4,3},{5,2},{6,1},{7,0}} | collective-permute-start | bytes 1572872 | tf_op jit(solution)/shard_map/ppermute | solution.py:443
  519.4 37.1 %copy-start.16 = (f32[128,128]{1,0:T(8,128)S(1)}, f32[128,128]{1,0:T(8,128)}, u32[]{:S(2)}) copy-start(f32[128,128]{1,0:T(8,128)} %get-tuple-element.168) | copy-start | bytes 196612
  519.4 37.1 %copy-start.17 = (f32[128,128]{1,0:T(8,128)S(1)}, f32[128,128]{1,0:T(8,128)}, u32[]{:S(2)}) copy-start(f32[128,128]{1,0:T(8,128)} %get-tuple-element.169) | copy-start | bytes 196612
  519.4 37.1 %copy-start.18 = (f32[128,128]{1,0:T(8,128)S(1)}, f32[128,128]{1,0:T(8,128)}, u32[]{:S(2)}) copy-start(f32[128,128]{1,0:T(8,128)} %get-tuple-element.170) | copy-start | bytes 196612
  552.9 35.5 %collective-permute-start.16 = (bf16[128,16,128]{2,1,0:T(8,128)(2,1)}, bf16[128,16,128]{2,1,0:T(8,128)(2,1)S(1)}, u32[]{:S(2)}, u32[]{:S(2)}) collective-permute-start(bf16[128,16,128]{2,1,0:T(8,128)(2,1)} %get-tuple-element.136), channel_id=1, source_target_pairs={{0,4},{1,5},{2,6},{3,7},{4,0},{5,1},{6,2},{7,3}} | collective-permute-start | bytes 1572872 | tf_op jit(solution)/shard_map/ppermute | solution.py:443
  554.5 34.0 %collective-permute-start.17 = (bf16[128,16,128]{2,1,0:T(8,128)(2,1)}, bf16[128,16,128]{2,1,0:T(8,128)(2,1)S(1)}, u32[]{:S(2)}, u32[]{:S(2)}) collective-permute-start(bf16[128,16,128]{2,1,0:T(8,128)(2,1)} %get-tuple-element.137), channel_id=1, source_target_pairs={{0,5},{1,4},{2,7},{3,6},{4,1},{5,0},{6,3},{7,2}} | collective-permute-start | bytes 1572872 | tf_op jit(solution)/shard_map/ppermute | solution.py:443
  554.5 34.0 %collective-permute-start.21 = (bf16[128,16,128]{2,1,0:T(8,128)(2,1)}, bf16[128,16,128]{2,1,0:T(8,128)(2,1)S(1)}, u32[]{:S(2)}, u32[]{:S(2)}) collective-permute-start(bf16[128,16,128]{2,1,0:T(8,128)(2,1)} %get-tuple-element.142), channel_id=1, source_target_pairs={{0,2},{1,3},{2,0},{3,1},{4,6},{5,7},{6,4},{7,5}} | collective-permute-start | bytes 1572872 | tf_op jit(solution)/shard_map/ppermute | solution.py:443
  555.1 33.4 %collective-permute-start.22 = (bf16[128,16,128]{2,1,0:T(8,128)(2,1)}, bf16[128,16,128]{2,1,0:T(8,128)(2,1)S(1)}, u32[]{:S(2)}, u32[]{:S(2)}) collective-permute-start(bf16[128,16,128]{2,1,0:T(8,128)(2,1)} %get-tuple-element.143), channel_id=1, source_target_pairs={{0,3},{1,2},{2,1},{3,0},{4,7},{5,6},{6,5},{7,4}} | collective-permute-start | bytes 1572872 | tf_op jit(solution)/shard_map/ppermute | solution.py:443
  (19 other events, 349.5 us)

commit v2 on v1

v2 whole, which is shorter than its diff:
```python
import functools
import jax
import jax.numpy as jnp
from jax import lax
from jax.experimental import pallas as pl
from jax.experimental.pallas import tpu as pltpu
from jax.sharding import PartitionSpec as P

LN_EPS = 1e-5
N = 512
C = 128
NR = 64
NB = 16
NQ = NR // NB
HALF = NR // 2
HOPS = ((0, 0), (2, 4), (6, 6), (4, 2))
SB = NB + 4
SO = NR + 4
WIDE = N // 2
F32 = jnp.float32
BF16 = jnp.bfloat16
PARAMS = pltpu.CompilerParams(vmem_limit_bytes=60 << 20)
COST = pl.CostEstimate(flops=1 << 33, bytes_accessed=1 << 26, transcendentals=0)


def sds(shape, dtype):
    return jax.ShapeDtypeStruct(shape, dtype)


def full_spec(shape):
    return pl.BlockSpec(shape, lambda *ids: (0,) * len(shape))


def sigmoid(x_val):
    return 1.0 / (1.0 + jnp.exp(-x_val))


def nt_dot(lhs, rhs):
    return lax.dot_general(lhs, rhs, (((1,), (1,)), ((), ())), preferred_element_type=F32)


def nn_dot(lhs, rhs):
    return lax.dot_general(lhs, rhs, (((1,), (0,)), ((), ())), preferred_element_type=F32)


def ones_rows(width):
    return jnp.where(lax.broadcasted_iota(jnp.int32, (16, width), 0) == 0, 1.0, 0.0).astype(BF16)


def norm_rows(x_val):
    mean_val = jnp.mean(x_val, axis=0, keepdims=True)
    centered = x_val - mean_val
    inv_std = lax.rsqrt(jnp.mean(centered * centered, axis=0, keepdims=True) + LN_EPS)
    return centered * inv_std, inv_std


def put_row(scr, row, pitch, val, lane=0):
    for tile in jnp.split(val, val.shape[1] // C, axis=1):
        scr[lane, pl.ds(row, C, stride=pitch), :] = tile
        lane += 1


def get_row(scr, row, pitch, lanes):
    return jnp.concatenate([scr[lane, pl.ds(row, C, stride=pitch), :] for lane in lanes], axis=1)


def flush_rows(scr, out_ref):
    def body(ch, carry):
        for lane in range(4):
            out_ref[ch, :, C * lane:C * (lane + 1)] = scr[lane, pl.ds(ch * SB, NB), :].astype(BF16)
        return carry

    lax.fori_loop(0, C, body, 0, unroll=8)


def gated_half(w_ref, scrs, row, half, z_norm, mask_f):
    aug = jnp.concatenate([z_norm, ones_rows(WIDE)], axis=0)
    for side, scr in enumerate(scrs):
        proj = nn_dot(w_ref[2 * C * side:2 * C * (side + 1)], aug)
        put_row(scr, row, SB, mask_f * sigmoid(proj[C:]) * proj[:C], 2 * half)
    return aug


def halves():
    return ((half, slice(WIDE * half, WIDE * (half + 1))) for half in range(2))


def pair_row(ref, row, ids_ref, half):
    return jnp.concatenate([ref[row, pl.ds(pl.multiple_of(ids_ref[8 * half + p], HALF), HALF), :] for p in range(8)], axis=0)


def normed_row(z_row, scale, offset):
    z_t = z_row.T.astype(F32)
    x_hat, inv_std = norm_rows(z_t)
    z_norm = (x_hat * scale + offset).astype(BF16)
    return x_hat, inv_std, z_norm


def pass_ids(ids_ref, tok_ref):
    for p in range(17):
        tok_ref[p] = ids_ref[p]


TOKEN = sds((17,), jnp.int32)
TOKEN_SPEC = pl.BlockSpec(memory_space=pltpu.SMEM)


def load_mask(m_ref, m_scr, ids_ref):
    for half, cols in halves():
        m_scr[:, cols] = pair_row(m_ref, 0, ids_ref, half).astype(F32).T


def gated_kernel(half_id, ids_ref, z_ref, m_ref, w_ref, scale_ref, offset_ref, a_ref, b_ref, tok_ref, a_scr, b_scr, m_scr):
    pass_ids(ids_ref, tok_ref)
    load_mask(m_ref, m_scr, ids_ref)
    first = half_id * HALF + pl.program_id(0) * NB

    def body(row, carry):
        for half, cols in halves():
            _, _, z_norm = normed_row(pair_row(z_ref, row, ids_ref, half), scale_ref[...], offset_ref[...])
            gated_half(w_ref, (a_scr, b_scr), row, half, z_norm, m_scr[pl.ds(first + row, 1), cols])
        return carry

    lax.fori_loop(0, NB, body, 0, unroll=4)
    flush_rows(a_scr, a_ref)
    flush_rows(b_scr, b_ref)


def gated_call(half_id, ids, piece, mask_t, w_t, scale, offset):
    out_spec = pl.BlockSpec((C, NB, N), lambda r, ids: (0, r, 0))
    return pl.pallas_call(
        functools.partial(gated_kernel, half_id),
        grid_spec=pltpu.PrefetchScalarGridSpec(
            num_scalar_prefetch=1,
            grid=(HALF // NB,),
            in_specs=[
                pl.BlockSpec((NB, N, C), lambda r, ids: (r, 0, 0)),
                full_spec((1, N, C)),
                full_spec((4 * C, C + 16)), full_spec((C, WIDE)), full_spec((C, WIDE)),
            ],
            out_specs=[out_spec, out_spec, TOKEN_SPEC],
            scratch_shapes=[pltpu.VMEM((4, C * SB, 128), F32)] * 2 + [pltpu.VMEM((C, N), F32)],
        ),
        out_shape=[sds((C, HALF, N), BF16)] * 2 + [TOKEN],
        compiler_params=PARAMS,
        cost_estimate=COST,
        name="gated_rows",
    )(ids, piece, mask_t, w_t, scale, offset)


def lanes(val):
    half = val.shape[1] // 2
    return val[:, :half] + val[:, half:]


def own_kernel(ids_ref, z_ref, dy_ref, m_ref, w_ref, scale_ref, offset_ref, w_out_ref,
               a_ref, b_ref, dup_ref, don_ref, g1_ref, dbout_ref, dooff_ref, tok_ref, a_scr, b_scr, m_scr):
    pass_ids(ids_ref, tok_ref)

    @pl.when(pl.program_id(0) == 0)
    def _():
        dbout_ref[...] = jnp.zeros_like(dbout_ref)
        dooff_ref[...] = jnp.zeros_like(dooff_ref)

    load_mask(m_ref, m_scr, ids_ref)
    first = pl.program_id(0) * NB

    def body(row, carry):
        for half, cols in halves():
            _, _, z_norm = normed_row(pair_row(z_ref, row, ids_ref, half), scale_ref[...], offset_ref[...])
            aug = gated_half(w_ref, (a_scr, b_scr), row, half, z_norm, m_scr[pl.ds(first + row, 1), cols])
            sig_g = sigmoid(nn_dot(w_ref[4 * C:5 * C], aug))
            d_upd = sig_g * pair_row(dy_ref, row, ids_ref, half).T.astype(F32)
            g1_ref[row, :, cols] = d_upd * (1.0 - sig_g)
            d_upd16 = d_upd.astype(BF16)
            dup_ref[row, :, cols] = d_upd16
            d_onorm = nn_dot(w_out_ref[...], d_upd16).astype(BF16)
            don_ref[row, :, cols] = d_onorm
            dbout_ref[...] += lanes(d_upd16.astype(F32))
            dooff_ref[...] += lanes(d_onorm.astype(F32))
        return carry

    lax.fori_loop(0, NB, body, 0, unroll=4)
    flush_rows(a_scr, a_ref)
    flush_rows(b_scr, b_ref)


def own_call(ids, z_loc, dy_loc, m_loc, w_t, scale, offset, w_out):
    row_spec = pl.BlockSpec((NB, N, C), lambda r, ids: (r, 0, 0))
    t_spec = pl.BlockSpec((NB, C, N), lambda r, ids: (r, 0, 0))
    act_spec = pl.BlockSpec((C, NB, N), lambda r, ids: (0, r, 0))
    return pl.pallas_call(
        own_kernel,
        grid_spec=pltpu.PrefetchScalarGridSpec(
            num_scalar_prefetch=1,
            grid=(NQ,),
            in_specs=[row_spec, row_spec, full_spec((1, N, C)),
                      full_spec((5 * C, C + 16)), full_spec((C, WIDE)), full_spec((C, WIDE)), full_spec((C, C))],
            out_specs=[act_spec, act_spec, t_spec, t_spec, t_spec, full_spec((C, 128)), full_spec((C, 128)), TOKEN_SPEC],
            scratch_shapes=[pltpu.VMEM((4, C * SB, 128), F32)] * 2 + [pltpu.VMEM((C, N), F32)],
        ),
        out_shape=[sds((C, NR, N), BF16), sds((C, NR, N), BF16), sds((NR, C, N), BF16), sds((NR, C, N), BF16), sds((NR, C, N), F32), sds((C, 128), F32), sds((C, 128), F32), TOKEN],
        compiler_params=PARAMS,
        cost_estimate=COST,
        name="own_rows",
    )(ids, z_loc, dy_loc, m_loc, w_t, scale, offset, w_out)


CB = 16
CP = 32
FIRST = C // CB
LAST = FIRST + NR // NB


def out_kernel(ids_ref, a_ref, b_own0, b_own1, b_par0, b_par1, don_ref, dup_ref, g1_ref, w_out_ref, scale_ref, offset_ref,
               do_ref, dg_ref, same0, same1, cross0, cross1, dwout_ref, dosc_ref, dbg_ref, tok_ref, o_scr):
    step = pl.program_id(0)
    first_core = ids_ref[16] == 0

    @pl.when(step == 0)
    def _():
        pass_ids(ids_ref, tok_ref)
        dwout_ref[...] = jnp.zeros_like(dwout_ref)
        dosc_ref[...] = jnp.zeros_like(dosc_ref)
        dbg_ref[...] = jnp.zeros_like(dbg_ref)

    @pl.when(step < FIRST)
    def _():
        def prod(ch, carry):
            b_rows = jnp.concatenate([ref[ch] for ref in (b_own0, b_own1, b_par0, b_par1)], axis=0)
            val = nt_dot(a_ref[ch], b_rows)
            o_scr[0, pl.ds((step * CB + ch) * SO, NR), :] = jnp.where(first_core, val, pltpu.roll(val, 64, 1))
            return carry

        lax.fori_loop(0, CB, prod, 0, unroll=8)

    @pl.when((step >= FIRST) & (step < LAST))
    def _():
        def chain(row, carry):
            o_row = (step - FIRST) * NB + row
            o_hat, inv_std = norm_rows(get_row(o_scr, o_row, SO, (0,)))
            o_norm = (o_hat * scale_ref[...] + offset_ref[...]).astype(BF16)
            aug = jnp.concatenate([o_norm, ones_rows(C)], axis=0)
            upd = nn_dot(w_out_ref[...], aug).astype(BF16).astype(F32)
            d_gate = g1_ref[row] * upd
            dbg_ref[...] += d_gate
            dg_ref[row] = d_gate.astype(BF16)
            d_onorm = don_ref[row].astype(F32)
            dosc_ref[...] += d_onorm * o_hat
            grad_hat = d_onorm * scale_ref[...]
            mean_grad = jnp.mean(grad_hat, axis=0, keepdims=True)
            mean_proj = jnp.mean(grad_hat * o_hat, axis=0, keepdims=True)
            put_row(o_scr, o_row, SO, inv_std * (grad_hat - mean_grad - o_hat * mean_proj))
            dwout_ref[...] += nt_dot(o_norm, dup_ref[row])
            return carry

        lax.fori_loop(0, NB, chain, 0, unroll=8)

    @pl.when(step >= LAST)
    def _():
        lane = lax.broadcasted_iota(jnp.int32, (NB, C), 1)
        low = lane < 64
        even = lane % 64 < HALF

        def swap(left, right, keep, width):
            return jnp.where(keep, left, pltpu.roll(right, width, 1)), jnp.where(keep, pltpu.roll(left, C - width, 1), right)

        def pack(ch, carry):
            val = o_scr[0, pl.ds(((step - LAST) * CP + ch) * SO, NR), :]
            do_ref[ch] = jnp.where(first_core, val, pltpu.roll(val, 64, 1)).astype(BF16)
            g0, g1, g2, g3 = jnp.split(val, 4, axis=0)
            g0, g2 = swap(g0, g2, low, 64)
            g1, g3 = swap(g1, g3, low, 64)
            g0, g1 = swap(g0, g1, even, HALF)
            g2, g3 = swap(g2, g3, even, HALF)
            same0[ch] = jnp.where(first_core, g0, g2).astype(BF16)
            same1[ch] = jnp.where(first_core, g1, g3).astype(BF16)
            cross0[ch] = jnp.where(first_core, g2, g0).astype(BF16)
            cross1[ch] = jnp.where(first_core, g3, g1).astype(BF16)
            return carry

        lax.fori_loop(0, CP, pack, 0, unroll=4)


def piece_spec(width, blk):
    return pl.BlockSpec((width, HALF, N), lambda s, *ids: (s, blk, 0))


def prod_step(step):
    return jnp.minimum(step, FIRST - 1)


def chain_step(step):
    return jnp.clip(step - FIRST, 0, NR // NB - 1)


def pack_step(step):
    return jnp.clip(step - LAST, 0, C // CP - 1)


def out_call(chunk, ids, a_own, b_pieces, don, dup, g1, w_out_t, scale, offset):
    lane_spec = pl.BlockSpec((NB, C, C), lambda s, ids: (chain_step(s), 0, chunk))
    acc_spec = full_spec((C, C))
    pack_spec = pl.BlockSpec((CP, NB, C), lambda s, ids: (pack_step(s), 0, 0))
    b_specs = [pl.BlockSpec((CB, HALF, N), lambda s, ids, blk=blk: (prod_step(s), blk, 0)) for _, blk in b_pieces]
    return pl.pallas_call(
        out_kernel,
        grid_spec=pltpu.PrefetchScalarGridSpec(
            num_scalar_prefetch=1,
            grid=(LAST + C // CP,),
            in_specs=[pl.BlockSpec((CB, NR, N), lambda s, ids: (prod_step(s), 0, 0))] + b_specs
            + [lane_spec, lane_spec, lane_spec, full_spec((C, C + 16)), acc_spec, acc_spec],
            out_specs=[pl.BlockSpec((CP, NR, C), lambda s, ids: (pack_step(s), 0, 0)),
                       pl.BlockSpec((NB, C, C), lambda s, ids: (chain_step(s), 0, 0))] + [pack_spec] * 4 + [acc_spec] * 3 + [TOKEN_SPEC],
            scratch_shapes=[pltpu.VMEM((1, C * SO, C), F32)],
        ),
        out_shape=[sds((C, NR, C), BF16), sds((NR, C, C), BF16)] + [sds((C, NB, C), BF16)] * 4 + [sds((C, C), F32)] * 3 + [TOKEN],
        compiler_params=PARAMS,
        cost_estimate=COST,
        name="out_chain",
    )(ids, a_own, *(arr for arr, _ in b_pieces), don, dup, g1, w_out_t, scale, offset)


CK = 16


def da_kernel(*refs):
    do_refs, b_refs, da_ref = refs[:4], refs[4:20], refs[20]
    for ch in range(CK):
        do_row = jnp.concatenate([ref[ch] for ref in do_refs], axis=1)
        b_rows = jnp.concatenate([ref[ch] for ref in b_refs], axis=0)
        da_ref[ch] = nn_dot(do_row, b_rows).astype(BF16)


def da_call(do_chunks, b_pieces):
    return pl.pallas_call(
        da_kernel,
        grid=(C // CK,),
        in_specs=[pl.BlockSpec((CK, NR, 128), lambda s: (s, 0, 0))] * 4 + [piece_spec(CK, blk) for _, blk in b_pieces],
        out_specs=pl.BlockSpec((CK, NR, N), lambda s: (s, 0, 0)),
        out_shape=sds((C, NR, N), BF16),
        compiler_params=PARAMS,
        cost_estimate=COST,
        name="grad_a",
    )(*do_chunks, *(arr for arr, _ in b_pieces))


def db_kernel(*refs):
    do_refs, a_refs, db_ref = refs[:16], refs[16:32], refs[32]
    for ch in range(CK):
        x_t = [jnp.concatenate([ref[ch] for ref in do_refs[8 * h:8 * h + 8]], axis=0).T for h in range(2)]
        total = None
        for g in range(4):
            lhs = jnp.concatenate([x[32 * g:32 * g + 32] for x in x_t], axis=0)
            half, sub = divmod(g, 2)
            rhs = jnp.concatenate([ref[ch, NB * sub:NB * (sub + 1), :] for ref in a_refs[8 * half:8 * half + 8]], axis=0)
            term = nn_dot(lhs, rhs)
            total = term if total is None else total + term
        db_ref[ch] = total.astype(BF16)


def db_call(do_pieces, a_pieces):
    return pl.pallas_call(
        db_kernel,
        grid=(C // CK,),
        in_specs=[pl.BlockSpec((CK, NB, 128), lambda s: (s, 0, 0))] * 16 + [piece_spec(CK, blk) for _, blk in a_pieces],
        out_specs=pl.BlockSpec((CK, NR, N), lambda s: (s, 0, 0)),
        out_shape=sds((C, NR, N), BF16),
        compiler_params=PARAMS,
        cost_estimate=COST,
        name="grad_b",
    )(*do_pieces, *(arr for arr, _ in a_pieces))


def in_kernel(ids_ref, z_ref, dy_ref, m_ref, da_ref, db_ref, dg0, dg1, dg2, dg3, w_ref, scale_ref, offset_ref, w_cat_ref,
              dz_ref, dw_ref, dbin_ref, dsc_ref, doff_ref, a_scr, b_scr, m_scr):
    dgs = (dg0, dg1, dg2, dg3)

    @pl.when(pl.program_id(0) == 0)
    def _():
        dw_ref[...] = jnp.zeros_like(dw_ref)
        dbin_ref[...] = jnp.zeros_like(dbin_ref)
        dsc_ref[...] = jnp.zeros_like(dsc_ref)
        doff_ref[...] = jnp.zeros_like(doff_ref)

    def unpack(ch, carry):
        for src, scr in ((da_ref, a_scr), (db_ref, b_scr)):
            for lane in range(4):
                scr[lane, pl.ds(ch * SB, NB), :] = src[ch, :, C * lane:C * (lane + 1)].astype(F32)
        return carry

    lax.fori_loop(0, C, unpack, 0, unroll=4)

    load_mask(m_ref, m_scr, ids_ref)
    first = pl.program_id(0) * NB

    def lanes4(val):
        return lanes(lanes(val))

    def body(row, carry):
        def full_row(ref):
            return jnp.concatenate([pair_row(ref, row, ids_ref, half) for half in range(2)], axis=0)

        x_hat, inv_std, z_norm = normed_row(full_row(z_ref), scale_ref[...], offset_ref[...])
        aug = jnp.concatenate([z_norm, ones_rows(N)], axis=0)
        mask_f = m_scr[pl.ds(first + row, 1), :]
        parts = []
        for side, scr in ((0, a_scr), (1, b_scr)):
            proj = nn_dot(w_ref[2 * C * side:2 * C * side + C], aug)
            sig = sigmoid(nn_dot(w_ref[2 * C * side + C:2 * C * (side + 1)], aug))
            d_proj = get_row(scr, row, SB, range(4)) * mask_f * sig
            d_lin = d_proj * proj * (1.0 - sig)
            dbin_ref[side] += lanes4(d_proj)
            dbin_ref[2 + side] += lanes4(d_lin)
            parts.append((d_proj.astype(BF16), d_lin.astype(BF16)))
        d_gate = jnp.concatenate([dg[row] for dg in dgs], axis=1)
        cat = jnp.concatenate([part[kind] for kind in range(2) for part in parts] + [d_gate], axis=0)
        dw_ref[...] += nt_dot(cat, z_norm)
        d_znorm = nn_dot(w_cat_ref[...], cat).astype(BF16).astype(F32)
        dsc_ref[...] += lanes4(d_znorm * x_hat)
        doff_ref[...] += lanes4(d_znorm)
        grad_hat = d_znorm * scale_ref[...]
        mean_grad = jnp.mean(grad_hat, axis=0, keepdims=True)
        mean_proj = jnp.mean(grad_hat * x_hat, axis=0, keepdims=True)
        d_zt = inv_std * (grad_hat - mean_grad - x_hat * mean_proj)
        d_row = (full_row(dy_ref).astype(F32) + d_zt.T).astype(BF16)
        for p in range(16):
            dz_ref[row, pl.ds(pl.multiple_of(ids_ref[p], HALF), HALF), :] = d_row[HALF * p:HALF * (p + 1)]
        return carry

    lax.fori_loop(0, NB, body, 0, unroll=4)


def in_call(ids, z_loc, dy_loc, m_loc, d_a, d_b, dg_chunks, w_t, scale, offset, w_cat):
    row_spec = pl.BlockSpec((NB, N, C), lambda r, ids: (r, 0, 0))
    act_spec = pl.BlockSpec((C, NB, N), lambda r, ids: (0, r, 0))
    return pl.pallas_call(
        in_kernel,
        grid_spec=pltpu.PrefetchScalarGridSpec(
            num_scalar_prefetch=1,
            grid=(NQ,),
            in_specs=[row_spec, row_spec, full_spec((1, N, C)), act_spec, act_spec]
            + [pl.BlockSpec((NB, C, 128), lambda r, ids: (r, 0, 0))] * 4
            + [full_spec((4 * C, C + 16)), full_spec((C, N)), full_spec((C, N)), full_spec((C, 5 * C))],
            out_specs=[row_spec, full_spec((5 * C, C)), full_spec((4, C, C)), full_spec((C, 128)), full_spec((C, 128))],
            scratch_shapes=[pltpu.VMEM((4, C * SB, 128), F32)] * 2 + [pltpu.VMEM((C, N), F32)],
        ),
        out_shape=[sds((NR, N, C), BF16), sds((5 * C, C), F32), sds((4, C, C), F32), sds((C, 128), F32), sds((C, 128), F32)],
        compiler_params=PARAMS,
        cost_estimate=COST,
        name="in_backward",
    )(ids, z_loc, dy_loc, m_loc, d_a, d_b, *dg_chunks, w_t, scale, offset, w_cat)


SHARD = 112
VECS = 6 * C


def sum_kernel(*refs):
    accs, wout_refs, w_ref = refs[:7], refs[7:11], refs[11]
    win_ref, wgate_ref, wout_ref, vec_ref, src, recv, mine, total, send1, recv1, send2, recv2 = refs[12:]
    me = lax.axis_index('dap')

    def peer(step):
        return {'dap': lax.rem(me + step, 8)}

    barrier = pltpu.get_barrier_semaphore()
    for step in range(1, 8):
        pl.semaphore_signal(barrier, inc=1, device_id=peer(step), device_id_type=pl.DeviceIdType.MESH)
    for blk in range(5):
        src[C * blk:C * (blk + 1)] = w_ref[C * blk:C * (blk + 1)].T
    src[5 * C:VECS] = sum(ref[...] for ref in wout_refs[1:]) + wout_refs[0][...]
    rows = []
    for ref in accs:
        rows += [ref[n] for n in range(4)] if len(ref.shape) > 2 else [ref[...]]
    rows = [jnp.sum(val.T, axis=0, keepdims=True) for val in rows]
    src[VECS:] = jnp.concatenate(rows + [jnp.zeros((8 * SHARD - VECS - len(rows), C), F32)], axis=0)
    pl.semaphore_wait(barrier, 7)

    def shard(owner):
        return pl.ds(pl.multiple_of(owner * SHARD, 16), SHARD)

    copies = []
    for step in range(1, 8):
        copy = pltpu.make_async_remote_copy(
            src_ref=src.at[shard(lax.rem(me + step, 8))], dst_ref=recv.at[step], send_sem=send1.at[step], recv_sem=recv1.at[step],
            device_id=peer(step), device_id_type=pl.DeviceIdType.MESH)
        copy.start()
        copies.append(copy)
    val = src[shard(me), :]
    for step, copy in enumerate(copies):
        copy.wait()
        val += recv[step + 1]
    mine[...] = val.astype(BF16)
    total[shard(me), :] = val.astype(BF16)
    copies = []
    for step in range(1, 8):
        copy = pltpu.make_async_remote_copy(
            src_ref=mine, dst_ref=total.at[shard(me)], send_sem=send2.at[step], recv_sem=recv2.at[step],
            device_id=peer(step), device_id_type=pl.DeviceIdType.MESH)
        copy.start()
        copies.append(copy)
    for copy in copies:
        copy.wait()
    for blk in range(4):
        win_ref[:, C * blk:C * (blk + 1)] = total[C * blk:C * (blk + 1)]
    wgate_ref[...] = total[4 * C:5 * C]
    wout_ref[...] = total[5 * C:VECS]
    vec_ref[...] = total[VECS:VECS + 16]


def sum_call(accs, wouts, acc_w):
    args = [*accs, *wouts, acc_w]
    outs = [sds((C, 4 * C), BF16), sds((C, C), BF16), sds((C, C), BF16), sds((16, C), BF16)]
    return pl.pallas_call(
        sum_kernel,
        in_specs=[pl.BlockSpec(memory_space=pltpu.VMEM)] * len(args),
        out_specs=[pl.BlockSpec(memory_space=pltpu.VMEM)] * len(outs),
        out_shape=outs,
        scratch_shapes=[pltpu.VMEM((8 * SHARD, C), F32), pltpu.VMEM((8, SHARD, C), F32), pltpu.VMEM((SHARD, C), BF16), pltpu.VMEM((8 * SHARD, C), BF16)]
        + [pltpu.SemaphoreType.DMA((8,))] * 4,
        compiler_params=pltpu.CompilerParams(collective_id=0, has_side_effects=True),
        cost_estimate=COST,
        name="sum_grads",
    )(*args)


def aug_weight(w_mat, bias):
    wide = jnp.zeros((w_mat.shape[1], 16), BF16).at[:, 0].set(bias)
    return jnp.concatenate([w_mat.T, wide], axis=1)


def column(vec, width):
    return jnp.broadcast_to(vec.astype(F32)[:, None], (C, width))


def local_grads(z_loc, mask_loc, dy_loc, ln_in_scale, ln_in_offset, w_in, b_in, ln_out_scale, ln_out_offset, w_out, b_out, w_gate, b_gate):
    me = lax.axis_index('dap')
    chip, core = me // 2, me % 2
    w_cat = jnp.concatenate([w_in, w_gate], axis=1)
    pa, pb, la, lb, gate = jnp.split(jnp.concatenate([w_cat, jnp.concatenate([b_in, b_gate])[None]], axis=0), 5, axis=1)
    w_t = jnp.concatenate([pa, la, pb, lb, gate], axis=1)
    w_t = aug_weight(w_t[:C], w_t[C])
    w_out_t = aug_weight(w_out, b_out)
    (in_scale, in_offset), wide_in = ((column(ln_in_scale, width), column(ln_in_offset, width)) for width in (WIDE, N))
    out_scale, out_offset = column(ln_out_scale, 128), column(ln_out_offset, 128)

    order = [((chip * 2) ^ HOPS[q][h]) * NR + core_of * NR + h * HALF for q in range(4) for core_of in range(2) for h in range(2)]
    ids = jnp.stack(order + [core]).astype(jnp.int32)
    mask_t = jnp.pad(mask_loc.T.astype(BF16), ((0, 0), (0, C - NR)))[None]

    def move(val, flips):
        return lax.ppermute(val, 'dap', [(d, d ^ flips) for d in range(8)])

    top, bottom = z_loc[:HALF], z_loc[HALF:]
    gathered = {}
    gathered[1, 0], gathered[1, 1] = move(top, HOPS[1][0]), move(bottom, HOPS[1][1])
    masks = {hop: move(mask_t, hop) for hop in (2, 4, 6)}
    gathered[2, 0], gathered[2, 1] = move(gathered[1, 0], HOPS[1][1]), move(gathered[1, 1], HOPS[1][0])
    gathered[3, 0], gathered[3, 1] = move(top, HOPS[3][0]), move(bottom, HOPS[3][1])

    a_own, b_own, dup, don, g1, acc_bout, acc_ooff, ids = own_call(ids, z_loc, dy_loc, mask_t, w_t, in_scale, in_offset, w_out)
    b_par, a_par = move(b_own, 1), move(a_own, 1)
    a_at = {(0, h, f): (val, h) for h in range(2) for f, val in ((0, a_own), (1, a_par))}
    b_at = {(0, h, f): (val, h) for h in range(2) for f, val in ((0, b_own), (1, b_par))}
    do_at, do_chunks, dg_chunks, sums = {}, [], [], []
    for q in range(4):
        for h in range(2):
            if q:
                act_a, act_b, ids = gated_call(h, ids, gathered[q, h], masks[HOPS[q][h]], w_t[:4 * C], in_scale, in_offset)
                a_at[q, h, 0], b_at[q, h, 0] = (act_a, 0), (act_b, 0)
                b_at[q, h, 1] = move(act_b, 1), 0
                a_at[q, h, 1] = move(act_a, 1), 0
        b_pieces = [b_at[q, h, f] for f in range(2) for h in range(2)]
        do_own, dg, same0, same1, cross0, cross1, *acc, ids = out_call(q, ids, a_own, b_pieces, don, dup, g1, w_out_t, out_scale, out_offset)
        do_chunks.append(do_own)
        dg_chunks.append(dg)
        sums.append(acc)
        for flip, h, val in ((0, 0, same0), (0, 1, same1), (1, 0, cross0), (1, 1, cross1)):
            flips = HOPS[q][h] ^ flip
            do_at[h, flips] = move(val, flips) if flips else val
    d_a = da_call(do_chunks, [b_at[q, h, f] for q in range(4) for f in range(2) for h in range(2)])
    chunk_of = {(HOPS[q][h], h): q for q in range(4) for h in range(2)}
    d_b = db_call([do_at[h, s] for h in range(2) for s in range(8)],
                  [a_at[chunk_of[s & 6, h], h, s & 1] for h in range(2) for s in range(8)])
    d_z, acc_w, acc_bin, acc_isc, acc_ioff = in_call(ids, z_loc, dy_loc, mask_t, d_a, d_b, dg_chunks, w_t[:4 * C], *wide_in, w_cat)

    wouts, oscs, bgs = zip(*sums)
    accs = (acc_isc, acc_ioff, acc_bin, sum(oscs), acc_ooff, acc_bout, sum(bgs))
    d_win, d_wgate, d_wout, vecs = sum_call(accs, wouts, acc_w)
    d_isc, d_ioff, d_osc, d_ooff, d_bout, d_bg = (vecs[n] for n in (0, 1, 6, 7, 8, 9))
    return d_z, d_isc, d_ioff, d_win, vecs[2:6].reshape(4 * C), d_osc, d_ooff, d_wout, d_bout, d_wgate, d_bg


def solution(mesh):
    pair_spec = P(('batch', 'dap'), None, None)
    mask_spec = P(('batch', 'dap'), None)
    vec_rep = P(None)
    mat_rep = P(None, None)
    vec_part = P('batch')
    mat_part = P('batch', None)
    in_specs = (pair_spec, mask_spec, pair_spec, vec_rep, vec_rep, mat_rep, vec_rep, vec_rep, vec_rep, mat_rep, vec_rep, mat_rep, vec_rep)
    out_specs = (pair_spec, vec_part, vec_part, mat_part, vec_part, vec_part, vec_part, mat_part, vec_part, mat_part, vec_part)
    return jax.shard_map(local_grads, mesh=mesh, in_specs=in_specs, out_specs=out_specs, check_vma=False)
```

time: 715 us -> 653 us (0.913)
  Pallas kernels: 416 us -> 370 us
  blocking collectives: 27.3 us -> 0 us
  local copies, waits for them, and re-layouts: 18.3 us -> 27.9 us
  other arithmetic: 14.2 us -> 5.62 us
    psum x1 -> x0, blocking collectives: 27.3 us -> none  [local_grads(): lax.psum((jnp.concatenate(vecs), acc_w, acc_wout), 'dap')]
    pallas_call x1, Pallas kernels: 55.5 us -> 38.6 us  [own_call(): pl.pallas_call(own_kernel, grid_spec=pltpu.PrefetchScalarGridSpec(num_sca...]
    pallas_call x4, Pallas kernels: 129 us -> 114 us  [out_call(): pl.pallas_call(out_kernel, grid_spec=pltpu.PrefetchScalarGridSpec(num_sca...]
    ppermute x34 -> x37, starting transfers between devices: 25.9 us -> 31 us  [move(): return lax.ppermute(val, 'dap', [(d, d ^ flips) for d in range(8)])]
    ppermute x34 -> x37, waiting for transfers between devices: 212 us -> 216 us  [move(): return lax.ppermute(val, 'dap', [(d, d ^ flips) for d in range(8)])]
    pallas_call x6 -> x7, Pallas kernels: 109 us -> 107 us  [the longest x6 90.9 us: gated_call(): pl.pallas_call(functools.partial(gated_kernel, half_id), grid_spec=pltpu....]
  transfers between devices with their start and end apart: 34 -> 37, of which waited for: 9 -> 10; matrix products, arithmetic and copies ran while one was open for 2% -> 2% of each run, Pallas kernels for 38% -> 36%
where the time goes in v2:
time: 653 us; the launch traced here: 652 us
  Pallas kernels  370 us (57%)
  waiting for transfers between devices  216 us (33%)
  starting transfers between devices  31 us (5%)
  local copies, waits for them, and re-layouts  27.9 us (4%)
    ppermute x37, waiting for transfers between devices, move(): return lax.ppermute(val, 'dap', [(d, d ^ flips) for d in range(8)])  216 us
    pallas_call x4, Pallas kernels, out_call(): pl.pallas_call(out_kernel, grid_spec=pltpu.PrefetchScalarGridSpec(num_sca...  114 us
    pallas_call x6, Pallas kernels, gated_call(): pl.pallas_call(functools.partial(gated_kernel, half_id), grid_spec=pltpu....  90.9 us
    pallas_call x1, Pallas kernels, in_call(): pl.pallas_call(in_kernel, grid_spec=pltpu.PrefetchScalarGridSpec(num_scal...  54.3 us
    pallas_call x1, Pallas kernels, own_call(): pl.pallas_call(own_kernel, grid_spec=pltpu.PrefetchScalarGridSpec(num_sca...  38.6 us
    ppermute x37, starting transfers between devices, move(): return lax.ppermute(val, 'dap', [(d, d ^ flips) for d in range(8)])  31 us
    pallas_call x1, Pallas kernels, db_call(): pl.pallas_call(db_kernel, grid=(C // CK,), in_specs=[pl.BlockSpec((CK, NB...  27.8 us
    pallas_call x1, Pallas kernels, da_call(): pl.pallas_call(da_kernel, grid=(C // CK,), in_specs=[pl.BlockSpec((CK, NR...  27.7 us
  transfers between devices with their start and end apart: 37, of which 10 were waited for; matrix products, arithmetic and copies ran while one was open for 2% of the time, Pallas kernels for 36%

profile of v2, /device:TPU:0, one launch (start us, length us, event | category | flops | bytes accessed | tf_op | source)
XLA Modules:
  0.0 651.7 jit_solution(9177778247056866863)
XLA Ops:
  6.7 0.9 copy.36.w_ref
  8.3 1.4 broadcast_in_dim.18.scale_ref
  9.7 1.4 broadcast_in_dim.19.offset_ref
  11.1 38.6 %own_rows.1 = (bf16[128,64,512]{2,1,0:T(8,128)(2,1)}, bf16[128,64,512]{2,1,0:T(8,128)(2,1)}, bf16[64,128,512]{2,1,0:T(8,128)(2,1)}, bf16[64,128,512]{2,1,0:T(8,1...) custom-call(s32[17]{0:T(128)} %stack.71.ids_ref, ...), custom_call_target="tpu_custom_call" | custom-call | flops 8589934592 | bytes 67108864 | tf_op jit(solution)/shard_map/own_rows/pallas_call | solution.py:192
  50.7 6.0 fusion.23
  56.7 2.5 collective-permute-start.1
  59.2 1.5 collective-permute-start.3
  65.2 28.2 %out_chain.4 = (bf16[128,64,128]{2,1,0:T(8,128)(2,1)}, bf16[64,128,128]{2,1,0:T(8,128)(2,1)}, bf16[128,16,128]{2,1,0:T(8,128)(2,1)}, bf16[128,16,128]{2,1,0:T(8,...) custom-call(s32[17]{0:T(128)} %get-tuple-element.110.ids_ref, ...), custom_call_target="tpu_custom_call" | custom-call | flops 8589934592 | bytes 67108864 | tf_op jit(solution)/shard_map/out_chain/pallas_call | solution.py:306
  93.4 60.0 %collective-permute-done.2.m_ref = bf16[1,512,128]{2,1,0:T(8,128)(2,1)S(1)} collective-permute-done((bf16[1,512,128]{2,1,0:T(8,128)(2,1)S(1)}, bf16[1,512,128]{2,1,0:T(8,128)(2,1)S(1)}, u32[]{:S(2)}, u32[]{:S(2)}) %collective-permute-start.2) | collective-permute-done | bytes 131104 | tf_op jit(solution)/shard_map/ppermute | solution.py:553
  154.1 15.1 %gated_rows.6 = (bf16[128,32,512]{2,1,0:T(8,128)(2,1)}, bf16[128,32,512]{2,1,0:T(8,128)(2,1)}, s32[17]{0:T(128)}) custom-call(s32[17]{0:T(128)} %get-tuple-element.116.ids_ref, bf16[32,512,128]{2,1,0:T(8,128)(2,1)} %collective-permute-done.1.z_ref, bf16[1,512,128]{2,1,0:T(8,128)(2,1)} %copy-done.30, bf16[512,144]{1,0:T(8,128)(2,1)} %copy.39.w_ref, ...), custom_call_target="tpu_custom_call" | custom-call | flops 8589934592 | bytes 67108864 | tf_op jit(solution)/shard_map/gated_rows/pallas_call | solution.py:131
  169.8 15.1 %gated_rows.7 = (bf16[128,32,512]{2,1,0:T(8,128)(2,1)}, bf16[128,32,512]{2,1,0:T(8,128)(2,1)}, s32[17]{0:T(128)}) custom-call(s32[17]{0:T(128)} %get-tuple-element.117.ids_ref, bf16[32,512,128]{2,1,0:T(8,128)(2,1)} %collective-permute-done.3.z_ref, bf16[1,512,128]{2,1,0:T(8,128)(2,1)} %copy-done.31, bf16[512,144]{1,0:T(8,128)(2,1)} %copy.39.w_ref, ...), custom_call_target="tpu_custom_call" | custom-call | flops 8589934592 | bytes 67108864 | tf_op jit(solution)/shard_map/gated_rows/pallas_call | solution.py:131
  185.5 1.8 collective-permute-start.7
  187.2 1.5 collective-permute-start.9
  189.0 1.8 collective-permute-start.12
  190.7 1.9 collective-permute-done.6.b_par1.refs_11_
  193.0 28.6 %out_chain.5 = (bf16[128,64,128]{2,1,0:T(8,128)(2,1)}, bf16[64,128,128]{2,1,0:T(8,128)(2,1)}, bf16[128,16,128]{2,1,0:T(8,128)(2,1)}, bf16[128,16,128]{2,1,0:T(8,...) custom-call(s32[17]{0:T(128)} %get-tuple-element.118.ids_ref, ...), custom_call_target="tpu_custom_call" | custom-call | flops 8589934592 | bytes 67108864 | tf_op jit(solution)/shard_map/out_chain/pallas_call | solution.py:306
  221.6 60.8 %collective-permute-done.8.m_ref = bf16[1,512,128]{2,1,0:T(8,128)(2,1)S(1)} collective-permute-done((bf16[1,512,128]{2,1,0:T(8,128)(2,1)S(1)}, bf16[1,512,128]{2,1,0:T(8,128)(2,1)S(1)}, u32[]{:S(2)}, u32[]{:S(2)}) %collective-permute-start.8) | collective-permute-done | bytes 131104 | tf_op jit(solution)/shard_map/ppermute | solution.py:553
  283.0 15.3 %gated_rows.8 = (bf16[128,32,512]{2,1,0:T(8,128)(2,1)}, bf16[128,32,512]{2,1,0:T(8,128)(2,1)}, s32[17]{0:T(128)}) custom-call(s32[17]{0:T(128)} %get-tuple-element.121.ids_ref, bf16[32,512,128]{2,1,0:T(8,128)(2,1)} %collective-permute-done.7.z_ref, bf16[1,512,128]{2,1,0:T(8,128)(2,1)} %copy-done.32, bf16[512,144]{1,0:T(8,128)(2,1)} %copy.39.w_ref, ...), custom_call_target="tpu_custom_call" | custom-call | flops 8589934592 | bytes 67108864 | tf_op jit(solution)/shard_map/gated_rows/pallas_call | solution.py:131
  298.3 15.0 %gated_rows.9 = (bf16[128,32,512]{2,1,0:T(8,128)(2,1)}, bf16[128,32,512]{2,1,0:T(8,128)(2,1)}, s32[17]{0:T(128)}) custom-call(s32[17]{0:T(128)} %get-tuple-element.122.ids_ref, bf16[32,512,128]{2,1,0:T(8,128)(2,1)} %collective-permute-done.9.z_ref, bf16[1,512,128]{2,1,0:T(8,128)(2,1)} %copy-done.32, bf16[512,144]{1,0:T(8,128)(2,1)} %copy.39.w_ref, ...), custom_call_target="tpu_custom_call" | custom-call | flops 8589934592 | bytes 67108864 | tf_op jit(solution)/shard_map/gated_rows/pallas_call | solution.py:131
  313.8 1.7 collective-permute-start.13
  315.5 55.5 %collective-permute-done.12.z_ref = bf16[32,512,128]{2,1,0:T(8,128)(2,1)} collective-permute-done((bf16[32,512,128]{2,1,0:T(8,128)(2,1)}, bf16[32,512,128]{2,1,0:T(8,128)(2,1)}, u32[]{:S(2)}, u32[]{:S(2)}) %collective-permute-start.12) | collective-permute-done | bytes 4194336 | tf_op jit(solution)/shard_map/ppermute | solution.py:553
  371.6 28.9 %out_chain.6 = (bf16[128,64,128]{2,1,0:T(8,128)(2,1)}, bf16[64,128,128]{2,1,0:T(8,128)(2,1)}, bf16[128,16,128]{2,1,0:T(8,128)(2,1)}, bf16[128,16,128]{2,1,0:T(8,...) custom-call(s32[17]{0:T(128)} %get-tuple-element.123.ids_ref, ...), custom_call_target="tpu_custom_call" | custom-call | flops 8589934592 | bytes 67108864 | tf_op jit(solution)/shard_map/out_chain/pallas_call | solution.py:306
  400.4 6.2 collective-permute-done.13.z_ref
  407.1 15.2 %gated_rows.10 = (bf16[128,32,512]{2,1,0:T(8,128)(2,1)}, bf16[128,32,512]{2,1,0:T(8,128)(2,1)}, s32[17]{0:T(128)}) custom-call(s32[17]{0:T(128)} %get-tuple-element.126.ids_ref, bf16[32,512,128]{2,1,0:T(8,128)(2,1)} %collective-permute-done.12.z_ref, bf16[1,512,128]{2,1,0:T(8,128)(2,1)} %copy-done.31, bf16[512,144]{1,0:T(8,128)(2,1)} %copy.39.w_ref, ...), custom_call_target="tpu_custom_call" | custom-call | flops 8589934592 | bytes 67108864 | tf_op jit(solution)/shard_map/gated_rows/pallas_call | solution.py:131
  422.3 1.7 collective-permute-start.17
  424.1 1.5 collective-permute-start.26
  425.9 15.2 %gated_rows.11 = (bf16[128,32,512]{2,1,0:T(8,128)(2,1)}, bf16[128,32,512]{2,1,0:T(8,128)(2,1)}, s32[17]{0:T(128)}) custom-call(s32[17]{0:T(128)} %get-tuple-element.127.ids_ref, bf16[32,512,128]{2,1,0:T(8,128)(2,1)} %collective-permute-done.13.z_ref, bf16[1,512,128]{2,1,0:T(8,128)(2,1)} %copy-done.30, bf16[512,144]{1,0:T(8,128)(2,1)} %copy.39.w_ref, ...), custom_call_target="tpu_custom_call" | custom-call | flops 8589934592 | bytes 67108864 | tf_op jit(solution)/shard_map/gated_rows/pallas_call | solution.py:131
  441.4 5.6 collective-permute-done.18.refs_3_
  447.5 1.4 collective-permute-start.27
  448.8 12.6 %collective-permute-done.27.refs_13_ = bf16[128,16,128]{2,1,0:T(8,128)(2,1)S(1)} collective-permute-done((bf16[128,16,128]{2,1,0:T(8,128)(2,1)S(1)}, bf16[128,16,128]{2,1,0:T(8,128)(2,1)S(1)}, u32[]{:S(2)}, u32[]{:S(2)}) %collective-permute-start.27) | collective-permute-done | bytes 524320 | tf_op jit(solution)/shard_map/ppermute | solution.py:553
  462.0 2.7 collective-permute-start.21
  464.7 12.4 %collective-permute-done.21.refs_6_ = bf16[128,16,128]{2,1,0:T(8,128)(2,1)S(1)} collective-permute-done((bf16[128,16,128]{2,1,0:T(8,128)(2,1)}, bf16[128,16,128]{2,1,0:T(8,128)(2,1)S(1)}, u32[]{:S(2)}, u32[]{:S(2)}) %collective-permute-start.21) | collective-permute-done | bytes 524320 | tf_op jit(solution)/shard_map/ppermute | solution.py:553
  477.1 1.5 collective-permute-start.22
  478.6 1.2 collective-permute-start.28
  479.8 2.3 collective-permute-start.29
  482.1 28.7 %out_chain.7 = (bf16[128,64,128]{2,1,0:T(8,128)(2,1)}, bf16[64,128,128]{2,1,0:T(8,128)(2,1)}, bf16[128,16,128]{2,1,0:T(8,128)(2,1)}, bf16[128,16,128]{2,1,0:T(8,...) custom-call(s32[17]{0:T(128)} %get-tuple-element.128.ids_ref, ...), custom_call_target="tpu_custom_call" | custom-call | flops 8589934592 | bytes 67108864 | tf_op jit(solution)/shard_map/out_chain/pallas_call | solution.py:306
  511.0 1.6 add_add_fusion
  513.5 1.2 collective-permute-done.29.refs_15_
  514.7 1.5 collective-permute-start.24
  516.2 27.7 %grad_a.1.da_ref = bf16[128,64,512]{2,1,0:T(8,128)(2,1)} custom-call(bf16[128,64,128]{2,1,0:T(8,128)(2,1)} %get-tuple-element.132.refs_0_, bf16[128,64,128]{2,1,0:T(8,128)(2,1)} %get-tuple-element.133.refs_1_, bf16[128,64,128]{2,1,0:T(8,128)(2,1)} %get-tuple-element.134.refs_2_, bf16[128,64,128]{2,1,0:T(8,128)(2,1)} %get-tuple-element.135.refs_3_, ...), custom_call_target="tpu_custom_call" | custom-call | flops 8589934592 | bytes 67108864 | tf_op jit(solution)/shard_map/grad_a/pallas_call | solution.py:336
  545.3 27.8 %grad_b.1.db_ref = bf16[128,64,512]{2,1,0:T(8,128)(2,1)} custom-call(bf16[128,16,128]{2,1,0:T(8,128)(2,1)} %get-tuple-element.136.refs_0_, bf16[128,16,128]{2,1,0:T(8,128)(2,1)} %copy-done.1, bf16[128,16,128]{2,1,0:T(8,128)(2,1)} %copy-done.3, bf16[128,16,128]{2,1,0:T(8,128)(2,1)} %copy-done.4, bf16[128,16,128]{2,1,0:T(8,128)(2,1)} %copy-done.10, ...), custom_call_target="tpu_custom_call" | custom-call | flops 8589934592 | bytes 67108864 | tf_op jit(solution)/shard_map/grad_b/pallas_call | solution.py:363
  574.6 54.3 %in_backward.1 = (bf16[64,512,128]{2,1,0:T(8,128)(2,1)}, f32[640,128]{1,0:T(8,128)}, f32[4,128,128]{2,1,0:T(8,128)}, f32[128,128]{1,0:T(8,128)}, f32[128,128]{1,0:T(8,128)}) custom-call(s32[17]{0:T(128)} %get-tuple-element.131.ids_ref, bf16[64,512,128]{2,1,0:T(8,128)(2,1)} %z_ref.3, bf16[64,512,128]{2,1,0:T(8,128)(2,1)} %dy_ref.3, ...), custom_call_target="tpu_custom_call" | custom-call | flops 8589934592 | bytes 67108864 | tf_op jit(solution)/shard_map/in_backward/pallas_call | solution.py:437
  629.0 15.8 %sum_grads.1 = (bf16[128,512]{1,0:T(8,128)(2,1)}, bf16[128,128]{1,0:T(8,128)(2,1)}, bf16[128,128]{1,0:T(8,128)(2,1)}, bf16[16,128]{1,0:T(8,128)(2,1)}) custom-call(f32[128,128]{1,0:T(8,128)} %get-tuple-element.163.refs_0_, f32[128,128]{1,0:T(8,128)} %get-tuple-element.164.refs_1_, f32[4,128,128]{2,1,0:T(8,128)} %get-tuple-element.165.refs_2_, ...), custom_call_target="tpu_custom_call" | custom-call | flops 8589934592 | bytes 67108864 | tf_op jit(solution)/shard_map/sum_grads/pallas_call | solution.py:515
  644.8 1.4 slice_bitcast_fusion.2
  646.1 1.2 slice_bitcast_fusion.1
  647.4 1.6 copy.50
  648.9 1.4 copy.51
  650.3 1.4 copy.52
  (142 shorter events, 22.1 us)
Async XLA Ops:
  49.8 14.0 %collective-permute-start = (bf16[128,64,512]{2,1,0:T(8,128)(2,1)}, bf16[128,64,512]{2,1,0:T(8,128)(2,1)}, u32[]{:S(2)}, u32[]{:S(2)}) collective-permute-start(bf16[128,64,512]{2,1,0:T(8,128)(2,1)} %get-tuple-element.112.b_own0.b_own1.refs_4_.refs_5_), channel_id=1, source_target_pairs={{0,1},{1,0},{2,3},{3,2},{4,5},{5,4},{6,7},{7,6}} | collective-permute-start | bytes 25165832 | tf_op jit(solution)/shard_map/ppermute | solution.py:553
  56.7 96.7 %collective-permute-start.1 = (bf16[32,512,128]{2,1,0:T(8,128)(2,1)}, bf16[32,512,128]{2,1,0:T(8,128)(2,1)}, u32[]{:S(2)}, u32[]{:S(2)}) collective-permute-start(bf16[32,512,128]{2,1,0:T(8,128)(2,1)} %get-tuple-element.186), channel_id=1, source_target_pairs={{0,2},{1,3},{2,0},{3,1},{4,6},{5,7},{6,4},{7,5}} | collective-permute-start | bytes 12582920 | tf_op jit(solution)/shard_map/ppermute | solution.py:553
  59.2 110.0 %collective-permute-start.3 = (bf16[32,512,128]{2,1,0:T(8,128)(2,1)}, bf16[32,512,128]{2,1,0:T(8,128)(2,1)}, u32[]{:S(2)}, u32[]{:S(2)}) collective-permute-start(bf16[32,512,128]{2,1,0:T(8,128)(2,1)} %get-tuple-element.185), channel_id=1, source_target_pairs={{0,4},{1,5},{2,6},{3,7},{4,0},{5,1},{6,2},{7,3}} | collective-permute-start | bytes 12582920 | tf_op jit(solution)/shard_map/ppermute | solution.py:553
  60.7 92.7 %collective-permute-start.2 = (bf16[1,512,128]{2,1,0:T(8,128)(2,1)S(1)}, bf16[1,512,128]{2,1,0:T(8,128)(2,1)S(1)}, u32[]{:S(2)}, u32[]{:S(2)}) collective-permute-start(bf16[1,512,128]{2,1,0:T(8,128)(2,1)S(1)} %copy-done.14), channel_id=1, source_target_pairs={{0,2},{1,3},{2,0},{3,1},{4,6},{5,7},{6,4},{7,5}} | collective-permute-start | bytes 393224 | tf_op jit(solution)/shard_map/ppermute | solution.py:553
  61.3 107.9 %collective-permute-start.4 = (bf16[1,512,128]{2,1,0:T(8,128)(2,1)S(1)}, bf16[1,512,128]{2,1,0:T(8,128)(2,1)S(1)}, u32[]{:S(2)}, u32[]{:S(2)}) collective-permute-start(bf16[1,512,128]{2,1,0:T(8,128)(2,1)S(1)} %copy-done.14), channel_id=1, source_target_pairs={{0,4},{1,5},{2,6},{3,7},{4,0},{5,1},{6,2},{7,3}} | collective-permute-start | bytes 393224 | tf_op jit(solution)/shard_map/ppermute | solution.py:553
  169.2 19.8 %collective-permute-start.5 = (bf16[128,32,512]{2,1,0:T(8,128)(2,1)}, bf16[128,32,512]{2,1,0:T(8,128)(2,1)}, u32[]{:S(2)}, u32[]{:S(2)}) collective-permute-start(bf16[128,32,512]{2,1,0:T(8,128)(2,1)} %get-tuple-element.119.b_own0.refs_8_), channel_id=1, source_target_pairs={{0,1},{1,0},{2,3},{3,2},{4,5},{5,4},{6,7},{7,6}} | collective-permute-start | bytes 12582920 | tf_op jit(solution)/shard_map/ppermute | solution.py:553
  185.0 7.6 %collective-permute-start.6 = (bf16[128,32,512]{2,1,0:T(8,128)(2,1)}, bf16[128,32,512]{2,1,0:T(8,128)(2,1)}, u32[]{:S(2)}, u32[]{:S(2)}) collective-permute-start(bf16[128,32,512]{2,1,0:T(8,128)(2,1)} %get-tuple-element.120.b_own1.refs_9_), channel_id=1, source_target_pairs={{0,1},{1,0},{2,3},{3,2},{4,5},{5,4},{6,7},{7,6}} | collective-permute-start | bytes 12582920 | tf_op jit(solution)/shard_map/ppermute | solution.py:553
  185.5 96.9 %collective-permute-start.7 = (bf16[32,512,128]{2,1,0:T(8,128)(2,1)}, bf16[32,512,128]{2,1,0:T(8,128)(2,1)}, u32[]{:S(2)}, u32[]{:S(2)}) collective-permute-start(bf16[32,512,128]{2,1,0:T(8,128)(2,1)} %collective-permute-done.1.z_ref), channel_id=1, source_target_pairs={{0,4},{1,5},{2,6},{3,7},{4,0},{5,1},{6,2},{7,3}} | collective-permute-start | bytes 12582920 | tf_op jit(solution)/shard_map/ppermute | solution.py:553
  187.2 111.0 %collective-permute-start.9 = (bf16[32,512,128]{2,1,0:T(8,128)(2,1)}, bf16[32,512,128]{2,1,0:T(8,128)(2,1)}, u32[]{:S(2)}, u32[]{:S(2)}) collective-permute-start(bf16[32,512,128]{2,1,0:T(8,128)(2,1)} %collective-permute-done.3.z_ref), channel_id=1, source_target_pairs={{0,2},{1,3},{2,0},{3,1},{4,6},{5,7},{6,4},{7,5}} | collective-permute-start | bytes 12582920 | tf_op jit(solution)/shard_map/ppermute | solution.py:553
  188.7 93.6 %collective-permute-start.8 = (bf16[1,512,128]{2,1,0:T(8,128)(2,1)S(1)}, bf16[1,512,128]{2,1,0:T(8,128)(2,1)S(1)}, u32[]{:S(2)}, u32[]{:S(2)}) collective-permute-start(bf16[1,512,128]{2,1,0:T(8,128)(2,1)S(1)} %copy-done.14), channel_id=1, source_target_pairs={{0,6},{1,7},{2,4},{3,5},{4,2},{5,3},{6,0},{7,1}} | collective-permute-start | bytes 393224 | tf_op jit(solution)/shard_map/ppermute | solution.py:553
  189.0 182.0 %collective-permute-start.12 = (bf16[32,512,128]{2,1,0:T(8,128)(2,1)}, bf16[32,512,128]{2,1,0:T(8,128)(2,1)}, u32[]{:S(2)}, u32[]{:S(2)}) collective-permute-start(bf16[32,512,128]{2,1,0:T(8,128)(2,1)} %get-tuple-element.186), channel_id=1, source_target_pairs={{0,4},{1,5},{2,6},{3,7},{4,0},{5,1},{6,2},{7,3}} | collective-permute-start | bytes 12582920 | tf_op jit(solution)/shard_map/ppermute | solution.py:553
  192.6 214.0 %collective-permute-start.30 = (bf16[128,64,512]{2,1,0:T(8,128)(2,1)}, bf16[128,64,512]{2,1,0:T(8,128)(2,1)}, u32[]{:S(2)}, u32[]{:S(2)}) collective-permute-start(bf16[128,64,512]{2,1,0:T(8,128)(2,1)} %get-tuple-element.111.a_ref.refs_16_.refs_24_), channel_id=1, source_target_pairs={{0,1},{1,0},{2,3},{3,2},{4,5},{5,4},{6,7},{7,6}} | collective-permute-start | bytes 25165832 | tf_op jit(solution)/shard_map/ppermute | solution.py:553
  298.3 72.7 %collective-permute-start.10 = (bf16[128,32,512]{2,1,0:T(8,128)(2,1)}, bf16[128,32,512]{2,1,0:T(8,128)(2,1)}, u32[]{:S(2)}, u32[]{:S(2)}) collective-permute-start(bf16[128,32,512]{2,1,0:T(8,128)(2,1)} %get-tuple-element.124.b_own0.refs_12_), channel_id=1, source_target_pairs={{0,1},{1,0},{2,3},{3,2},{4,5},{5,4},{6,7},{7,6}} | collective-permute-start | bytes 12582920 | tf_op jit(solution)/shard_map/ppermute | solution.py:553
  313.3 58.2 %collective-permute-start.11 = (bf16[128,32,512]{2,1,0:T(8,128)(2,1)}, bf16[128,32,512]{2,1,0:T(8,128)(2,1)}, u32[]{:S(2)}, u32[]{:S(2)}) collective-permute-start(bf16[128,32,512]{2,1,0:T(8,128)(2,1)} %get-tuple-element.125.b_own1.refs_13_), channel_id=1, source_target_pairs={{0,1},{1,0},{2,3},{3,2},{4,5},{5,4},{6,7},{7,6}} | collective-permute-start | bytes 12582920 | tf_op jit(solution)/shard_map/ppermute | solution.py:553
  313.8 92.8 %collective-permute-start.13 = (bf16[32,512,128]{2,1,0:T(8,128)(2,1)}, bf16[32,512,128]{2,1,0:T(8,128)(2,1)}, u32[]{:S(2)}, u32[]{:S(2)}) collective-permute-start(bf16[32,512,128]{2,1,0:T(8,128)(2,1)} %get-tuple-element.185), channel_id=1, source_target_pairs={{0,2},{1,3},{2,0},{3,1},{4,6},{5,7},{6,4},{7,5}} | collective-permute-start | bytes 12582920 | tf_op jit(solution)/shard_map/ppermute | solution.py:553
  371.0 53.0 %collective-permute-start.31 = (bf16[128,32,512]{2,1,0:T(8,128)(2,1)}, bf16[128,32,512]{2,1,0:T(8,128)(2,1)}, u32[]{:S(2)}, u32[]{:S(2)}) collective-permute-start(bf16[128,32,512]{2,1,0:T(8,128)(2,1)} %get-tuple-element.152.refs_18_), channel_id=1, source_target_pairs={{0,1},{1,0},{2,3},{3,2},{4,5},{5,4},{6,7},{7,6}} | collective-permute-start | bytes 12582920 | tf_op jit(solution)/shard_map/ppermute | solution.py:553
  371.0 54.6 %collective-permute-start.35 = (bf16[128,32,512]{2,1,0:T(8,128)(2,1)}, bf16[128,32,512]{2,1,0:T(8,128)(2,1)}, u32[]{:S(2)}, u32[]{:S(2)}) collective-permute-start(bf16[128,32,512]{2,1,0:T(8,128)(2,1)} %get-tuple-element.156.refs_28_), channel_id=1, source_target_pairs={{0,1},{1,0},{2,3},{3,2},{4,5},{5,4},{6,7},{7,6}} | collective-permute-start | bytes 12582920 | tf_op jit(solution)/shard_map/ppermute | solution.py:553
  371.5 90.1 %collective-permute-start.33 = (bf16[128,32,512]{2,1,0:T(8,128)(2,1)}, bf16[128,32,512]{2,1,0:T(8,128)(2,1)}, u32[]{:S(2)}, u32[]{:S(2)}) collective-permute-start(bf16[128,32,512]{2,1,0:T(8,128)(2,1)} %get-tuple-element.154.refs_22_), channel_id=1, source_target_pairs={{0,1},{1,0},{2,3},{3,2},{4,5},{5,4},{6,7},{7,6}} | collective-permute-start | bytes 12582920 | tf_op jit(solution)/shard_map/ppermute | solution.py:553
  371.5 35.1 %copy-start.27 = (bf16[128,16,128]{2,1,0:T(8,128)(2,1)S(1)}, bf16[128,16,128]{2,1,0:T(8,128)(2,1)}, u32[]{:S(2)}) copy-start(bf16[128,16,128]{2,1,0:T(8,128)(2,1)} %get-tuple-element.137) | copy-start | bytes 1572868
  371.6 35.1 %copy-start.26 = (bf16[128,16,128]{2,1,0:T(8,128)(2,1)S(1)}, bf16[128,16,128]{2,1,0:T(8,128)(2,1)}, u32[]{:S(2)}) copy-start(bf16[128,16,128]{2,1,0:T(8,128)(2,1)} %get-tuple-element.145) | copy-start | bytes 1572868
  406.6 15.7 %collective-permute-start.16 = (bf16[128,16,128]{2,1,0:T(8,128)(2,1)S(1)}, bf16[128,16,128]{2,1,0:T(8,128)(2,1)S(1)}, u32[]{:S(2)}, u32[]{:S(2)}) collective-permute-start(bf16[128,16,128]{2,1,0:T(8,128)(2,1)S(1)} %copy-done.27), channel_id=1, source_target_pairs={{0,1},{1,0},{2,3},{3,2},{4,5},{5,4},{6,7},{7,6}} | collective-permute-start | bytes 1572872 | tf_op jit(solution)/shard_map/ppermute | solution.py:553
  406.6 17.4 %collective-permute-start.23 = (bf16[128,16,128]{2,1,0:T(8,128)(2,1)S(1)}, bf16[128,16,128]{2,1,0:T(8,128)(2,1)S(1)}, u32[]{:S(2)}, u32[]{:S(2)}) collective-permute-start(bf16[128,16,128]{2,1,0:T(8,128)(2,1)S(1)} %copy-done.26), channel_id=1, source_target_pairs={{0,1},{1,0},{2,3},{3,2},{4,5},{5,4},{6,7},{7,6}} | collective-permute-start | bytes 1572872 | tf_op jit(solution)/shard_map/ppermute | solution.py:553
  422.3 18.8 %collective-permute-start.17 = (bf16[128,16,128]{2,1,0:T(8,128)(2,1)}, bf16[128,16,128]{2,1,0:T(8,128)(2,1)S(1)}, u32[]{:S(2)}, u32[]{:S(2)}) collective-permute-start(bf16[128,16,128]{2,1,0:T(8,128)(2,1)} %get-tuple-element.138), channel_id=1, source_target_pairs={{0,2},{1,3},{2,0},{3,1},{4,6},{5,7},{6,4},{7,5}} | collective-permute-start | bytes 1572872 | tf_op jit(solution)/shard_map/ppermute | solution.py:553
  424.0 22.9 %collective-permute-start.18 = (bf16[128,16,128]{2,1,0:T(8,128)(2,1)}, bf16[128,16,128]{2,1,0:T(8,128)(2,1)S(1)}, u32[]{:S(2)}, u32[]{:S(2)}) collective-permute-start(bf16[128,16,128]{2,1,0:T(8,128)(2,1)} %get-tuple-element.139), channel_id=1, source_target_pairs={{0,3},{1,2},{2,1},{3,0},{4,7},{5,6},{6,5},{7,4}} | collective-permute-start | bytes 1572872 | tf_op jit(solution)/shard_map/ppermute | solution.py:553
  424.1 23.4 %collective-permute-start.26 = (bf16[128,16,128]{2,1,0:T(8,128)(2,1)S(1)}, bf16[128,16,128]{2,1,0:T(8,128)(2,1)S(1)}, u32[]{:S(2)}, u32[]{:S(2)}) collective-permute-start(bf16[128,16,128]{2,1,0:T(8,128)(2,1)S(1)} %copy-done.29), channel_id=1, source_target_pairs={{0,4},{1,5},{2,6},{3,7},{4,0},{5,1},{6,2},{7,3}} | collective-permute-start | bytes 1572872 | tf_op jit(solution)/shard_map/ppermute | solution.py:553
  425.6 36.4 %collective-permute-start.36 = (bf16[128,32,512]{2,1,0:T(8,128)(2,1)}, bf16[128,32,512]{2,1,0:T(8,128)(2,1)}, u32[]{:S(2)}, u32[]{:S(2)}) collective-permute-start(bf16[128,32,512]{2,1,0:T(8,128)(2,1)} %get-tuple-element.157.refs_30_), channel_id=1, source_target_pairs={{0,1},{1,0},{2,3},{3,2},{4,5},{5,4},{6,7},{7,6}} | collective-permute-start | bytes 12582920 | tf_op jit(solution)/shard_map/ppermute | solution.py:553
  441.2 69.7 %copy-start.3 = (bf16[128,16,128]{2,1,0:T(8,128)(2,1)}, bf16[128,16,128]{2,1,0:T(8,128)(2,1)S(1)}, u32[]{:S(2)}) copy-start(bf16[128,16,128]{2,1,0:T(8,128)(2,1)S(1)} %collective-permute-done.17.refs_2_) | copy-start | bytes 1572868
  441.2 37.4 %collective-permute-start.14 = (bf16[128,32,512]{2,1,0:T(8,128)(2,1)}, bf16[128,32,512]{2,1,0:T(8,128)(2,1)}, u32[]{:S(2)}, u32[]{:S(2)}) collective-permute-start(bf16[128,32,512]{2,1,0:T(8,128)(2,1)} %get-tuple-element.129.b_own0.refs_16_), channel_id=1, source_target_pairs={{0,1},{1,0},{2,3},{3,2},{4,5},{5,4},{6,7},{7,6}} | collective-permute-start | bytes 12582920 | tf_op jit(solution)/shard_map/ppermute | solution.py:553
  447.0 63.9 %copy-start.4 = (bf16[128,16,128]{2,1,0:T(8,128)(2,1)}, bf16[128,16,128]{2,1,0:T(8,128)(2,1)S(1)}, u32[]{:S(2)}) copy-start(bf16[128,16,128]{2,1,0:T(8,128)(2,1)S(1)} %collective-permute-done.18.refs_3_) | copy-start | bytes 1572868
  447.0 32.8 %collective-permute-start.15 = (bf16[128,32,512]{2,1,0:T(8,128)(2,1)}, bf16[128,32,512]{2,1,0:T(8,128)(2,1)}, u32[]{:S(2)}, u32[]{:S(2)}) collective-permute-start(bf16[128,32,512]{2,1,0:T(8,128)(2,1)} %get-tuple-element.130.b_own1.refs_17_), channel_id=1, source_target_pairs={{0,1},{1,0},{2,3},{3,2},{4,5},{5,4},{6,7},{7,6}} | collective-permute-start | bytes 12582920 | tf_op jit(solution)/shard_map/ppermute | solution.py:553
  447.5 63.4 %copy-start.5 = (bf16[128,16,128]{2,1,0:T(8,128)(2,1)}, bf16[128,16,128]{2,1,0:T(8,128)(2,1)S(1)}, u32[]{:S(2)}) copy-start(bf16[128,16,128]{2,1,0:T(8,128)(2,1)S(1)} %collective-permute-done.26.refs_12_) | copy-start | bytes 1572868
  447.5 14.0 %collective-permute-start.27 = (bf16[128,16,128]{2,1,0:T(8,128)(2,1)S(1)}, bf16[128,16,128]{2,1,0:T(8,128)(2,1)S(1)}, u32[]{:S(2)}, u32[]{:S(2)}) collective-permute-start(bf16[128,16,128]{2,1,0:T(8,128)(2,1)S(1)} %copy-done.28), channel_id=1, source_target_pairs={{0,5},{1,4},{2,7},{3,6},{4,1},{5,0},{6,3},{7,2}} | collective-permute-start | bytes 1572872 | tf_op jit(solution)/shard_map/ppermute | solution.py:553
  461.5 49.5 %copy-start.6 = (bf16[128,16,128]{2,1,0:T(8,128)(2,1)}, bf16[128,16,128]{2,1,0:T(8,128)(2,1)S(1)}, u32[]{:S(2)}) copy-start(bf16[128,16,128]{2,1,0:T(8,128)(2,1)S(1)} %collective-permute-done.27.refs_13_) | copy-start | bytes 1572868
  461.5 54.7 %collective-permute-start.32 = (bf16[128,32,512]{2,1,0:T(8,128)(2,1)}, bf16[128,32,512]{2,1,0:T(8,128)(2,1)}, u32[]{:S(2)}, u32[]{:S(2)}) collective-permute-start(bf16[128,32,512]{2,1,0:T(8,128)(2,1)} %get-tuple-element.153.refs_20_), channel_id=1, source_target_pairs={{0,1},{1,0},{2,3},{3,2},{4,5},{5,4},{6,7},{7,6}} | collective-permute-start | bytes 12582920 | tf_op jit(solution)/shard_map/ppermute | solution.py:553
  461.6 82.3 %collective-permute-start.34 = (bf16[128,32,512]{2,1,0:T(8,128)(2,1)}, bf16[128,32,512]{2,1,0:T(8,128)(2,1)}, u32[]{:S(2)}, u32[]{:S(2)}) collective-permute-start(bf16[128,32,512]{2,1,0:T(8,128)(2,1)} %get-tuple-element.155.refs_26_), channel_id=1, source_target_pairs={{0,1},{1,0},{2,3},{3,2},{4,5},{5,4},{6,7},{7,6}} | collective-permute-start | bytes 12582920 | tf_op jit(solution)/shard_map/ppermute | solution.py:553
  462.0 15.1 %collective-permute-start.21 = (bf16[128,16,128]{2,1,0:T(8,128)(2,1)}, bf16[128,16,128]{2,1,0:T(8,128)(2,1)S(1)}, u32[]{:S(2)}, u32[]{:S(2)}) collective-permute-start(bf16[128,16,128]{2,1,0:T(8,128)(2,1)} %get-tuple-element.142), channel_id=1, source_target_pairs={{0,6},{1,7},{2,4},{3,5},{4,2},{5,3},{6,0},{7,1}} | collective-permute-start | bytes 1572872 | tf_op jit(solution)/shard_map/ppermute | solution.py:553
  477.1 33.8 %copy-start.7 = (bf16[128,16,128]{2,1,0:T(8,128)(2,1)}, bf16[128,16,128]{2,1,0:T(8,128)(2,1)S(1)}, u32[]{:S(2)}) copy-start(bf16[128,16,128]{2,1,0:T(8,128)(2,1)S(1)} %collective-permute-done.21.refs_6_) | copy-start | bytes 1572868
  477.1 35.5 %collective-permute-start.22 = (bf16[128,16,128]{2,1,0:T(8,128)(2,1)}, bf16[128,16,128]{2,1,0:T(8,128)(2,1)S(1)}, u32[]{:S(2)}, u32[]{:S(2)}) collective-permute-start(bf16[128,16,128]{2,1,0:T(8,128)(2,1)} %get-tuple-element.143), channel_id=1, source_target_pairs={{0,7},{1,6},{2,5},{3,4},{4,3},{5,2},{6,1},{7,0}} | collective-permute-start | bytes 1572872 | tf_op jit(solution)/shard_map/ppermute | solution.py:553
  478.6 34.5 %collective-permute-start.28 = (bf16[128,16,128]{2,1,0:T(8,128)(2,1)}, bf16[128,16,128]{2,1,0:T(8,128)(2,1)S(1)}, u32[]{:S(2)}, u32[]{:S(2)}) collective-permute-start(bf16[128,16,128]{2,1,0:T(8,128)(2,1)} %get-tuple-element.150), channel_id=1, source_target_pairs={{0,6},{1,7},{2,4},{3,5},{4,2},{5,3},{6,0},{7,1}} | collective-permute-start | bytes 1572872 | tf_op jit(solution)/shard_map/ppermute | solution.py:553
  479.8 34.9 %collective-permute-start.29 = (bf16[128,16,128]{2,1,0:T(8,128)(2,1)}, bf16[128,16,128]{2,1,0:T(8,128)(2,1)}, u32[]{:S(2)}, u32[]{:S(2)}) collective-permute-start(bf16[128,16,128]{2,1,0:T(8,128)(2,1)} %get-tuple-element.151), channel_id=1, source_target_pairs={{0,7},{1,6},{2,5},{3,4},{4,3},{5,2},{6,1},{7,0}} | collective-permute-start | bytes 1572872 | tf_op jit(solution)/shard_map/ppermute | solution.py:553
  482.1 28.9 %copy-start.19 = (f32[128,128]{1,0:T(8,128)S(1)}, f32[128,128]{1,0:T(8,128)}, u32[]{:S(2)}) copy-start(f32[128,128]{1,0:T(8,128)} %get-tuple-element.168) | copy-start | bytes 196612
  482.1 28.9 %copy-start.20 = (f32[128,128]{1,0:T(8,128)S(1)}, f32[128,128]{1,0:T(8,128)}, u32[]{:S(2)}) copy-start(f32[128,128]{1,0:T(8,128)} %get-tuple-element.174) | copy-start | bytes 196612
  512.5 31.4 %copy-start.8 = (bf16[128,16,128]{2,1,0:T(8,128)(2,1)}, bf16[128,16,128]{2,1,0:T(8,128)(2,1)S(1)}, u32[]{:S(2)}) copy-start(bf16[128,16,128]{2,1,0:T(8,128)(2,1)S(1)} %collective-permute-done.22.refs_7_) | copy-start | bytes 1572868
  512.5 31.4 %collective-permute-start.19 = (bf16[128,16,128]{2,1,0:T(8,128)(2,1)}, bf16[128,16,128]{2,1,0:T(8,128)(2,1)S(1)}, u32[]{:S(2)}, u32[]{:S(2)}) collective-permute-start(bf16[128,16,128]{2,1,0:T(8,128)(2,1)} %get-tuple-element.140), channel_id=1, source_target_pairs={{0,4},{1,5},{2,6},{3,7},{4,0},{5,1},{6,2},{7,3}} | collective-permute-start | bytes 1572872 | tf_op jit(solution)/shard_map/ppermute | solution.py:553
  513.1 30.8 %copy-start.9 = (bf16[128,16,128]{2,1,0:T(8,128)(2,1)}, bf16[128,16,128]{2,1,0:T(8,128)(2,1)S(1)}, u32[]{:S(2)}) copy-start(bf16[128,16,128]{2,1,0:T(8,128)(2,1)S(1)} %collective-permute-done.28.refs_14_) | copy-start | bytes 1572868
  513.1 30.9 %collective-permute-start.20 = (bf16[128,16,128]{2,1,0:T(8,128)(2,1)}, bf16[128,16,128]{2,1,0:T(8,128)(2,1)S(1)}, u32[]{:S(2)}, u32[]{:S(2)}) collective-permute-start(bf16[128,16,128]{2,1,0:T(8,128)(2,1)} %get-tuple-element.141), channel_id=1, source_target_pairs={{0,5},{1,4},{2,7},{3,6},{4,1},{5,0},{6,3},{7,2}} | collective-permute-start | bytes 1572872 | tf_op jit(solution)/shard_map/ppermute | solution.py:553
  514.7 29.3 %collective-permute-start.24 = (bf16[128,16,128]{2,1,0:T(8,128)(2,1)}, bf16[128,16,128]{2,1,0:T(8,128)(2,1)S(1)}, u32[]{:S(2)}, u32[]{:S(2)}) collective-permute-start(bf16[128,16,128]{2,1,0:T(8,128)(2,1)} %get-tuple-element.146), channel_id=1, source_target_pairs={{0,2},{1,3},{2,0},{3,1},{4,6},{5,7},{6,4},{7,5}} | collective-permute-start | bytes 1572872 | tf_op jit(solution)/shard_map/ppermute | solution.py:553
  516.2 27.8 %collective-permute-start.25 = (bf16[128,16,128]{2,1,0:T(8,128)(2,1)}, bf16[128,16,128]{2,1,0:T(8,128)(2,1)S(1)}, u32[]{:S(2)}, u32[]{:S(2)}) collective-permute-start(bf16[128,16,128]{2,1,0:T(8,128)(2,1)} %get-tuple-element.147), channel_id=1, source_target_pairs={{0,3},{1,2},{2,1},{3,0},{4,7},{5,6},{6,5},{7,4}} | collective-permute-start | bytes 1572872 | tf_op jit(solution)/shard_map/ppermute | solution.py:553
  (23 other events, 315.8 us)

commit v3 on v2

--- a/solution.py
+++ b/solution.py
@@ -206,10 +206,11 @@
     )(ids, z_loc, dy_loc, m_loc, w_t, scale, offset, w_out)
 
 
-CB = 16
-CP = 32
+CB = 32
+CR = 32
+CP = 64
 FIRST = C // CB
-LAST = FIRST + NR // NB
+LAST = FIRST + NR // CR
 
 
 def out_kernel(ids_ref, a_ref, b_own0, b_own1, b_par0, b_par1, don_ref, dup_ref, g1_ref, w_out_ref, scale_ref, offset_ref,
@@ -232,12 +233,12 @@
             o_scr[0, pl.ds((step * CB + ch) * SO, NR), :] = jnp.where(first_core, val, pltpu.roll(val, 64, 1))
             return carry
 
-        lax.fori_loop(0, CB, prod, 0, unroll=8)
+        lax.fori_loop(0, CB, prod, 0, unroll=16)
 
     @pl.when((step >= FIRST) & (step < LAST))
     def _():
         def chain(row, carry):
-            o_row = (step - FIRST) * NB + row
+            o_row = (step - FIRST) * CR + row
             o_hat, inv_std = norm_rows(get_row(o_scr, o_row, SO, (0,)))
             o_norm = (o_hat * scale_ref[...] + offset_ref[...]).astype(BF16)
             aug = jnp.concatenate([o_norm, ones_rows(C)], axis=0)
@@ -254,7 +255,7 @@
             dwout_ref[...] += nt_dot(o_norm, dup_ref[row])
             return carry
 
-        lax.fori_loop(0, NB, chain, 0, unroll=8)
+        lax.fori_loop(0, CR, chain, 0, unroll=8)
 
     @pl.when(step >= LAST)
     def _():
@@ -279,7 +280,7 @@
             cross1[ch] = jnp.where(first_core, g3, g1).astype(BF16)
             return carry
 
-        lax.fori_loop(0, CP, pack, 0, unroll=4)
+        lax.fori_loop(0, CP, pack, 0, unroll=8)
 
 
 def piece_spec(width, blk):
@@ -291,7 +292,7 @@
 
 
 def chain_step(step):
-    return jnp.clip(step - FIRST, 0, NR // NB - 1)
+    return jnp.clip(step - FIRST, 0, NR // CR - 1)
 
 
 def pack_step(step):
@@ -299,7 +300,7 @@
 
 
 def out_call(chunk, ids, a_own, b_pieces, don, dup, g1, w_out_t, scale, offset):
-    lane_spec = pl.BlockSpec((NB, C, C), lambda s, ids: (chain_step(s), 0, chunk))
+    lane_spec = pl.BlockSpec((CR, C, C), lambda s, ids: (chain_step(s), 0, chunk))
     acc_spec = full_spec((C, C))
     pack_spec = pl.BlockSpec((CP, NB, C), lambda s, ids: (pack_step(s), 0, 0))
     b_specs = [pl.BlockSpec((CB, HALF, N), lambda s, ids, blk=blk: (prod_step(s), blk, 0)) for _, blk in b_pieces]
@@ -311,7 +312,7 @@
             in_specs=[pl.BlockSpec((CB, NR, N), lambda s, ids: (prod_step(s), 0, 0))] + b_specs
             + [lane_spec, lane_spec, lane_spec, full_spec((C, C + 16)), acc_spec, acc_spec],
             out_specs=[pl.BlockSpec((CP, NR, C), lambda s, ids: (pack_step(s), 0, 0)),
-                       pl.BlockSpec((NB, C, C), lambda s, ids: (chain_step(s), 0, 0))] + [pack_spec] * 4 + [acc_spec] * 3 + [TOKEN_SPEC],
+                       pl.BlockSpec((CR, C, C), lambda s, ids: (chain_step(s), 0, 0))] + [pack_spec] * 4 + [acc_spec] * 3 + [TOKEN_SPEC],
             scratch_shapes=[pltpu.VMEM((1, C * SO, C), F32)],
         ),
         out_shape=[sds((C, NR, C), BF16), sds((NR, C, C), BF16)] + [sds((C, NB, C), BF16)] * 4 + [sds((C, C), F32)] * 3 + [TOKEN],
@@ -324,25 +325,29 @@
 CK = 16
 
 
-def da_kernel(*refs):
-    do_refs, b_refs, da_ref = refs[:4], refs[4:20], refs[20]
+def da_kernel(count, *refs):
+    do_refs, b_refs, da_ref = refs[:count], refs[count:5 * count], refs[-1]
     for ch in range(CK):
         do_row = jnp.concatenate([ref[ch] for ref in do_refs], axis=1)
         b_rows = jnp.concatenate([ref[ch] for ref in b_refs], axis=0)
-        da_ref[ch] = nn_dot(do_row, b_rows).astype(BF16)
-
-
-def da_call(do_chunks, b_pieces):
+        val = nn_dot(do_row, b_rows)
+        for ref in refs[5 * count:-1]:
+            val += ref[ch]
+        da_ref[ch] = val.astype(da_ref.dtype)
+
+
+def da_call(do_chunks, b_pieces, partial, dtype):
+    row_spec = pl.BlockSpec((CK, NR, N), lambda s: (s, 0, 0))
     return pl.pallas_call(
-        da_kernel,
+        functools.partial(da_kernel, len(do_chunks)),
         grid=(C // CK,),
-        in_specs=[pl.BlockSpec((CK, NR, 128), lambda s: (s, 0, 0))] * 4 + [piece_spec(CK, blk) for _, blk in b_pieces],
-        out_specs=pl.BlockSpec((CK, NR, N), lambda s: (s, 0, 0)),
-        out_shape=sds((C, NR, N), BF16),
+        in_specs=[pl.BlockSpec((CK, NR, C), lambda s: (s, 0, 0))] * len(do_chunks) + [piece_spec(CK, blk) for _, blk in b_pieces] + [row_spec] * len(partial),
+        out_specs=row_spec,
+        out_shape=sds((C, NR, N), dtype),
         compiler_params=PARAMS,
         cost_estimate=COST,
         name="grad_a",
-    )(*do_chunks, *(arr for arr, _ in b_pieces))
+    )(*do_chunks, *(arr for arr, _ in b_pieces), *partial)
 
 
 def db_kernel(*refs):
@@ -406,10 +411,10 @@
         mask_f = m_scr[pl.ds(first + row, 1), :]
         parts = []
         for side, scr in ((0, a_scr), (1, b_scr)):
-            proj = nn_dot(w_ref[2 * C * side:2 * C * side + C], aug)
-            sig = sigmoid(nn_dot(w_ref[2 * C * side + C:2 * C * (side + 1)], aug))
+            proj = nn_dot(w_ref[2 * C * side:2 * C * (side + 1)], aug)
+            sig = sigmoid(proj[C:])
             d_proj = get_row(scr, row, SB, range(4)) * mask_f * sig
-            d_lin = d_proj * proj * (1.0 - sig)
+            d_lin = d_proj * proj[:C] * (1.0 - sig)
             dbin_ref[side] += lanes4(d_proj)
             dbin_ref[2 + side] += lanes4(d_lin)
             parts.append((d_proj.astype(BF16), d_lin.astype(BF16)))
@@ -454,11 +459,12 @@
 
 SHARD = 112
 VECS = 6 * C
+VEC_ROWS = (0, 1, 6, 7, 8, 9)
 
 
 def sum_kernel(*refs):
-    accs, wout_refs, w_ref = refs[:7], refs[7:11], refs[11]
-    win_ref, wgate_ref, wout_ref, vec_ref, src, recv, mine, total, send1, recv1, send2, recv2 = refs[12:]
+    accs, wout_refs, osc_refs, bg_refs, w_ref = refs[:7], refs[7:11], refs[11:14], refs[14:17], refs[17]
+    total, src, recv, mine, send1, recv1, send2, recv2 = refs[18:]
     me = lax.axis_index('dap')
 
     def peer(step):
@@ -471,8 +477,8 @@
         src[C * blk:C * (blk + 1)] = w_ref[C * blk:C * (blk + 1)].T
     src[5 * C:VECS] = sum(ref[...] for ref in wout_refs[1:]) + wout_refs[0][...]
     rows = []
-    for ref in accs:
-        rows += [ref[n] for n in range(4)] if len(ref.shape) > 2 else [ref[...]]
+    for ref, more in zip(accs, ((), (), (), osc_refs, (), (), bg_refs)):
+        rows += [ref[n] for n in range(4)] if len(ref.shape) > 2 else [sum((other[...] for other in more), ref[...])]
     rows = [jnp.sum(val.T, axis=0, keepdims=True) for val in rows]
     src[VECS:] = jnp.concatenate(rows + [jnp.zeros((8 * SHARD - VECS - len(rows), C), F32)], axis=0)
     pl.semaphore_wait(barrier, 7)
@@ -502,27 +508,45 @@
         copies.append(copy)
     for copy in copies:
         copy.wait()
+
+
+def split_kernel(total, win_ref, wgate_ref, wout_ref, bin_ref, *vec_refs):
     for blk in range(4):
         win_ref[:, C * blk:C * (blk + 1)] = total[C * blk:C * (blk + 1)]
     wgate_ref[...] = total[4 * C:5 * C]
     wout_ref[...] = total[5 * C:VECS]
-    vec_ref[...] = total[VECS:VECS + 16]
+    vecs = total[VECS:VECS + 16]
+    bin_ref[...] = vecs[2:6].reshape(4 * C)
+    for ref, n in zip(vec_refs, VEC_ROWS):
+        ref[...] = vecs[n:n + 1]
+
+
+def vmem_specs(count):
+    return [pl.BlockSpec(memory_space=pltpu.VMEM)] * count
 
 
 def sum_call(accs, wouts, acc_w):
     args = [*accs, *wouts, acc_w]
-    outs = [sds((C, 4 * C), BF16), sds((C, C), BF16), sds((C, C), BF16), sds((16, C), BF16)]
-    return pl.pallas_call(
+    total = pl.pallas_call(
         sum_kernel,
-        in_specs=[pl.BlockSpec(memory_space=pltpu.VMEM)] * len(args),
-        out_specs=[pl.BlockSpec(memory_space=pltpu.VMEM)] * len(outs),
-        out_shape=outs,
-        scratch_shapes=[pltpu.VMEM((8 * SHARD, C), F32), pltpu.VMEM((8, SHARD, C), F32), pltpu.VMEM((SHARD, C), BF16), pltpu.VMEM((8 * SHARD, C), BF16)]
+        in_specs=vmem_specs(len(args)),
+        out_specs=vmem_specs(1)[0],
+        out_shape=sds((8 * SHARD, C), BF16),
+        scratch_shapes=[pltpu.VMEM((8 * SHARD, C), F32), pltpu.VMEM((8, SHARD, C), F32), pltpu.VMEM((SHARD, C), BF16)]
         + [pltpu.SemaphoreType.DMA((8,))] * 4,
         compiler_params=pltpu.CompilerParams(collective_id=0, has_side_effects=True),
         cost_estimate=COST,
         name="sum_grads",
     )(*args)
+    outs = [sds((C, width), BF16) for width in (4 * C, C, C)] + [sds((4 * C,), BF16)] + [sds((1, C), BF16)] * len(VEC_ROWS)
+    return pl.pallas_call(
+        split_kernel,
+        in_specs=vmem_specs(1),
+        out_specs=vmem_specs(len(outs)),
+        out_shape=outs,
+        cost_estimate=COST,
+        name="split_grads",
+    )(total)
 
 
 def aug_weight(w_mat, bias):
@@ -563,7 +587,7 @@
     b_par, a_par = move(b_own, 1), move(a_own, 1)
     a_at = {(0, h, f): (val, h) for h in range(2) for f, val in ((0, a_own), (1, a_par))}
     b_at = {(0, h, f): (val, h) for h in range(2) for f, val in ((0, b_own), (1, b_par))}
-    do_at, do_chunks, dg_chunks, sums = {}, [], [], []
+    do_at, do_chunks, chunk_b, d_a, dg_chunks, sums = {}, [], [], [], [], []
     for q in range(4):
         for h in range(2):
             if q:
@@ -576,20 +600,23 @@
         do_chunks.append(do_own)
         dg_chunks.append(dg)
         sums.append(acc)
+        chunk_b += b_pieces
+        if q:
+            d_a = da_call(do_chunks, chunk_b, d_a, BF16 if q == 3 else F32)
+            do_chunks, chunk_b, d_a = [], [], [d_a]
         for flip, h, val in ((0, 0, same0), (0, 1, same1), (1, 0, cross0), (1, 1, cross1)):
             flips = HOPS[q][h] ^ flip
             do_at[h, flips] = move(val, flips) if flips else val
-    d_a = da_call(do_chunks, [b_at[q, h, f] for q in range(4) for f in range(2) for h in range(2)])
     chunk_of = {(HOPS[q][h], h): q for q in range(4) for h in range(2)}
     d_b = db_call([do_at[h, s] for h in range(2) for s in range(8)],
                   [a_at[chunk_of[s & 6, h], h, s & 1] for h in range(2) for s in range(8)])
-    d_z, acc_w, acc_bin, acc_isc, acc_ioff = in_call(ids, z_loc, dy_loc, mask_t, d_a, d_b, dg_chunks, w_t[:4 * C], *wide_in, w_cat)
+    d_z, acc_w, acc_bin, acc_isc, acc_ioff = in_call(ids, z_loc, dy_loc, mask_t, d_a[0], d_b, dg_chunks, w_t[:4 * C], *wide_in, w_cat)
 
     wouts, oscs, bgs = zip(*sums)
-    accs = (acc_isc, acc_ioff, acc_bin, sum(oscs), acc_ooff, acc_bout, sum(bgs))
-    d_win, d_wgate, d_wout, vecs = sum_call(accs, wouts, acc_w)
-    d_isc, d_ioff, d_osc, d_ooff, d_bout, d_bg = (vecs[n] for n in (0, 1, 6, 7, 8, 9))
-    return d_z, d_isc, d_ioff, d_win, vecs[2:6].reshape(4 * C), d_osc, d_ooff, d_wout, d_bout, d_wgate, d_bg
+    accs = (acc_isc, acc_ioff, acc_bin, oscs[0], acc_ooff, acc_bout, bgs[0])
+    d_win, d_wgate, d_wout, *vecs = sum_call(accs, wouts + oscs[1:] + bgs[1:], acc_w)
+    d_bin, d_isc, d_ioff, d_osc, d_ooff, d_bout, d_bg = (vec.reshape(vec.size) for vec in vecs)
+    return d_z, d_isc, d_ioff, d_win, d_bin, d_osc, d_ooff, d_wout, d_bout, d_wgate, d_bg
 
 
 def solution(mesh):

time: 653 us -> 667 us (1.021)
  waiting for transfers between devices: 216 us -> 231 us
  Pallas kernels: 370 us -> 380 us
  local copies, waits for them, and re-layouts: 27.9 us -> 20.5 us
    pallas_call x2 -> x5, Pallas kernels: 43.5 us -> 71.8 us  [the longest x3 55.2 us: da_call(): pl.pallas_call(functools.partial(da_kernel, len(do_chunks)), grid=(C // C...]
    pallas_call x4, Pallas kernels: 114 us -> 98.1 us  [out_call(): pl.pallas_call(out_kernel, grid_spec=pltpu.PrefetchScalarGridSpec(num_sca...]
    ppermute x37, waiting for transfers between devices: 216 us -> 231 us  [move(): return lax.ppermute(val, 'dap', [(d, d ^ flips) for d in range(8)])]
  transfers between devices with their start and end apart: 37 -> 37, of which waited for: 10 -> 12; matrix products, arithmetic and copies ran while one was open for 2% -> 1% of each run, Pallas kernels for 36% -> 34%
where the time goes in v3:
time: 667 us
  Pallas kernels  380 us (57%)
  waiting for transfers between devices  231 us (35%)
  starting transfers between devices  29.6 us (4%)
  local copies, waits for them, and re-layouts  20.5 us (3%)
    ppermute x37, waiting for transfers between devices, move(): return lax.ppermute(val, 'dap', [(d, d ^ flips) for d in range(8)])  231 us
    pallas_call x4, Pallas kernels, out_call(): pl.pallas_call(out_kernel, grid_spec=pltpu.PrefetchScalarGridSpec(num_sca...  98.1 us
    pallas_call x6, Pallas kernels, gated_call(): pl.pallas_call(functools.partial(gated_kernel, half_id), grid_spec=pltpu....  90.6 us
    pallas_call x3, Pallas kernels, da_call(): pl.pallas_call(functools.partial(da_kernel, len(do_chunks)), grid=(C // C...  55.2 us
    pallas_call x1, Pallas kernels, in_call(): pl.pallas_call(in_kernel, grid_spec=pltpu.PrefetchScalarGridSpec(num_scal...  52.9 us
    pallas_call x1, Pallas kernels, own_call(): pl.pallas_call(own_kernel, grid_spec=pltpu.PrefetchScalarGridSpec(num_sca...  38.6 us
    ppermute x37, starting transfers between devices, move(): return lax.ppermute(val, 'dap', [(d, d ^ flips) for d in range(8)])  29.6 us
    pallas_call x1, Pallas kernels, db_call(): pl.pallas_call(db_kernel, grid=(C // CK,), in_specs=[pl.BlockSpec((CK, NB...  27.8 us
  transfers between devices with their start and end apart: 37, of which 12 were waited for; matrix products, arithmetic and copies ran while one was open for 1% of the time, Pallas kernels for 34%

profile of v3, /device:TPU:0, one launch (start us, length us, event | category | flops | bytes accessed | tf_op | source)
XLA Modules:
  0.0 666.6 jit_solution(1573849427189480962)
XLA Ops:
  2.0 0.9 convert_element_type.22
  3.7 0.9 constant_dynamic-update-slice_fusion.1
  6.7 0.9 copy.36.w_ref
  8.3 1.4 broadcast_in_dim.18.scale_ref
  9.6 1.4 broadcast_in_dim.19.offset_ref
  11.0 38.6 %own_rows.1 = (bf16[128,64,512]{2,1,0:T(8,128)(2,1)}, bf16[128,64,512]{2,1,0:T(8,128)(2,1)}, bf16[64,128,512]{2,1,0:T(8,128)(2,1)}, bf16[64,128,512]{2,1,0:T(8,1...) custom-call(s32[17]{0:T(128)} %stack.71.ids_ref, ...), custom_call_target="tpu_custom_call" | custom-call | flops 8589934592 | bytes 67108864 | tf_op jit(solution)/shard_map/own_rows/pallas_call | solution.py:192
  50.5 6.0 fusion.23
  56.6 2.5 collective-permute-start.1
  59.1 1.5 collective-permute-start.3
  65.1 23.9 %out_chain.4 = (bf16[128,64,128]{2,1,0:T(8,128)(2,1)}, bf16[64,128,128]{2,1,0:T(8,128)(2,1)}, bf16[128,16,128]{2,1,0:T(8,128)(2,1)}, bf16[128,16,128]{2,1,0:T(8,...) custom-call(s32[17]{0:T(128)} %get-tuple-element.116.ids_ref, ...), custom_call_target="tpu_custom_call" | custom-call | flops 8589934592 | bytes 67108864 | tf_op jit(solution)/shard_map/out_chain/pallas_call | solution.py:307
  88.9 64.4 %collective-permute-done.2.m_ref = bf16[1,512,128]{2,1,0:T(8,128)(2,1)S(1)} collective-permute-done((bf16[1,512,128]{2,1,0:T(8,128)(2,1)S(1)}, bf16[1,512,128]{2,1,0:T(8,128)(2,1)S(1)}, u32[]{:S(2)}, u32[]{:S(2)}) %collective-permute-start.2) | collective-permute-done | bytes 131104 | tf_op jit(solution)/shard_map/ppermute | solution.py:577
  154.0 15.2 %gated_rows.6 = (bf16[128,32,512]{2,1,0:T(8,128)(2,1)}, bf16[128,32,512]{2,1,0:T(8,128)(2,1)}, s32[17]{0:T(128)}) custom-call(s32[17]{0:T(128)} %get-tuple-element.122.ids_ref, bf16[32,512,128]{2,1,0:T(8,128)(2,1)} %collective-permute-done.1.z_ref, bf16[1,512,128]{2,1,0:T(8,128)(2,1)} %copy-done.29, bf16[512,144]{1,0:T(8,128)(2,1)} %copy.39.w_ref, ...), custom_call_target="tpu_custom_call" | custom-call | flops 8589934592 | bytes 67108864 | tf_op jit(solution)/shard_map/gated_rows/pallas_call | solution.py:131
  169.8 15.1 %gated_rows.7 = (bf16[128,32,512]{2,1,0:T(8,128)(2,1)}, bf16[128,32,512]{2,1,0:T(8,128)(2,1)}, s32[17]{0:T(128)}) custom-call(s32[17]{0:T(128)} %get-tuple-element.123.ids_ref, bf16[32,512,128]{2,1,0:T(8,128)(2,1)} %collective-permute-done.3.z_ref, bf16[1,512,128]{2,1,0:T(8,128)(2,1)} %copy-done.30, bf16[512,144]{1,0:T(8,128)(2,1)} %copy.39.w_ref, ...), custom_call_target="tpu_custom_call" | custom-call | flops 8589934592 | bytes 67108864 | tf_op jit(solution)/shard_map/gated_rows/pallas_call | solution.py:131
  185.4 1.8 collective-permute-start.7
  187.1 1.5 collective-permute-start.9
  188.9 3.5 collective-permute-done.6.b_par1.refs_9_
  192.4 1.7 collective-permute-start.13
  194.1 4.3 collective-permute-done.5.b_par0.refs_8_
  198.5 24.7 %out_chain.5 = (bf16[128,64,128]{2,1,0:T(8,128)(2,1)}, bf16[64,128,128]{2,1,0:T(8,128)(2,1)}, bf16[128,16,128]{2,1,0:T(8,128)(2,1)}, bf16[128,16,128]{2,1,0:T(8,...) custom-call(s32[17]{0:T(128)} %get-tuple-element.124.ids_ref, ...), custom_call_target="tpu_custom_call" | custom-call | flops 8589934592 | bytes 67108864 | tf_op jit(solution)/shard_map/out_chain/pallas_call | solution.py:307
  223.2 60.1 %collective-permute-done.8.m_ref = bf16[1,512,128]{2,1,0:T(8,128)(2,1)S(1)} collective-permute-done((bf16[1,512,128]{2,1,0:T(8,128)(2,1)S(1)}, bf16[1,512,128]{2,1,0:T(8,128)(2,1)S(1)}, u32[]{:S(2)}, u32[]{:S(2)}) %collective-permute-start.8) | collective-permute-done | bytes 131104 | tf_op jit(solution)/shard_map/ppermute | solution.py:577
  283.9 15.0 %gated_rows.8 = (bf16[128,32,512]{2,1,0:T(8,128)(2,1)}, bf16[128,32,512]{2,1,0:T(8,128)(2,1)}, s32[17]{0:T(128)}) custom-call(s32[17]{0:T(128)} %get-tuple-element.127.ids_ref, bf16[32,512,128]{2,1,0:T(8,128)(2,1)} %collective-permute-done.7.z_ref, bf16[1,512,128]{2,1,0:T(8,128)(2,1)} %copy-done.31, bf16[512,144]{1,0:T(8,128)(2,1)} %copy.39.w_ref, ...), custom_call_target="tpu_custom_call" | custom-call | flops 8589934592 | bytes 67108864 | tf_op jit(solution)/shard_map/gated_rows/pallas_call | solution.py:131
  299.0 15.0 %gated_rows.9 = (bf16[128,32,512]{2,1,0:T(8,128)(2,1)}, bf16[128,32,512]{2,1,0:T(8,128)(2,1)}, s32[17]{0:T(128)}) custom-call(s32[17]{0:T(128)} %get-tuple-element.128.ids_ref, bf16[32,512,128]{2,1,0:T(8,128)(2,1)} %collective-permute-done.9.z_ref, bf16[1,512,128]{2,1,0:T(8,128)(2,1)} %copy-done.31, bf16[512,144]{1,0:T(8,128)(2,1)} %copy.39.w_ref, ...), custom_call_target="tpu_custom_call" | custom-call | flops 8589934592 | bytes 67108864 | tf_op jit(solution)/shard_map/gated_rows/pallas_call | solution.py:131
  314.5 1.8 collective-permute-start.12
  316.3 56.1 %collective-permute-done.13.z_ref = bf16[32,512,128]{2,1,0:T(8,128)(2,1)} collective-permute-done((bf16[32,512,128]{2,1,0:T(8,128)(2,1)}, bf16[32,512,128]{2,1,0:T(8,128)(2,1)}, u32[]{:S(2)}, u32[]{:S(2)}) %collective-permute-start.13) | collective-permute-done | bytes 4194336 | tf_op jit(solution)/shard_map/ppermute | solution.py:577
  372.9 25.0 %out_chain.6 = (bf16[128,64,128]{2,1,0:T(8,128)(2,1)}, bf16[64,128,128]{2,1,0:T(8,128)(2,1)}, bf16[128,16,128]{2,1,0:T(8,128)(2,1)}, bf16[128,16,128]{2,1,0:T(8,...) custom-call(s32[17]{0:T(128)} %get-tuple-element.129.ids_ref, ...), custom_call_target="tpu_custom_call" | custom-call | flops 8589934592 | bytes 67108864 | tf_op jit(solution)/shard_map/out_chain/pallas_call | solution.py:307
  397.9 9.4 %collective-permute-done.12.z_ref = bf16[32,512,128]{2,1,0:T(8,128)(2,1)} collective-permute-done((bf16[32,512,128]{2,1,0:T(8,128)(2,1)}, bf16[32,512,128]{2,1,0:T(8,128)(2,1)}, u32[]{:S(2)}, u32[]{:S(2)}) %collective-permute-start.12) | collective-permute-done | bytes 4194336 | tf_op jit(solution)/shard_map/ppermute | solution.py:577
  407.9 15.2 %gated_rows.10 = (bf16[128,32,512]{2,1,0:T(8,128)(2,1)}, bf16[128,32,512]{2,1,0:T(8,128)(2,1)}, s32[17]{0:T(128)}) custom-call(s32[17]{0:T(128)} %get-tuple-element.132.ids_ref, bf16[32,512,128]{2,1,0:T(8,128)(2,1)} %collective-permute-done.12.z_ref, bf16[1,512,128]{2,1,0:T(8,128)(2,1)} %copy-done.30, bf16[512,144]{1,0:T(8,128)(2,1)} %copy.39.w_ref, ...), custom_call_target="tpu_custom_call" | custom-call | flops 8589934592 | bytes 67108864 | tf_op jit(solution)/shard_map/gated_rows/pallas_call | solution.py:131
  423.1 1.7 collective-permute-start.17
  425.2 1.7 collective-permute-start.26
  427.0 15.2 %gated_rows.11 = (bf16[128,32,512]{2,1,0:T(8,128)(2,1)}, bf16[128,32,512]{2,1,0:T(8,128)(2,1)}, s32[17]{0:T(128)}) custom-call(s32[17]{0:T(128)} %get-tuple-element.133.ids_ref, bf16[32,512,128]{2,1,0:T(8,128)(2,1)} %collective-permute-done.13.z_ref, bf16[1,512,128]{2,1,0:T(8,128)(2,1)} %copy-done.29, bf16[512,144]{1,0:T(8,128)(2,1)} %copy.39.w_ref, ...), custom_call_target="tpu_custom_call" | custom-call | flops 8589934592 | bytes 67108864 | tf_op jit(solution)/shard_map/gated_rows/pallas_call | solution.py:131
  442.2 5.5 collective-permute-done.18.refs_3_
  448.2 1.4 collective-permute-start.27
  449.6 12.6 %collective-permute-done.27.refs_13_ = bf16[128,16,128]{2,1,0:T(8,128)(2,1)S(1)} collective-permute-done((bf16[128,16,128]{2,1,0:T(8,128)(2,1)S(1)}, bf16[128,16,128]{2,1,0:T(8,128)(2,1)S(1)}, u32[]{:S(2)}, u32[]{:S(2)}) %collective-permute-start.27) | collective-permute-done | bytes 524320 | tf_op jit(solution)/shard_map/ppermute | solution.py:577
  462.7 20.2 %grad_a.3.refs_5_ = f32[128,64,512]{2,1,0:T(8,128)} custom-call(bf16[128,64,128]{2,1,0:T(8,128)(2,1)} %get-tuple-element.140.refs_0_, bf16[128,64,128]{2,1,0:T(8,128)(2,1)} %get-tuple-element.141.refs_1_, bf16[128,64,512]{2,1,0:T(8,128)(2,1)} %get-tuple-element.118.b_own0.b_own1.refs_2_.refs_3_, ...), custom_call_target="tpu_custom_call" | custom-call | flops 8589934592 | bytes 67108864 | tf_op jit(solution)/shard_map/grad_a/pallas_call | solution.py:341
  482.9 2.8 collective-permute-start.21
  485.7 18.9 %grad_a.4.refs_5_ = f32[128,64,512]{2,1,0:T(8,128)} custom-call(bf16[128,64,128]{2,1,0:T(8,128)(2,1)} %get-tuple-element.139.refs_0_, bf16[128,32,512]{2,1,0:T(8,128)(2,1)} %get-tuple-element.130.b_own0.refs_1_, bf16[128,32,512]{2,1,0:T(8,128)(2,1)} %get-tuple-element.131.b_own1.refs_2_, bf16[128,32,512]{2,1,0:T(8,128)(2,1)} %collective-permute-done.10.b_par0.refs_3_, ...), custom_call_target="tpu_custom_call" | custom-call | flops 8589934592 | bytes 67108864 | tf_op jit(solution)/shard_map/grad_a/pallas_call | solution.py:341
  504.7 2.3 collective-permute-start.28
  507.3 24.5 %out_chain.7 = (bf16[128,64,128]{2,1,0:T(8,128)(2,1)}, bf16[64,128,128]{2,1,0:T(8,128)(2,1)}, bf16[128,16,128]{2,1,0:T(8,128)(2,1)}, bf16[128,16,128]{2,1,0:T(8,...) custom-call(s32[17]{0:T(128)} %get-tuple-element.134.ids_ref, ...), custom_call_target="tpu_custom_call" | custom-call | flops 8589934592 | bytes 67108864 | tf_op jit(solution)/shard_map/out_chain/pallas_call | solution.py:307
  531.9 1.7 collective-permute-start.19
  533.7 8.6 %collective-permute-done.29.refs_15_ = bf16[128,16,128]{2,1,0:T(8,128)(2,1)S(1)} collective-permute-done((bf16[128,16,128]{2,1,0:T(8,128)(2,1)S(1)}, bf16[128,16,128]{2,1,0:T(8,128)(2,1)S(1)}, u32[]{:S(2)}, u32[]{:S(2)}) %collective-permute-start.29) | collective-permute-done | bytes 524320 | tf_op jit(solution)/shard_map/ppermute | solution.py:577
  542.8 0.9 collective-permute-start.25
  543.7 16.1 %grad_a.5.da_ref = bf16[128,64,512]{2,1,0:T(8,128)(2,1)} custom-call(bf16[128,64,128]{2,1,0:T(8,128)(2,1)} %get-tuple-element.138.refs_0_, bf16[128,32,512]{2,1,0:T(8,128)(2,1)} %get-tuple-element.135.b_own0.refs_1_, bf16[128,32,512]{2,1,0:T(8,128)(2,1)} %get-tuple-element.136.b_own1.refs_2_, bf16[128,32,512]{2,1,0:T(8,128)(2,1)} %collective-permute-done.14.b_par0.refs_3_, ...), custom_call_target="tpu_custom_call" | custom-call | flops 8589934592 | bytes 67108864 | tf_op jit(solution)/shard_map/grad_a/pallas_call | solution.py:341
  559.9 4.7 collective-permute-done.20.refs_5_
  564.6 2.1 collective-permute-done.25.refs_11_
  567.5 27.8 %grad_b.1.db_ref = bf16[128,64,512]{2,1,0:T(8,128)(2,1)} custom-call(bf16[128,16,128]{2,1,0:T(8,128)(2,1)} %get-tuple-element.142.refs_0_, bf16[128,16,128]{2,1,0:T(8,128)(2,1)} %copy-done.1, bf16[128,16,128]{2,1,0:T(8,128)(2,1)} %copy-done.3, bf16[128,16,128]{2,1,0:T(8,128)(2,1)} %copy-done.4, bf16[128,16,128]{2,1,0:T(8,128)(2,1)} %copy-done.11, ...), custom_call_target="tpu_custom_call" | custom-call | flops 8589934592 | bytes 67108864 | tf_op jit(solution)/shard_map/grad_b/pallas_call | solution.py:368
  596.9 52.9 %in_backward.1 = (bf16[64,512,128]{2,1,0:T(8,128)(2,1)}, f32[640,128]{1,0:T(8,128)}, f32[4,128,128]{2,1,0:T(8,128)}, f32[128,128]{1,0:T(8,128)}, f32[128,128]{1,0:T(8,128)}) custom-call(s32[17]{0:T(128)} %get-tuple-element.137.ids_ref, bf16[64,512,128]{2,1,0:T(8,128)(2,1)} %z_ref.3, bf16[64,512,128]{2,1,0:T(8,128)(2,1)} %dy_ref.3, ...), custom_call_target="tpu_custom_call" | custom-call | flops 8589934592 | bytes 67108864 | tf_op jit(solution)/shard_map/in_backward/pallas_call | solution.py:442
  649.9 14.9 %sum_grads.1.total = bf16[896,128]{1,0:T(8,128)(2,1)} custom-call(f32[128,128]{1,0:T(8,128)} %get-tuple-element.169.refs_0_, f32[128,128]{1,0:T(8,128)} %get-tuple-element.170.refs_1_, f32[4,128,128]{2,1,0:T(8,128)} %get-tuple-element.171.refs_2_, f32[128,128]{1,0:T(8,128)} %get-tuple-element.172.refs_3_, f32[128,128]{1,0:T(8,128)} %get-tuple-element.173.refs_4_, ...), custom_call_target="tpu_custom_call" | custom-call | flops 8589934592 | bytes 67108864 | tf_op jit(solution)/shard_map/sum_grads/pallas_call | solution.py:530
  664.8 1.7 split_grads.1
  (137 shorter events, 19.5 us)
Async XLA Ops:
  49.7 14.0 %collective-permute-start = (bf16[128,64,512]{2,1,0:T(8,128)(2,1)}, bf16[128,64,512]{2,1,0:T(8,128)(2,1)}, u32[]{:S(2)}, u32[]{:S(2)}) collective-permute-start(bf16[128,64,512]{2,1,0:T(8,128)(2,1)} %get-tuple-element.118.b_own0.b_own1.refs_2_.refs_3_), channel_id=1, source_target_pairs={{0,1},{1,0},{2,3},{3,2},{4,5},{5,4},{6,7},{7,6}} | collective-permute-start | bytes 25165832 | tf_op jit(solution)/shard_map/ppermute | solution.py:577
  56.6 96.7 %collective-permute-start.1 = (bf16[32,512,128]{2,1,0:T(8,128)(2,1)}, bf16[32,512,128]{2,1,0:T(8,128)(2,1)}, u32[]{:S(2)}, u32[]{:S(2)}) collective-permute-start(bf16[32,512,128]{2,1,0:T(8,128)(2,1)} %get-tuple-element.198), channel_id=1, source_target_pairs={{0,2},{1,3},{2,0},{3,1},{4,6},{5,7},{6,4},{7,5}} | collective-permute-start | bytes 12582920 | tf_op jit(solution)/shard_map/ppermute | solution.py:577
  59.1 110.0 %collective-permute-start.3 = (bf16[32,512,128]{2,1,0:T(8,128)(2,1)}, bf16[32,512,128]{2,1,0:T(8,128)(2,1)}, u32[]{:S(2)}, u32[]{:S(2)}) collective-permute-start(bf16[32,512,128]{2,1,0:T(8,128)(2,1)} %get-tuple-element.197), channel_id=1, source_target_pairs={{0,4},{1,5},{2,6},{3,7},{4,0},{5,1},{6,2},{7,3}} | collective-permute-start | bytes 12582920 | tf_op jit(solution)/shard_map/ppermute | solution.py:577
  60.6 108.5 %collective-permute-start.4 = (bf16[1,512,128]{2,1,0:T(8,128)(2,1)S(1)}, bf16[1,512,128]{2,1,0:T(8,128)(2,1)S(1)}, u32[]{:S(2)}, u32[]{:S(2)}) collective-permute-start(bf16[1,512,128]{2,1,0:T(8,128)(2,1)S(1)} %copy-done.15), channel_id=1, source_target_pairs={{0,4},{1,5},{2,6},{3,7},{4,0},{5,1},{6,2},{7,3}} | collective-permute-start | bytes 393224 | tf_op jit(solution)/shard_map/ppermute | solution.py:577
  61.1 92.2 %collective-permute-start.2 = (bf16[1,512,128]{2,1,0:T(8,128)(2,1)S(1)}, bf16[1,512,128]{2,1,0:T(8,128)(2,1)S(1)}, u32[]{:S(2)}, u32[]{:S(2)}) collective-permute-start(bf16[1,512,128]{2,1,0:T(8,128)(2,1)S(1)} %copy-done.15), channel_id=1, source_target_pairs={{0,2},{1,3},{2,0},{3,1},{4,6},{5,7},{6,4},{7,5}} | collective-permute-start | bytes 393224 | tf_op jit(solution)/shard_map/ppermute | solution.py:577
  184.9 7.5 %collective-permute-start.6 = (bf16[128,32,512]{2,1,0:T(8,128)(2,1)}, bf16[128,32,512]{2,1,0:T(8,128)(2,1)}, u32[]{:S(2)}, u32[]{:S(2)}) collective-permute-start(bf16[128,32,512]{2,1,0:T(8,128)(2,1)} %get-tuple-element.126.b_own1.refs_7_), channel_id=1, source_target_pairs={{0,1},{1,0},{2,3},{3,2},{4,5},{5,4},{6,7},{7,6}} | collective-permute-start | bytes 12582920 | tf_op jit(solution)/shard_map/ppermute | solution.py:577
  184.9 13.5 %collective-permute-start.5 = (bf16[128,32,512]{2,1,0:T(8,128)(2,1)}, bf16[128,32,512]{2,1,0:T(8,128)(2,1)}, u32[]{:S(2)}, u32[]{:S(2)}) collective-permute-start(bf16[128,32,512]{2,1,0:T(8,128)(2,1)} %get-tuple-element.125.b_own0.refs_6_), channel_id=1, source_target_pairs={{0,1},{1,0},{2,3},{3,2},{4,5},{5,4},{6,7},{7,6}} | collective-permute-start | bytes 12582920 | tf_op jit(solution)/shard_map/ppermute | solution.py:577
  185.4 97.9 %collective-permute-start.7 = (bf16[32,512,128]{2,1,0:T(8,128)(2,1)}, bf16[32,512,128]{2,1,0:T(8,128)(2,1)}, u32[]{:S(2)}, u32[]{:S(2)}) collective-permute-start(bf16[32,512,128]{2,1,0:T(8,128)(2,1)} %collective-permute-done.1.z_ref), channel_id=1, source_target_pairs={{0,4},{1,5},{2,6},{3,7},{4,0},{5,1},{6,2},{7,3}} | collective-permute-start | bytes 12582920 | tf_op jit(solution)/shard_map/ppermute | solution.py:577
  187.1 111.9 %collective-permute-start.9 = (bf16[32,512,128]{2,1,0:T(8,128)(2,1)}, bf16[32,512,128]{2,1,0:T(8,128)(2,1)}, u32[]{:S(2)}, u32[]{:S(2)}) collective-permute-start(bf16[32,512,128]{2,1,0:T(8,128)(2,1)} %collective-permute-done.3.z_ref), channel_id=1, source_target_pairs={{0,2},{1,3},{2,0},{3,1},{4,6},{5,7},{6,4},{7,5}} | collective-permute-start | bytes 12582920 | tf_op jit(solution)/shard_map/ppermute | solution.py:577
  188.6 94.7 %collective-permute-start.8 = (bf16[1,512,128]{2,1,0:T(8,128)(2,1)S(1)}, bf16[1,512,128]{2,1,0:T(8,128)(2,1)S(1)}, u32[]{:S(2)}, u32[]{:S(2)}) collective-permute-start(bf16[1,512,128]{2,1,0:T(8,128)(2,1)S(1)} %copy-done.15), channel_id=1, source_target_pairs={{0,6},{1,7},{2,4},{3,5},{4,2},{5,3},{6,0},{7,1}} | collective-permute-start | bytes 393224 | tf_op jit(solution)/shard_map/ppermute | solution.py:577
  192.4 180.0 %collective-permute-start.13 = (bf16[32,512,128]{2,1,0:T(8,128)(2,1)}, bf16[32,512,128]{2,1,0:T(8,128)(2,1)}, u32[]{:S(2)}, u32[]{:S(2)}) collective-permute-start(bf16[32,512,128]{2,1,0:T(8,128)(2,1)} %get-tuple-element.197), channel_id=1, source_target_pairs={{0,2},{1,3},{2,0},{3,1},{4,6},{5,7},{6,4},{7,5}} | collective-permute-start | bytes 12582920 | tf_op jit(solution)/shard_map/ppermute | solution.py:577
  198.4 209.0 %collective-permute-start.30 = (bf16[128,64,512]{2,1,0:T(8,128)(2,1)}, bf16[128,64,512]{2,1,0:T(8,128)(2,1)}, u32[]{:S(2)}, u32[]{:S(2)}) collective-permute-start(bf16[128,64,512]{2,1,0:T(8,128)(2,1)} %get-tuple-element.117.a_ref.refs_16_.refs_24_), channel_id=1, source_target_pairs={{0,1},{1,0},{2,3},{3,2},{4,5},{5,4},{6,7},{7,6}} | collective-permute-start | bytes 25165832 | tf_op jit(solution)/shard_map/ppermute | solution.py:577
  314.0 58.4 %collective-permute-start.11 = (bf16[128,32,512]{2,1,0:T(8,128)(2,1)}, bf16[128,32,512]{2,1,0:T(8,128)(2,1)}, u32[]{:S(2)}, u32[]{:S(2)}) collective-permute-start(bf16[128,32,512]{2,1,0:T(8,128)(2,1)} %get-tuple-element.131.b_own1.refs_2_), channel_id=1, source_target_pairs={{0,1},{1,0},{2,3},{3,2},{4,5},{5,4},{6,7},{7,6}} | collective-permute-start | bytes 12582920 | tf_op jit(solution)/shard_map/ppermute | solution.py:577
  314.0 58.9 %collective-permute-start.10 = (bf16[128,32,512]{2,1,0:T(8,128)(2,1)}, bf16[128,32,512]{2,1,0:T(8,128)(2,1)}, u32[]{:S(2)}, u32[]{:S(2)}) collective-permute-start(bf16[128,32,512]{2,1,0:T(8,128)(2,1)} %get-tuple-element.130.b_own0.refs_1_), channel_id=1, source_target_pairs={{0,1},{1,0},{2,3},{3,2},{4,5},{5,4},{6,7},{7,6}} | collective-permute-start | bytes 12582920 | tf_op jit(solution)/shard_map/ppermute | solution.py:577
  314.5 92.8 %collective-permute-start.12 = (bf16[32,512,128]{2,1,0:T(8,128)(2,1)}, bf16[32,512,128]{2,1,0:T(8,128)(2,1)}, u32[]{:S(2)}, u32[]{:S(2)}) collective-permute-start(bf16[32,512,128]{2,1,0:T(8,128)(2,1)} %get-tuple-element.198), channel_id=1, source_target_pairs={{0,4},{1,5},{2,6},{3,7},{4,0},{5,1},{6,2},{7,3}} | collective-permute-start | bytes 12582920 | tf_op jit(solution)/shard_map/ppermute | solution.py:577
  372.4 52.4 %collective-permute-start.35 = (bf16[128,32,512]{2,1,0:T(8,128)(2,1)}, bf16[128,32,512]{2,1,0:T(8,128)(2,1)}, u32[]{:S(2)}, u32[]{:S(2)}) collective-permute-start(bf16[128,32,512]{2,1,0:T(8,128)(2,1)} %get-tuple-element.162.refs_28_), channel_id=1, source_target_pairs={{0,1},{1,0},{2,3},{3,2},{4,5},{5,4},{6,7},{7,6}} | collective-permute-start | bytes 12582920 | tf_op jit(solution)/shard_map/ppermute | solution.py:577
  372.4 52.9 %collective-permute-start.31 = (bf16[128,32,512]{2,1,0:T(8,128)(2,1)}, bf16[128,32,512]{2,1,0:T(8,128)(2,1)}, u32[]{:S(2)}, u32[]{:S(2)}) collective-permute-start(bf16[128,32,512]{2,1,0:T(8,128)(2,1)} %get-tuple-element.158.refs_18_), channel_id=1, source_target_pairs={{0,1},{1,0},{2,3},{3,2},{4,5},{5,4},{6,7},{7,6}} | collective-permute-start | bytes 12582920 | tf_op jit(solution)/shard_map/ppermute | solution.py:577
  372.9 89.4 %collective-permute-start.36 = (bf16[128,32,512]{2,1,0:T(8,128)(2,1)}, bf16[128,32,512]{2,1,0:T(8,128)(2,1)}, u32[]{:S(2)}, u32[]{:S(2)}) collective-permute-start(bf16[128,32,512]{2,1,0:T(8,128)(2,1)} %get-tuple-element.163.refs_30_), channel_id=1, source_target_pairs={{0,1},{1,0},{2,3},{3,2},{4,5},{5,4},{6,7},{7,6}} | collective-permute-start | bytes 12582920 | tf_op jit(solution)/shard_map/ppermute | solution.py:577
  372.9 34.5 %copy-start.25 = (bf16[128,16,128]{2,1,0:T(8,128)(2,1)S(1)}, bf16[128,16,128]{2,1,0:T(8,128)(2,1)}, u32[]{:S(2)}) copy-start(bf16[128,16,128]{2,1,0:T(8,128)(2,1)} %get-tuple-element.143) | copy-start | bytes 1572868
  372.9 34.5 %copy-start.23 = (bf16[128,16,128]{2,1,0:T(8,128)(2,1)S(1)}, bf16[128,16,128]{2,1,0:T(8,128)(2,1)}, u32[]{:S(2)}) copy-start(bf16[128,16,128]{2,1,0:T(8,128)(2,1)} %get-tuple-element.151) | copy-start | bytes 1572868
  407.4 15.7 %collective-permute-start.16 = (bf16[128,16,128]{2,1,0:T(8,128)(2,1)S(1)}, bf16[128,16,128]{2,1,0:T(8,128)(2,1)S(1)}, u32[]{:S(2)}, u32[]{:S(2)}) collective-permute-start(bf16[128,16,128]{2,1,0:T(8,128)(2,1)S(1)} %copy-done.25), channel_id=1, source_target_pairs={{0,1},{1,0},{2,3},{3,2},{4,5},{5,4},{6,7},{7,6}} | collective-permute-start | bytes 1572872 | tf_op jit(solution)/shard_map/ppermute | solution.py:577
  407.4 17.4 %collective-permute-start.23 = (bf16[128,16,128]{2,1,0:T(8,128)(2,1)S(1)}, bf16[128,16,128]{2,1,0:T(8,128)(2,1)S(1)}, u32[]{:S(2)}, u32[]{:S(2)}) collective-permute-start(bf16[128,16,128]{2,1,0:T(8,128)(2,1)S(1)} %copy-done.23), channel_id=1, source_target_pairs={{0,1},{1,0},{2,3},{3,2},{4,5},{5,4},{6,7},{7,6}} | collective-permute-start | bytes 1572872 | tf_op jit(solution)/shard_map/ppermute | solution.py:577
  423.1 19.1 %collective-permute-start.17 = (bf16[128,16,128]{2,1,0:T(8,128)(2,1)}, bf16[128,16,128]{2,1,0:T(8,128)(2,1)S(1)}, u32[]{:S(2)}, u32[]{:S(2)}) collective-permute-start(bf16[128,16,128]{2,1,0:T(8,128)(2,1)} %get-tuple-element.144), channel_id=1, source_target_pairs={{0,2},{1,3},{2,0},{3,1},{4,6},{5,7},{6,4},{7,5}} | collective-permute-start | bytes 1572872 | tf_op jit(solution)/shard_map/ppermute | solution.py:577
  424.8 22.9 %collective-permute-start.18 = (bf16[128,16,128]{2,1,0:T(8,128)(2,1)}, bf16[128,16,128]{2,1,0:T(8,128)(2,1)S(1)}, u32[]{:S(2)}, u32[]{:S(2)}) collective-permute-start(bf16[128,16,128]{2,1,0:T(8,128)(2,1)} %get-tuple-element.145), channel_id=1, source_target_pairs={{0,3},{1,2},{2,1},{3,0},{4,7},{5,6},{6,5},{7,4}} | collective-permute-start | bytes 1572872 | tf_op jit(solution)/shard_map/ppermute | solution.py:577
  424.8 58.1 %collective-permute-start.33 = (bf16[128,32,512]{2,1,0:T(8,128)(2,1)}, bf16[128,32,512]{2,1,0:T(8,128)(2,1)}, u32[]{:S(2)}, u32[]{:S(2)}) collective-permute-start(bf16[128,32,512]{2,1,0:T(8,128)(2,1)} %get-tuple-element.160.refs_22_), channel_id=1, source_target_pairs={{0,1},{1,0},{2,3},{3,2},{4,5},{5,4},{6,7},{7,6}} | collective-permute-start | bytes 12582920 | tf_op jit(solution)/shard_map/ppermute | solution.py:577
  425.2 23.0 %collective-permute-start.26 = (bf16[128,16,128]{2,1,0:T(8,128)(2,1)S(1)}, bf16[128,16,128]{2,1,0:T(8,128)(2,1)S(1)}, u32[]{:S(2)}, u32[]{:S(2)}) collective-permute-start(bf16[128,16,128]{2,1,0:T(8,128)(2,1)S(1)} %copy-done.27), channel_id=1, source_target_pairs={{0,4},{1,5},{2,6},{3,7},{4,0},{5,1},{6,2},{7,3}} | collective-permute-start | bytes 1572872 | tf_op jit(solution)/shard_map/ppermute | solution.py:577
  442.2 40.7 %copy-start.3 = (bf16[128,16,128]{2,1,0:T(8,128)(2,1)}, bf16[128,16,128]{2,1,0:T(8,128)(2,1)S(1)}, u32[]{:S(2)}) copy-start(bf16[128,16,128]{2,1,0:T(8,128)(2,1)S(1)} %collective-permute-done.17.refs_2_) | copy-start | bytes 1572868
  442.2 62.5 %collective-permute-start.15 = (bf16[128,32,512]{2,1,0:T(8,128)(2,1)}, bf16[128,32,512]{2,1,0:T(8,128)(2,1)}, u32[]{:S(2)}, u32[]{:S(2)}) collective-permute-start(bf16[128,32,512]{2,1,0:T(8,128)(2,1)} %get-tuple-element.136.b_own1.refs_2_), channel_id=1, source_target_pairs={{0,1},{1,0},{2,3},{3,2},{4,5},{5,4},{6,7},{7,6}} | collective-permute-start | bytes 12582920 | tf_op jit(solution)/shard_map/ppermute | solution.py:577
  447.7 35.2 %copy-start.4 = (bf16[128,16,128]{2,1,0:T(8,128)(2,1)}, bf16[128,16,128]{2,1,0:T(8,128)(2,1)S(1)}, u32[]{:S(2)}) copy-start(bf16[128,16,128]{2,1,0:T(8,128)(2,1)S(1)} %collective-permute-done.18.refs_3_) | copy-start | bytes 1572868
  447.7 59.3 %collective-permute-start.14 = (bf16[128,32,512]{2,1,0:T(8,128)(2,1)}, bf16[128,32,512]{2,1,0:T(8,128)(2,1)}, u32[]{:S(2)}, u32[]{:S(2)}) collective-permute-start(bf16[128,32,512]{2,1,0:T(8,128)(2,1)} %get-tuple-element.135.b_own0.refs_1_), channel_id=1, source_target_pairs={{0,1},{1,0},{2,3},{3,2},{4,5},{5,4},{6,7},{7,6}} | collective-permute-start | bytes 12582920 | tf_op jit(solution)/shard_map/ppermute | solution.py:577
  448.2 34.7 %copy-start.5 = (bf16[128,16,128]{2,1,0:T(8,128)(2,1)}, bf16[128,16,128]{2,1,0:T(8,128)(2,1)S(1)}, u32[]{:S(2)}) copy-start(bf16[128,16,128]{2,1,0:T(8,128)(2,1)S(1)} %collective-permute-done.26.refs_12_) | copy-start | bytes 1572868
  448.2 13.9 %collective-permute-start.27 = (bf16[128,16,128]{2,1,0:T(8,128)(2,1)S(1)}, bf16[128,16,128]{2,1,0:T(8,128)(2,1)S(1)}, u32[]{:S(2)}, u32[]{:S(2)}) collective-permute-start(bf16[128,16,128]{2,1,0:T(8,128)(2,1)S(1)} %copy-done.26), channel_id=1, source_target_pairs={{0,5},{1,4},{2,7},{3,6},{4,1},{5,0},{6,3},{7,2}} | collective-permute-start | bytes 1572872 | tf_op jit(solution)/shard_map/ppermute | solution.py:577
  462.2 80.7 %collective-permute-start.34 = (bf16[128,32,512]{2,1,0:T(8,128)(2,1)}, bf16[128,32,512]{2,1,0:T(8,128)(2,1)}, u32[]{:S(2)}, u32[]{:S(2)}) collective-permute-start(bf16[128,32,512]{2,1,0:T(8,128)(2,1)} %get-tuple-element.161.refs_26_), channel_id=1, source_target_pairs={{0,1},{1,0},{2,3},{3,2},{4,5},{5,4},{6,7},{7,6}} | collective-permute-start | bytes 12582920 | tf_op jit(solution)/shard_map/ppermute | solution.py:577
  462.3 97.6 %collective-permute-start.32 = (bf16[128,32,512]{2,1,0:T(8,128)(2,1)}, bf16[128,32,512]{2,1,0:T(8,128)(2,1)}, u32[]{:S(2)}, u32[]{:S(2)}) collective-permute-start(bf16[128,32,512]{2,1,0:T(8,128)(2,1)} %get-tuple-element.159.refs_20_), channel_id=1, source_target_pairs={{0,1},{1,0},{2,3},{3,2},{4,5},{5,4},{6,7},{7,6}} | collective-permute-start | bytes 12582920 | tf_op jit(solution)/shard_map/ppermute | solution.py:577
  482.9 21.6 %collective-permute-start.21 = (bf16[128,16,128]{2,1,0:T(8,128)(2,1)S(1)}, bf16[128,16,128]{2,1,0:T(8,128)(2,1)S(1)}, u32[]{:S(2)}, u32[]{:S(2)}) collective-permute-start(bf16[128,16,128]{2,1,0:T(8,128)(2,1)S(1)} %copy-done.28), channel_id=1, source_target_pairs={{0,6},{1,7},{2,4},{3,5},{4,2},{5,3},{6,0},{7,1}} | collective-permute-start | bytes 1572872 | tf_op jit(solution)/shard_map/ppermute | solution.py:577
  485.7 21.3 %copy-start.21 = (bf16[128,16,128]{2,1,0:T(8,128)(2,1)S(1)}, bf16[128,16,128]{2,1,0:T(8,128)(2,1)}, u32[]{:S(2)}) copy-start(bf16[128,16,128]{2,1,0:T(8,128)(2,1)} %get-tuple-element.157) | copy-start | bytes 1572868
  504.6 27.3 %copy-start.7 = (bf16[128,16,128]{2,1,0:T(8,128)(2,1)}, bf16[128,16,128]{2,1,0:T(8,128)(2,1)S(1)}, u32[]{:S(2)}) copy-start(bf16[128,16,128]{2,1,0:T(8,128)(2,1)S(1)} %collective-permute-done.21.refs_6_) | copy-start | bytes 1572868
  504.6 27.3 %collective-permute-start.22 = (bf16[128,16,128]{2,1,0:T(8,128)(2,1)S(1)}, bf16[128,16,128]{2,1,0:T(8,128)(2,1)S(1)}, u32[]{:S(2)}, u32[]{:S(2)}) collective-permute-start(bf16[128,16,128]{2,1,0:T(8,128)(2,1)S(1)} %copy-done.24), channel_id=1, source_target_pairs={{0,7},{1,6},{2,5},{3,4},{4,3},{5,2},{6,1},{7,0}} | collective-permute-start | bytes 1572872 | tf_op jit(solution)/shard_map/ppermute | solution.py:577
  504.7 29.0 %collective-permute-start.28 = (bf16[128,16,128]{2,1,0:T(8,128)(2,1)S(1)}, bf16[128,16,128]{2,1,0:T(8,128)(2,1)S(1)}, u32[]{:S(2)}, u32[]{:S(2)}) collective-permute-start(bf16[128,16,128]{2,1,0:T(8,128)(2,1)S(1)} %copy-done.22), channel_id=1, source_target_pairs={{0,6},{1,7},{2,4},{3,5},{4,2},{5,3},{6,0},{7,1}} | collective-permute-start | bytes 1572872 | tf_op jit(solution)/shard_map/ppermute | solution.py:577
  507.0 35.3 %collective-permute-start.29 = (bf16[128,16,128]{2,1,0:T(8,128)(2,1)S(1)}, bf16[128,16,128]{2,1,0:T(8,128)(2,1)S(1)}, u32[]{:S(2)}, u32[]{:S(2)}) collective-permute-start(bf16[128,16,128]{2,1,0:T(8,128)(2,1)S(1)} %copy-done.21), channel_id=1, source_target_pairs={{0,7},{1,6},{2,5},{3,4},{4,3},{5,2},{6,1},{7,0}} | collective-permute-start | bytes 1572872 | tf_op jit(solution)/shard_map/ppermute | solution.py:577
  531.9 28.0 %copy-start.8 = (bf16[128,16,128]{2,1,0:T(8,128)(2,1)}, bf16[128,16,128]{2,1,0:T(8,128)(2,1)S(1)}, u32[]{:S(2)}) copy-start(bf16[128,16,128]{2,1,0:T(8,128)(2,1)S(1)} %collective-permute-done.22.refs_7_) | copy-start | bytes 1572868
  531.9 28.0 %collective-permute-start.19 = (bf16[128,16,128]{2,1,0:T(8,128)(2,1)}, bf16[128,16,128]{2,1,0:T(8,128)(2,1)S(1)}, u32[]{:S(2)}, u32[]{:S(2)}) collective-permute-start(bf16[128,16,128]{2,1,0:T(8,128)(2,1)} %get-tuple-element.146), channel_id=1, source_target_pairs={{0,4},{1,5},{2,6},{3,7},{4,0},{5,1},{6,2},{7,3}} | collective-permute-start | bytes 1572872 | tf_op jit(solution)/shard_map/ppermute | solution.py:577
  533.6 26.2 %copy-start.9 = (bf16[128,16,128]{2,1,0:T(8,128)(2,1)}, bf16[128,16,128]{2,1,0:T(8,128)(2,1)S(1)}, u32[]{:S(2)}) copy-start(bf16[128,16,128]{2,1,0:T(8,128)(2,1)S(1)} %collective-permute-done.28.refs_14_) | copy-start | bytes 1572868
  533.6 31.0 %collective-permute-start.20 = (bf16[128,16,128]{2,1,0:T(8,128)(2,1)}, bf16[128,16,128]{2,1,0:T(8,128)(2,1)S(1)}, u32[]{:S(2)}, u32[]{:S(2)}) collective-permute-start(bf16[128,16,128]{2,1,0:T(8,128)(2,1)} %get-tuple-element.147), channel_id=1, source_target_pairs={{0,5},{1,4},{2,7},{3,6},{4,1},{5,0},{6,3},{7,2}} | collective-permute-start | bytes 1572872 | tf_op jit(solution)/shard_map/ppermute | solution.py:577
  542.3 22.3 %collective-permute-start.24 = (bf16[128,16,128]{2,1,0:T(8,128)(2,1)}, bf16[128,16,128]{2,1,0:T(8,128)(2,1)S(1)}, u32[]{:S(2)}, u32[]{:S(2)}) collective-permute-start(bf16[128,16,128]{2,1,0:T(8,128)(2,1)} %get-tuple-element.152), channel_id=1, source_target_pairs={{0,2},{1,3},{2,0},{3,1},{4,6},{5,7},{6,4},{7,5}} | collective-permute-start | bytes 1572872 | tf_op jit(solution)/shard_map/ppermute | solution.py:577
  542.8 23.9 %collective-permute-start.25 = (bf16[128,16,128]{2,1,0:T(8,128)(2,1)}, bf16[128,16,128]{2,1,0:T(8,128)(2,1)S(1)}, u32[]{:S(2)}, u32[]{:S(2)}) collective-permute-start(bf16[128,16,128]{2,1,0:T(8,128)(2,1)} %get-tuple-element.153), channel_id=1, source_target_pairs={{0,3},{1,2},{2,1},{3,0},{4,7},{5,6},{6,5},{7,4}} | collective-permute-start | bytes 1572872 | tf_op jit(solution)/shard_map/ppermute | solution.py:577
  567.5 27.8 %copy-start.17 = (bf16[128]{0:T(256)(128)(2,1)S(1)}, bf16[128]{0:T(256)(128)(2,1)}, u32[]{:S(2)}) copy-start(bf16[128]{0:T(256)(128)(2,1)} %param.20) | copy-start | bytes 772
  567.5 28.6 %copy-start.18 = (bf16[128]{0:T(256)(128)(2,1)S(1)}, bf16[128]{0:T(256)(128)(2,1)}, u32[]{:S(2)}) copy-start(bf16[128]{0:T(256)(128)(2,1)} %param.21) | copy-start | bytes 772
  (22 other events, 248.8 us)

commit v4 on v3

--- a/solution.py
+++ b/solution.py
@@ -105,14 +105,15 @@
 TOKEN_SPEC = pl.BlockSpec(memory_space=pltpu.SMEM)
 
 
-def load_mask(m_ref, m_scr, ids_ref):
+def load_mask(m_ref, m_scr, t_scr, ids_ref):
+    t_scr[...] = m_ref[...].astype(F32).T
     for half, cols in halves():
-        m_scr[:, cols] = pair_row(m_ref, 0, ids_ref, half).astype(F32).T
-
-
-def gated_kernel(half_id, ids_ref, z_ref, m_ref, w_ref, scale_ref, offset_ref, a_ref, b_ref, tok_ref, a_scr, b_scr, m_scr):
+        m_scr[:, cols] = jnp.concatenate([t_scr[pl.ds(pl.multiple_of(ids_ref[8 * half + p], HALF), HALF), :] for p in range(8)], axis=0).T
+
+
+def gated_kernel(half_id, ids_ref, z_ref, m_ref, w_ref, scale_ref, offset_ref, a_ref, b_ref, tok_ref, a_scr, b_scr, m_scr, t_scr):
     pass_ids(ids_ref, tok_ref)
-    load_mask(m_ref, m_scr, ids_ref)
+    load_mask(m_ref, m_scr, t_scr, ids_ref)
     first = half_id * HALF + pl.program_id(0) * NB
 
     def body(row, carry):
@@ -121,7 +122,7 @@
             gated_half(w_ref, (a_scr, b_scr), row, half, z_norm, m_scr[pl.ds(first + row, 1), cols])
         return carry
 
-    lax.fori_loop(0, NB, body, 0, unroll=4)
+    lax.fori_loop(0, NB, body, 0, unroll=8)
     flush_rows(a_scr, a_ref)
     flush_rows(b_scr, b_ref)
 
@@ -135,11 +136,11 @@
             grid=(HALF // NB,),
             in_specs=[
                 pl.BlockSpec((NB, N, C), lambda r, ids: (r, 0, 0)),
-                full_spec((1, N, C)),
+                full_spec((NR, N)),
                 full_spec((4 * C, C + 16)), full_spec((C, WIDE)), full_spec((C, WIDE)),
             ],
             out_specs=[out_spec, out_spec, TOKEN_SPEC],
-            scratch_shapes=[pltpu.VMEM((4, C * SB, 128), F32)] * 2 + [pltpu.VMEM((C, N), F32)],
+            scratch_shapes=[pltpu.VMEM((4, C * SB, 128), F32)] * 2 + [pltpu.VMEM((NR, N), F32), pltpu.VMEM((N, NR), F32)],
         ),
         out_shape=[sds((C, HALF, N), BF16)] * 2 + [TOKEN],
         compiler_params=PARAMS,
@@ -154,7 +155,7 @@
 
 
 def own_kernel(ids_ref, z_ref, dy_ref, m_ref, w_ref, scale_ref, offset_ref, w_out_ref,
-               a_ref, b_ref, dup_ref, don_ref, g1_ref, dbout_ref, dooff_ref, tok_ref, a_scr, b_scr, m_scr):
+               a_ref, b_ref, dup_ref, don_ref, g1_ref, dbout_ref, dooff_ref, tok_ref, a_scr, b_scr, m_scr, t_scr):
     pass_ids(ids_ref, tok_ref)
 
     @pl.when(pl.program_id(0) == 0)
@@ -162,7 +163,7 @@
         dbout_ref[...] = jnp.zeros_like(dbout_ref)
         dooff_ref[...] = jnp.zeros_like(dooff_ref)
 
-    load_mask(m_ref, m_scr, ids_ref)
+    load_mask(m_ref, m_scr, t_scr, ids_ref)
     first = pl.program_id(0) * NB
 
     def body(row, carry):
@@ -194,10 +195,10 @@
         grid_spec=pltpu.PrefetchScalarGridSpec(
             num_scalar_prefetch=1,
             grid=(NQ,),
-            in_specs=[row_spec, row_spec, full_spec((1, N, C)),
+            in_specs=[row_spec, row_spec, full_spec((NR, N)),
                       full_spec((5 * C, C + 16)), full_spec((C, WIDE)), full_spec((C, WIDE)), full_spec((C, C))],
             out_specs=[act_spec, act_spec, t_spec, t_spec, t_spec, full_spec((C, 128)), full_spec((C, 128)), TOKEN_SPEC],
-            scratch_shapes=[pltpu.VMEM((4, C * SB, 128), F32)] * 2 + [pltpu.VMEM((C, N), F32)],
+            scratch_shapes=[pltpu.VMEM((4, C * SB, 128), F32)] * 2 + [pltpu.VMEM((NR, N), F32), pltpu.VMEM((N, NR), F32)],
         ),
         out_shape=[sds((C, NR, N), BF16), sds((C, NR, N), BF16), sds((NR, C, N), BF16), sds((NR, C, N), BF16), sds((NR, C, N), F32), sds((C, 128), F32), sds((C, 128), F32), TOKEN],
         compiler_params=PARAMS,
@@ -214,7 +215,9 @@
 
 
 def out_kernel(ids_ref, a_ref, b_own0, b_own1, b_par0, b_par1, don_ref, dup_ref, g1_ref, w_out_ref, scale_ref, offset_ref,
-               do_ref, dg_ref, same0, same1, cross0, cross1, dwout_ref, dosc_ref, dbg_ref, tok_ref, o_scr):
+               do_ref, dg_ref, *rest):
+    dwout_ref, dosc_ref, dbg_ref, tok_ref, o_scr = rest[-5:]
+    same0, same1, cross0, cross1 = rest[:-5] if len(rest) > 7 else [ref.at[h] for ref in rest[:2] for h in range(2)]
     step = pl.program_id(0)
     first_core = ids_ref[16] == 0
 
@@ -302,7 +305,10 @@
 def out_call(chunk, ids, a_own, b_pieces, don, dup, g1, w_out_t, scale, offset):
     lane_spec = pl.BlockSpec((CR, C, C), lambda s, ids: (chain_step(s), 0, chunk))
     acc_spec = full_spec((C, C))
-    pack_spec = pl.BlockSpec((CP, NB, C), lambda s, ids: (pack_step(s), 0, 0))
+    if chunk % 2:
+        packs, pack_spec = [sds((C, NB, C), BF16)] * 4, pl.BlockSpec((CP, NB, C), lambda s, ids: (pack_step(s), 0, 0))
+    else:
+        packs, pack_spec = [sds((2, C, NB, C), BF16)] * 2, pl.BlockSpec((2, CP, NB, C), lambda s, ids: (0, pack_step(s), 0, 0))
     b_specs = [pl.BlockSpec((CB, HALF, N), lambda s, ids, blk=blk: (prod_step(s), blk, 0)) for _, blk in b_pieces]
     return pl.pallas_call(
         out_kernel,
@@ -312,10 +318,10 @@
             in_specs=[pl.BlockSpec((CB, NR, N), lambda s, ids: (prod_step(s), 0, 0))] + b_specs
             + [lane_spec, lane_spec, lane_spec, full_spec((C, C + 16)), acc_spec, acc_spec],
             out_specs=[pl.BlockSpec((CP, NR, C), lambda s, ids: (pack_step(s), 0, 0)),
-                       pl.BlockSpec((CR, C, C), lambda s, ids: (chain_step(s), 0, 0))] + [pack_spec] * 4 + [acc_spec] * 3 + [TOKEN_SPEC],
+                       pl.BlockSpec((CR, C, C), lambda s, ids: (chain_step(s), 0, 0))] + [pack_spec] * len(packs) + [acc_spec] * 3 + [TOKEN_SPEC],
             scratch_shapes=[pltpu.VMEM((1, C * SO, C), F32)],
         ),
-        out_shape=[sds((C, NR, C), BF16), sds((NR, C, C), BF16)] + [sds((C, NB, C), BF16)] * 4 + [sds((C, C), F32)] * 3 + [TOKEN],
+        out_shape=[sds((C, NR, C), BF16), sds((NR, C, C), BF16)] + packs + [sds((C, C), F32)] * 3 + [TOKEN],
         compiler_params=PARAMS,
         cost_estimate=COST,
         name="out_chain",
@@ -364,21 +370,27 @@
         db_ref[ch] = total.astype(BF16)
 
 
+def do_spec(arr, half):
+    if len(arr.shape) > 3:
+        return pl.BlockSpec((None, CK, NB, C), lambda s: (half, s, 0, 0))
+    return pl.BlockSpec((CK, NB, C), lambda s: (s, 0, 0))
+
+
 def db_call(do_pieces, a_pieces):
     return pl.pallas_call(
         db_kernel,
         grid=(C // CK,),
-        in_specs=[pl.BlockSpec((CK, NB, 128), lambda s: (s, 0, 0))] * 16 + [piece_spec(CK, blk) for _, blk in a_pieces],
+        in_specs=[do_spec(*piece) for piece in do_pieces] + [piece_spec(CK, blk) for _, blk in a_pieces],
         out_specs=pl.BlockSpec((CK, NR, N), lambda s: (s, 0, 0)),
         out_shape=sds((C, NR, N), BF16),
         compiler_params=PARAMS,
         cost_estimate=COST,
         name="grad_b",
-    )(*do_pieces, *(arr for arr, _ in a_pieces))
+    )(*(arr for arr, _ in do_pieces), *(arr for arr, _ in a_pieces))
 
 
 def in_kernel(ids_ref, z_ref, dy_ref, m_ref, da_ref, db_ref, dg0, dg1, dg2, dg3, w_ref, scale_ref, offset_ref, w_cat_ref,
-              dz_ref, dw_ref, dbin_ref, dsc_ref, doff_ref, a_scr, b_scr, m_scr):
+              dz_ref, dw_ref, dbin_ref, dsc_ref, doff_ref, a_scr, b_scr, m_scr, t_scr):
     dgs = (dg0, dg1, dg2, dg3)
 
     @pl.when(pl.program_id(0) == 0)
@@ -396,7 +408,7 @@
 
     lax.fori_loop(0, C, unpack, 0, unroll=4)
 
-    load_mask(m_ref, m_scr, ids_ref)
+    load_mask(m_ref, m_scr, t_scr, ids_ref)
     first = pl.program_id(0) * NB
 
     def lanes4(val):
@@ -433,7 +445,7 @@
             dz_ref[row, pl.ds(pl.multiple_of(ids_ref[p], HALF), HALF), :] = d_row[HALF * p:HALF * (p + 1)]
         return carry
 
-    lax.fori_loop(0, NB, body, 0, unroll=4)
+    lax.fori_loop(0, NB, body, 0, unroll=8)
 
 
 def in_call(ids, z_loc, dy_loc, m_loc, d_a, d_b, dg_chunks, w_t, scale, offset, w_cat):
@@ -444,11 +456,11 @@
         grid_spec=pltpu.PrefetchScalarGridSpec(
             num_scalar_prefetch=1,
             grid=(NQ,),
-            in_specs=[row_spec, row_spec, full_spec((1, N, C)), act_spec, act_spec]
+            in_specs=[row_spec, row_spec, full_spec((NR, N)), act_spec, act_spec]
             + [pl.BlockSpec((NB, C, 128), lambda r, ids: (r, 0, 0))] * 4
             + [full_spec((4 * C, C + 16)), full_spec((C, N)), full_spec((C, N)), full_spec((C, 5 * C))],
             out_specs=[row_spec, full_spec((5 * C, C)), full_spec((4, C, C)), full_spec((C, 128)), full_spec((C, 128))],
-            scratch_shapes=[pltpu.VMEM((4, C * SB, 128), F32)] * 2 + [pltpu.VMEM((C, N), F32)],
+            scratch_shapes=[pltpu.VMEM((4, C * SB, 128), F32)] * 2 + [pltpu.VMEM((NR, N), F32), pltpu.VMEM((N, NR), F32)],
         ),
         out_shape=[sds((NR, N, C), BF16), sds((5 * C, C), F32), sds((4, C, C), F32), sds((C, 128), F32), sds((C, 128), F32)],
         compiler_params=PARAMS,
@@ -571,7 +583,7 @@
 
     order = [((chip * 2) ^ HOPS[q][h]) * NR + core_of * NR + h * HALF for q in range(4) for core_of in range(2) for h in range(2)]
     ids = jnp.stack(order + [core]).astype(jnp.int32)
-    mask_t = jnp.pad(mask_loc.T.astype(BF16), ((0, 0), (0, C - NR)))[None]
+    mask_t = mask_loc.astype(BF16)
 
     def move(val, flips):
         return lax.ppermute(val, 'dap', [(d, d ^ flips) for d in range(8)])
@@ -596,17 +608,22 @@
                 b_at[q, h, 1] = move(act_b, 1), 0
                 a_at[q, h, 1] = move(act_a, 1), 0
         b_pieces = [b_at[q, h, f] for f in range(2) for h in range(2)]
-        do_own, dg, same0, same1, cross0, cross1, *acc, ids = out_call(q, ids, a_own, b_pieces, don, dup, g1, w_out_t, out_scale, out_offset)
+        do_own, dg, *packs, acc_out, acc_osc, acc_bg, ids = out_call(q, ids, a_own, b_pieces, don, dup, g1, w_out_t, out_scale, out_offset)
         do_chunks.append(do_own)
         dg_chunks.append(dg)
-        sums.append(acc)
+        sums.append((acc_out, acc_osc, acc_bg))
         chunk_b += b_pieces
         if q:
             d_a = da_call(do_chunks, chunk_b, d_a, BF16 if q == 3 else F32)
             do_chunks, chunk_b, d_a = [], [], [d_a]
-        for flip, h, val in ((0, 0, same0), (0, 1, same1), (1, 0, cross0), (1, 1, cross1)):
+        for n, val in enumerate(packs):
+            flip, h = divmod(n, 2) if q % 2 else (n, 0)
             flips = HOPS[q][h] ^ flip
-            do_at[h, flips] = move(val, flips) if flips else val
+            val = move(val, flips) if flips else val
+            if q % 2:
+                do_at[h, flips] = (val, h)
+            else:
+                do_at[0, flips], do_at[1, flips] = (val, 0), (val, 1)
     chunk_of = {(HOPS[q][h], h): q for q in range(4) for h in range(2)}
     d_b = db_call([do_at[h, s] for h in range(2) for s in range(8)],
                   [a_at[chunk_of[s & 6, h], h, s & 1] for h in range(2) for s in range(8)])

time: 667 us -> 667 us (level)
    ppermute x37 -> x34, waiting for transfers between devices: 231 us -> 237 us  [move(): return lax.ppermute(val, 'dap', [(d, d ^ flips) for d in range(8)])]
    ppermute x37 -> x34, starting transfers between devices: 29.6 us -> 26.9 us  [move(): return lax.ppermute(val, 'dap', [(d, d ^ flips) for d in range(8)])]
  transfers between devices with their start and end apart: 37 -> 34, of which waited for: 12 -> 14; matrix products, arithmetic and copies ran while one was open for 1% -> 1% of each run, Pallas kernels for 34% -> 34%
where the time goes in v4:
time: 667 us
  Pallas kernels  378 us (57%)
  waiting for transfers between devices  237 us (36%)
  starting transfers between devices  26.9 us (4%)
  local copies, waits for them, and re-layouts  18.6 us (3%)
    ppermute x34, waiting for transfers between devices, move(): return lax.ppermute(val, 'dap', [(d, d ^ flips) for d in range(8)])  237 us
    pallas_call x4, Pallas kernels, out_call(): pl.pallas_call(out_kernel, grid_spec=pltpu.PrefetchScalarGridSpec(num_sca...  97.9 us
    pallas_call x6, Pallas kernels, gated_call(): pl.pallas_call(functools.partial(gated_kernel, half_id), grid_spec=pltpu....  89.3 us
    pallas_call x3, Pallas kernels, da_call(): pl.pallas_call(functools.partial(da_kernel, len(do_chunks)), grid=(C // C...  54.8 us
    pallas_call x1, Pallas kernels, in_call(): pl.pallas_call(in_kernel, grid_spec=pltpu.PrefetchScalarGridSpec(num_scal...  51.9 us
    pallas_call x1, Pallas kernels, own_call(): pl.pallas_call(own_kernel, grid_spec=pltpu.PrefetchScalarGridSpec(num_sca...  39 us
    pallas_call x1, Pallas kernels, db_call(): pl.pallas_call(db_kernel, grid=(C // CK,), in_specs=[do_spec(*piece) for...  27.8 us
    ppermute x34, starting transfers between devices, move(): return lax.ppermute(val, 'dap', [(d, d ^ flips) for d in range(8)])  26.9 us
  transfers between devices with their start and end apart: 34, of which 14 were waited for; matrix products, arithmetic and copies ran while one was open for 1% of the time, Pallas kernels for 34%

profile of v4, /device:TPU:0, one launch (start us, length us, event | category | flops | bytes accessed | tf_op | source)
XLA Modules:
  0.0 666.6 jit_solution(15540203250409264996)
XLA Ops:
  2.1 1.5 convert_element_type.17.m_ref
  3.6 0.9 constant_dynamic-update-slice_fusion.1
  6.7 0.9 copy.24.w_ref
  8.2 1.4 broadcast_in_dim.15.scale_ref
  9.5 1.4 broadcast_in_dim.16.offset_ref
  10.9 39.0 %own_rows.1 = (bf16[128,64,512]{2,1,0:T(8,128)(2,1)}, bf16[128,64,512]{2,1,0:T(8,128)(2,1)}, bf16[64,128,512]{2,1,0:T(8,128)(2,1)}, bf16[64,128,512]{2,1,0:T(8,1...) custom-call(s32[17]{0:T(128)} %stack.71.ids_ref, ...), custom_call_target="tpu_custom_call" | custom-call | flops 8589934592 | bytes 67108864 | tf_op jit(solution)/shard_map/own_rows/pallas_call | solution.py:193
  50.9 5.9 fusion.23
  56.8 2.5 collective-permute-start.1
  59.3 1.5 collective-permute-start.3
  65.4 24.0 %out_chain.4 = (bf16[128,64,128]{2,1,0:T(8,128)(2,1)}, bf16[64,128,128]{2,1,0:T(8,128)(2,1)}, bf16[2,128,16,128]{3,2,1,0:T(8,128)(2,1)}, bf16[2,128,16,128]{3,2,...) custom-call(s32[17]{0:T(128)} %get-tuple-element.112.ids_ref, ...), custom_call_target="tpu_custom_call" | custom-call | flops 8589934592 | bytes 67108864 | tf_op jit(solution)/shard_map/out_chain/pallas_call | solution.py:313
  89.5 62.7 %collective-permute-done.2.m_ref = bf16[64,512]{1,0:T(8,128)(2,1)S(1)} collective-permute-done((bf16[64,512]{1,0:T(8,128)(2,1)S(1)}, bf16[64,512]{1,0:T(8,128)(2,1)S(1)}, u32[]{:S(2)}, u32[]{:S(2)}) %collective-permute-start.2) | collective-permute-done | bytes 65568 | tf_op jit(solution)/shard_map/ppermute | solution.py:589
  152.8 14.8 %gated_rows.6 = (bf16[128,32,512]{2,1,0:T(8,128)(2,1)}, bf16[128,32,512]{2,1,0:T(8,128)(2,1)}, s32[17]{0:T(128)}) custom-call(s32[17]{0:T(128)} %get-tuple-element.118.ids_ref, bf16[32,512,128]{2,1,0:T(8,128)(2,1)} %collective-permute-done.1.z_ref, bf16[64,512]{1,0:T(8,128)(2,1)} %copy-done.19, bf16[512,144]{1,0:T(8,128)(2,1)} %copy.27.w_ref, ...), custom_call_target="tpu_custom_call" | custom-call | flops 8589934592 | bytes 67108864 | tf_op jit(solution)/shard_map/gated_rows/pallas_call | solution.py:132
  168.2 14.8 %gated_rows.7 = (bf16[128,32,512]{2,1,0:T(8,128)(2,1)}, bf16[128,32,512]{2,1,0:T(8,128)(2,1)}, s32[17]{0:T(128)}) custom-call(s32[17]{0:T(128)} %get-tuple-element.119.ids_ref, bf16[32,512,128]{2,1,0:T(8,128)(2,1)} %collective-permute-done.3.z_ref, bf16[64,512]{1,0:T(8,128)(2,1)} %copy-done.20, bf16[512,144]{1,0:T(8,128)(2,1)} %copy.27.w_ref, ...), custom_call_target="tpu_custom_call" | custom-call | flops 8589934592 | bytes 67108864 | tf_op jit(solution)/shard_map/gated_rows/pallas_call | solution.py:132
  183.6 1.8 collective-permute-start.7
  185.3 1.5 collective-permute-start.9
  187.1 3.5 collective-permute-done.6.b_par1.refs_9_
  190.6 1.8 collective-permute-start.13
  192.3 4.2 collective-permute-done.5.b_par0.refs_8_
  196.7 24.5 %out_chain.5 = (bf16[128,64,128]{2,1,0:T(8,128)(2,1)}, bf16[64,128,128]{2,1,0:T(8,128)(2,1)}, bf16[128,16,128]{2,1,0:T(8,128)(2,1)}, bf16[128,16,128]{2,1,0:T(8,...) custom-call(s32[17]{0:T(128)} %get-tuple-element.120.ids_ref, ...), custom_call_target="tpu_custom_call" | custom-call | flops 8589934592 | bytes 67108864 | tf_op jit(solution)/shard_map/out_chain/pallas_call | solution.py:313
  221.2 58.9 %collective-permute-done.8.m_ref = bf16[64,512]{1,0:T(8,128)(2,1)S(1)} collective-permute-done((bf16[64,512]{1,0:T(8,128)(2,1)S(1)}, bf16[64,512]{1,0:T(8,128)(2,1)S(1)}, u32[]{:S(2)}, u32[]{:S(2)}) %collective-permute-start.8) | collective-permute-done | bytes 65568 | tf_op jit(solution)/shard_map/ppermute | solution.py:589
  280.7 15.0 %gated_rows.8 = (bf16[128,32,512]{2,1,0:T(8,128)(2,1)}, bf16[128,32,512]{2,1,0:T(8,128)(2,1)}, s32[17]{0:T(128)}) custom-call(s32[17]{0:T(128)} %get-tuple-element.123.ids_ref, bf16[32,512,128]{2,1,0:T(8,128)(2,1)} %collective-permute-done.7.z_ref, bf16[64,512]{1,0:T(8,128)(2,1)} %copy-done.21, bf16[512,144]{1,0:T(8,128)(2,1)} %copy.27.w_ref, ...), custom_call_target="tpu_custom_call" | custom-call | flops 8589934592 | bytes 67108864 | tf_op jit(solution)/shard_map/gated_rows/pallas_call | solution.py:132
  295.7 14.8 %gated_rows.9 = (bf16[128,32,512]{2,1,0:T(8,128)(2,1)}, bf16[128,32,512]{2,1,0:T(8,128)(2,1)}, s32[17]{0:T(128)}) custom-call(s32[17]{0:T(128)} %get-tuple-element.124.ids_ref, bf16[32,512,128]{2,1,0:T(8,128)(2,1)} %collective-permute-done.9.z_ref, bf16[64,512]{1,0:T(8,128)(2,1)} %copy-done.21, bf16[512,144]{1,0:T(8,128)(2,1)} %copy.27.w_ref, ...), custom_call_target="tpu_custom_call" | custom-call | flops 8589934592 | bytes 67108864 | tf_op jit(solution)/shard_map/gated_rows/pallas_call | solution.py:132
  311.0 1.8 collective-permute-start.12
  312.8 56.4 %collective-permute-done.13.z_ref = bf16[32,512,128]{2,1,0:T(8,128)(2,1)} collective-permute-done((bf16[32,512,128]{2,1,0:T(8,128)(2,1)}, bf16[32,512,128]{2,1,0:T(8,128)(2,1)}, u32[]{:S(2)}, u32[]{:S(2)}) %collective-permute-start.13) | collective-permute-done | bytes 4194336 | tf_op jit(solution)/shard_map/ppermute | solution.py:589
  369.7 24.6 %out_chain.6 = (bf16[128,64,128]{2,1,0:T(8,128)(2,1)}, bf16[64,128,128]{2,1,0:T(8,128)(2,1)}, bf16[2,128,16,128]{3,2,1,0:T(8,128)(2,1)}, bf16[2,128,16,128]{3,2,...) custom-call(s32[17]{0:T(128)} %get-tuple-element.125.ids_ref, ...), custom_call_target="tpu_custom_call" | custom-call | flops 8589934592 | bytes 67108864 | tf_op jit(solution)/shard_map/out_chain/pallas_call | solution.py:313
  394.4 9.5 %collective-permute-done.12.z_ref = bf16[32,512,128]{2,1,0:T(8,128)(2,1)} collective-permute-done((bf16[32,512,128]{2,1,0:T(8,128)(2,1)}, bf16[32,512,128]{2,1,0:T(8,128)(2,1)}, u32[]{:S(2)}, u32[]{:S(2)}) %collective-permute-start.12) | collective-permute-done | bytes 4194336 | tf_op jit(solution)/shard_map/ppermute | solution.py:589
  403.9 14.8 %gated_rows.10 = (bf16[128,32,512]{2,1,0:T(8,128)(2,1)}, bf16[128,32,512]{2,1,0:T(8,128)(2,1)}, s32[17]{0:T(128)}) custom-call(s32[17]{0:T(128)} %get-tuple-element.128.ids_ref, bf16[32,512,128]{2,1,0:T(8,128)(2,1)} %collective-permute-done.12.z_ref, bf16[64,512]{1,0:T(8,128)(2,1)} %copy-done.20, bf16[512,144]{1,0:T(8,128)(2,1)} %copy.27.w_ref, ...), custom_call_target="tpu_custom_call" | custom-call | flops 8589934592 | bytes 67108864 | tf_op jit(solution)/shard_map/gated_rows/pallas_call | solution.py:132
  418.7 15.0 %gated_rows.11 = (bf16[128,32,512]{2,1,0:T(8,128)(2,1)}, bf16[128,32,512]{2,1,0:T(8,128)(2,1)}, s32[17]{0:T(128)}) custom-call(s32[17]{0:T(128)} %get-tuple-element.129.ids_ref, bf16[32,512,128]{2,1,0:T(8,128)(2,1)} %collective-permute-done.13.z_ref, bf16[64,512]{1,0:T(8,128)(2,1)} %copy-done.19, bf16[512,144]{1,0:T(8,128)(2,1)} %copy.27.w_ref, ...), custom_call_target="tpu_custom_call" | custom-call | flops 8589934592 | bytes 67108864 | tf_op jit(solution)/shard_map/gated_rows/pallas_call | solution.py:132
  434.3 1.7 collective-permute-start.17
  436.1 13.0 %collective-permute-done.17.refs_2_ = bf16[128,16,128]{2,1,0:T(8,128)(2,1)S(1)} collective-permute-done((bf16[128,16,128]{2,1,0:T(8,128)(2,1)S(1)}, bf16[128,16,128]{2,1,0:T(8,128)(2,1)S(1)}, u32[]{:S(2)}, u32[]{:S(2)}) %collective-permute-start.17) | collective-permute-done | bytes 524320 | tf_op jit(solution)/shard_map/ppermute | solution.py:589
  449.1 1.7 collective-permute-start.25
  450.9 8.5 %collective-permute-done.18.refs_3_ = bf16[128,16,128]{2,1,0:T(8,128)(2,1)S(1)} collective-permute-done((bf16[128,16,128]{2,1,0:T(8,128)(2,1)}, bf16[128,16,128]{2,1,0:T(8,128)(2,1)S(1)}, u32[]{:S(2)}, u32[]{:S(2)}) %collective-permute-start.18) | collective-permute-done | bytes 524320 | tf_op jit(solution)/shard_map/ppermute | solution.py:589
  459.3 2.0 collective-permute-start.26
  461.3 1.0 collective-permute-done.25.refs_12_
  462.3 11.2 %collective-permute-done.26.refs_13_ = bf16[128,16,128]{2,1,0:T(8,128)(2,1)S(1)} collective-permute-done((bf16[128,16,128]{2,1,0:T(8,128)(2,1)}, bf16[128,16,128]{2,1,0:T(8,128)(2,1)S(1)}, u32[]{:S(2)}, u32[]{:S(2)}) %collective-permute-start.26) | collective-permute-done | bytes 524320 | tf_op jit(solution)/shard_map/ppermute | solution.py:589
  473.9 20.2 %grad_a.3.refs_5_ = f32[128,64,512]{2,1,0:T(8,128)} custom-call(bf16[128,64,128]{2,1,0:T(8,128)(2,1)} %get-tuple-element.136.refs_0_, bf16[128,64,128]{2,1,0:T(8,128)(2,1)} %get-tuple-element.137.refs_1_, bf16[128,64,512]{2,1,0:T(8,128)(2,1)} %get-tuple-element.114.b_own0.b_own1.refs_2_.refs_3_, ...), custom_call_target="tpu_custom_call" | custom-call | flops 8589934592 | bytes 67108864 | tf_op jit(solution)/shard_map/grad_a/pallas_call | solution.py:347
  494.2 2.4 collective-permute-start.21
  496.8 18.6 %grad_a.4.refs_5_ = f32[128,64,512]{2,1,0:T(8,128)} custom-call(bf16[128,64,128]{2,1,0:T(8,128)(2,1)} %get-tuple-element.135.refs_0_, bf16[128,32,512]{2,1,0:T(8,128)(2,1)} %get-tuple-element.126.b_own0.refs_1_, bf16[128,32,512]{2,1,0:T(8,128)(2,1)} %get-tuple-element.127.b_own1.refs_2_, bf16[128,32,512]{2,1,0:T(8,128)(2,1)} %collective-permute-done.10.b_par0.refs_3_, ...), custom_call_target="tpu_custom_call" | custom-call | flops 8589934592 | bytes 67108864 | tf_op jit(solution)/shard_map/grad_a/pallas_call | solution.py:347
  515.4 24.7 %out_chain.7 = (bf16[128,64,128]{2,1,0:T(8,128)(2,1)}, bf16[64,128,128]{2,1,0:T(8,128)(2,1)}, bf16[128,16,128]{2,1,0:T(8,128)(2,1)}, bf16[128,16,128]{2,1,0:T(8,...) custom-call(s32[17]{0:T(128)} %get-tuple-element.130.ids_ref, ...), custom_call_target="tpu_custom_call" | custom-call | flops 8589934592 | bytes 67108864 | tf_op jit(solution)/shard_map/out_chain/pallas_call | solution.py:313
  540.1 1.5 collective-permute-start.19
  542.7 1.6 collective-permute-start.23
  544.4 16.1 %grad_a.5.da_ref = bf16[128,64,512]{2,1,0:T(8,128)(2,1)} custom-call(bf16[128,64,128]{2,1,0:T(8,128)(2,1)} %get-tuple-element.134.refs_0_, bf16[128,32,512]{2,1,0:T(8,128)(2,1)} %get-tuple-element.131.b_own0.refs_1_, bf16[128,32,512]{2,1,0:T(8,128)(2,1)} %get-tuple-element.132.b_own1.refs_2_, bf16[128,32,512]{2,1,0:T(8,128)(2,1)} %collective-permute-done.14.b_par0.refs_3_, ...), custom_call_target="tpu_custom_call" | custom-call | flops 8589934592 | bytes 67108864 | tf_op jit(solution)/shard_map/grad_a/pallas_call | solution.py:347
  560.6 4.6 collective-permute-done.20.refs_5_
  565.2 2.7 collective-permute-done.24.refs_11_
  567.9 27.8 %grad_b.1.db_ref = bf16[128,64,512]{2,1,0:T(8,128)(2,1)} custom-call(bf16[2,128,16,128]{3,2,1,0:T(8,128)(2,1)} %get-tuple-element.138.refs_0_.refs_8_, bf16[2,128,16,128]{3,2,1,0:T(8,128)(2,1)} %copy-done, bf16[128,16,128]{2,1,0:T(8,128)(2,1)} %copy-done.4, bf16[128,16,128]{2,1,0:T(8,128)(2,1)} %copy-done.5, bf16[128,16,128]{2,1,0:T(8,128)(2,1)} %copy-done.8, ...), custom_call_target="tpu_custom_call" | custom-call | flops 8589934592 | bytes 67108864 | tf_op jit(solution)/shard_map/grad_b/pallas_call | solution.py:380
  597.3 51.9 %in_backward.1 = (bf16[64,512,128]{2,1,0:T(8,128)(2,1)}, f32[640,128]{1,0:T(8,128)}, f32[4,128,128]{2,1,0:T(8,128)}, f32[128,128]{1,0:T(8,128)}, f32[128,128]{1,0:T(8,128)}) custom-call(s32[17]{0:T(128)} %get-tuple-element.133.ids_ref, bf16[64,512,128]{2,1,0:T(8,128)(2,1)} %z_ref.3, bf16[64,512,128]{2,1,0:T(8,128)(2,1)} %dy_ref.3, ...), custom_call_target="tpu_custom_call" | custom-call | flops 8589934592 | bytes 67108864 | tf_op jit(solution)/shard_map/in_backward/pallas_call | solution.py:454
  649.2 15.6 %sum_grads.1.total = bf16[896,128]{1,0:T(8,128)(2,1)} custom-call(f32[128,128]{1,0:T(8,128)} %get-tuple-element.161.refs_0_, f32[128,128]{1,0:T(8,128)} %get-tuple-element.162.refs_1_, f32[4,128,128]{2,1,0:T(8,128)} %get-tuple-element.163.refs_2_, f32[128,128]{1,0:T(8,128)} %get-tuple-element.164.refs_3_, f32[128,128]{1,0:T(8,128)} %get-tuple-element.165.refs_4_, ...), custom_call_target="tpu_custom_call" | custom-call | flops 8589934592 | bytes 67108864 | tf_op jit(solution)/shard_map/sum_grads/pallas_call | solution.py:542
  664.8 1.7 split_grads.1
  (109 shorter events, 17.8 us)
Async XLA Ops:
  50.0 11.5 %copy-start.22 = (bf16[128]{0:T(256)(128)(2,1)S(1)}, bf16[128]{0:T(256)(128)(2,1)}, u32[]{:S(2)}) copy-start(bf16[128]{0:T(256)(128)(2,1)} %param.27) | copy-start | bytes 772
  50.0 14.0 %copy-start.15 = (bf16[128]{0:T(256)(128)(2,1)S(1)}, bf16[128]{0:T(256)(128)(2,1)}, u32[]{:S(2)}) copy-start(bf16[128]{0:T(256)(128)(2,1)} %param.24) | copy-start | bytes 772
  50.0 14.7 %copy-start.16 = (bf16[128]{0:T(256)(128)(2,1)S(1)}, bf16[128]{0:T(256)(128)(2,1)}, u32[]{:S(2)}) copy-start(bf16[128]{0:T(256)(128)(2,1)} %param.25) | copy-start | bytes 772
  50.0 14.0 %collective-permute-start = (bf16[128,64,512]{2,1,0:T(8,128)(2,1)}, bf16[128,64,512]{2,1,0:T(8,128)(2,1)}, u32[]{:S(2)}, u32[]{:S(2)}) collective-permute-start(bf16[128,64,512]{2,1,0:T(8,128)(2,1)} %get-tuple-element.114.b_own0.b_own1.refs_2_.refs_3_), channel_id=1, source_target_pairs={{0,1},{1,0},{2,3},{3,2},{4,5},{5,4},{6,7},{7,6}} | collective-permute-start | bytes 25165832 | tf_op jit(solution)/shard_map/ppermute | solution.py:589
  56.8 95.3 %collective-permute-start.1 = (bf16[32,512,128]{2,1,0:T(8,128)(2,1)}, bf16[32,512,128]{2,1,0:T(8,128)(2,1)}, u32[]{:S(2)}, u32[]{:S(2)}) collective-permute-start(bf16[32,512,128]{2,1,0:T(8,128)(2,1)} %get-tuple-element.190), channel_id=1, source_target_pairs={{0,2},{1,3},{2,0},{3,1},{4,6},{5,7},{6,4},{7,5}} | collective-permute-start | bytes 12582920 | tf_op jit(solution)/shard_map/ppermute | solution.py:589
  59.3 108.3 %collective-permute-start.3 = (bf16[32,512,128]{2,1,0:T(8,128)(2,1)}, bf16[32,512,128]{2,1,0:T(8,128)(2,1)}, u32[]{:S(2)}, u32[]{:S(2)}) collective-permute-start(bf16[32,512,128]{2,1,0:T(8,128)(2,1)} %get-tuple-element.189), channel_id=1, source_target_pairs={{0,4},{1,5},{2,6},{3,7},{4,0},{5,1},{6,2},{7,3}} | collective-permute-start | bytes 12582920 | tf_op jit(solution)/shard_map/ppermute | solution.py:589
  60.8 106.7 %collective-permute-start.4 = (bf16[64,512]{1,0:T(8,128)(2,1)S(1)}, bf16[64,512]{1,0:T(8,128)(2,1)S(1)}, u32[]{:S(2)}, u32[]{:S(2)}) collective-permute-start(bf16[64,512]{1,0:T(8,128)(2,1)S(1)} %copy-done.11), channel_id=1, source_target_pairs={{0,4},{1,5},{2,6},{3,7},{4,0},{5,1},{6,2},{7,3}} | collective-permute-start | bytes 196616 | tf_op jit(solution)/shard_map/ppermute | solution.py:589
  61.4 90.8 %collective-permute-start.2 = (bf16[64,512]{1,0:T(8,128)(2,1)S(1)}, bf16[64,512]{1,0:T(8,128)(2,1)S(1)}, u32[]{:S(2)}, u32[]{:S(2)}) collective-permute-start(bf16[64,512]{1,0:T(8,128)(2,1)S(1)} %copy-done.11), channel_id=1, source_target_pairs={{0,2},{1,3},{2,0},{3,1},{4,6},{5,7},{6,4},{7,5}} | collective-permute-start | bytes 196616 | tf_op jit(solution)/shard_map/ppermute | solution.py:589
  183.1 7.5 %collective-permute-start.6 = (bf16[128,32,512]{2,1,0:T(8,128)(2,1)}, bf16[128,32,512]{2,1,0:T(8,128)(2,1)}, u32[]{:S(2)}, u32[]{:S(2)}) collective-permute-start(bf16[128,32,512]{2,1,0:T(8,128)(2,1)} %get-tuple-element.122.b_own1.refs_7_), channel_id=1, source_target_pairs={{0,1},{1,0},{2,3},{3,2},{4,5},{5,4},{6,7},{7,6}} | collective-permute-start | bytes 12582920 | tf_op jit(solution)/shard_map/ppermute | solution.py:589
  183.1 13.5 %collective-permute-start.5 = (bf16[128,32,512]{2,1,0:T(8,128)(2,1)}, bf16[128,32,512]{2,1,0:T(8,128)(2,1)}, u32[]{:S(2)}, u32[]{:S(2)}) collective-permute-start(bf16[128,32,512]{2,1,0:T(8,128)(2,1)} %get-tuple-element.121.b_own0.refs_6_), channel_id=1, source_target_pairs={{0,1},{1,0},{2,3},{3,2},{4,5},{5,4},{6,7},{7,6}} | collective-permute-start | bytes 12582920 | tf_op jit(solution)/shard_map/ppermute | solution.py:589
  183.6 96.5 %collective-permute-start.7 = (bf16[32,512,128]{2,1,0:T(8,128)(2,1)}, bf16[32,512,128]{2,1,0:T(8,128)(2,1)}, u32[]{:S(2)}, u32[]{:S(2)}) collective-permute-start(bf16[32,512,128]{2,1,0:T(8,128)(2,1)} %collective-permute-done.1.z_ref), channel_id=1, source_target_pairs={{0,4},{1,5},{2,6},{3,7},{4,0},{5,1},{6,2},{7,3}} | collective-permute-start | bytes 12582920 | tf_op jit(solution)/shard_map/ppermute | solution.py:589
  185.3 110.4 %collective-permute-start.9 = (bf16[32,512,128]{2,1,0:T(8,128)(2,1)}, bf16[32,512,128]{2,1,0:T(8,128)(2,1)}, u32[]{:S(2)}, u32[]{:S(2)}) collective-permute-start(bf16[32,512,128]{2,1,0:T(8,128)(2,1)} %collective-permute-done.3.z_ref), channel_id=1, source_target_pairs={{0,2},{1,3},{2,0},{3,1},{4,6},{5,7},{6,4},{7,5}} | collective-permute-start | bytes 12582920 | tf_op jit(solution)/shard_map/ppermute | solution.py:589
  186.8 93.3 %collective-permute-start.8 = (bf16[64,512]{1,0:T(8,128)(2,1)S(1)}, bf16[64,512]{1,0:T(8,128)(2,1)S(1)}, u32[]{:S(2)}, u32[]{:S(2)}) collective-permute-start(bf16[64,512]{1,0:T(8,128)(2,1)S(1)} %copy-done.11), channel_id=1, source_target_pairs={{0,6},{1,7},{2,4},{3,5},{4,2},{5,3},{6,0},{7,1}} | collective-permute-start | bytes 196616 | tf_op jit(solution)/shard_map/ppermute | solution.py:589
  190.6 178.6 %collective-permute-start.13 = (bf16[32,512,128]{2,1,0:T(8,128)(2,1)}, bf16[32,512,128]{2,1,0:T(8,128)(2,1)}, u32[]{:S(2)}, u32[]{:S(2)}) collective-permute-start(bf16[32,512,128]{2,1,0:T(8,128)(2,1)} %get-tuple-element.189), channel_id=1, source_target_pairs={{0,2},{1,3},{2,0},{3,1},{4,6},{5,7},{6,4},{7,5}} | collective-permute-start | bytes 12582920 | tf_op jit(solution)/shard_map/ppermute | solution.py:589
  196.6 237.2 %collective-permute-start.27 = (bf16[128,64,512]{2,1,0:T(8,128)(2,1)}, bf16[128,64,512]{2,1,0:T(8,128)(2,1)}, u32[]{:S(2)}, u32[]{:S(2)}) collective-permute-start(bf16[128,64,512]{2,1,0:T(8,128)(2,1)} %get-tuple-element.113.a_ref.refs_16_.refs_24_), channel_id=1, source_target_pairs={{0,1},{1,0},{2,3},{3,2},{4,5},{5,4},{6,7},{7,6}} | collective-permute-start | bytes 25165832 | tf_op jit(solution)/shard_map/ppermute | solution.py:589
  310.5 58.7 %collective-permute-start.11 = (bf16[128,32,512]{2,1,0:T(8,128)(2,1)}, bf16[128,32,512]{2,1,0:T(8,128)(2,1)}, u32[]{:S(2)}, u32[]{:S(2)}) collective-permute-start(bf16[128,32,512]{2,1,0:T(8,128)(2,1)} %get-tuple-element.127.b_own1.refs_2_), channel_id=1, source_target_pairs={{0,1},{1,0},{2,3},{3,2},{4,5},{5,4},{6,7},{7,6}} | collective-permute-start | bytes 12582920 | tf_op jit(solution)/shard_map/ppermute | solution.py:589
  310.5 59.2 %collective-permute-start.10 = (bf16[128,32,512]{2,1,0:T(8,128)(2,1)}, bf16[128,32,512]{2,1,0:T(8,128)(2,1)}, u32[]{:S(2)}, u32[]{:S(2)}) collective-permute-start(bf16[128,32,512]{2,1,0:T(8,128)(2,1)} %get-tuple-element.126.b_own0.refs_1_), channel_id=1, source_target_pairs={{0,1},{1,0},{2,3},{3,2},{4,5},{5,4},{6,7},{7,6}} | collective-permute-start | bytes 12582920 | tf_op jit(solution)/shard_map/ppermute | solution.py:589
  311.0 92.9 %collective-permute-start.12 = (bf16[32,512,128]{2,1,0:T(8,128)(2,1)}, bf16[32,512,128]{2,1,0:T(8,128)(2,1)}, u32[]{:S(2)}, u32[]{:S(2)}) collective-permute-start(bf16[32,512,128]{2,1,0:T(8,128)(2,1)} %get-tuple-element.190), channel_id=1, source_target_pairs={{0,4},{1,5},{2,6},{3,7},{4,0},{5,1},{6,2},{7,3}} | collective-permute-start | bytes 12582920 | tf_op jit(solution)/shard_map/ppermute | solution.py:589
  369.2 65.2 %collective-permute-start.32 = (bf16[128,32,512]{2,1,0:T(8,128)(2,1)}, bf16[128,32,512]{2,1,0:T(8,128)(2,1)}, u32[]{:S(2)}, u32[]{:S(2)}) collective-permute-start(bf16[128,32,512]{2,1,0:T(8,128)(2,1)} %get-tuple-element.154.refs_28_), channel_id=1, source_target_pairs={{0,1},{1,0},{2,3},{3,2},{4,5},{5,4},{6,7},{7,6}} | collective-permute-start | bytes 12582920 | tf_op jit(solution)/shard_map/ppermute | solution.py:589
  369.2 66.9 %collective-permute-start.28 = (bf16[128,32,512]{2,1,0:T(8,128)(2,1)}, bf16[128,32,512]{2,1,0:T(8,128)(2,1)}, u32[]{:S(2)}, u32[]{:S(2)}) collective-permute-start(bf16[128,32,512]{2,1,0:T(8,128)(2,1)} %get-tuple-element.150.refs_18_), channel_id=1, source_target_pairs={{0,1},{1,0},{2,3},{3,2},{4,5},{5,4},{6,7},{7,6}} | collective-permute-start | bytes 12582920 | tf_op jit(solution)/shard_map/ppermute | solution.py:589
  369.7 104.1 %collective-permute-start.33 = (bf16[128,32,512]{2,1,0:T(8,128)(2,1)}, bf16[128,32,512]{2,1,0:T(8,128)(2,1)}, u32[]{:S(2)}, u32[]{:S(2)}) collective-permute-start(bf16[128,32,512]{2,1,0:T(8,128)(2,1)} %get-tuple-element.155.refs_30_), channel_id=1, source_target_pairs={{0,1},{1,0},{2,3},{3,2},{4,5},{5,4},{6,7},{7,6}} | collective-permute-start | bytes 12582920 | tf_op jit(solution)/shard_map/ppermute | solution.py:589
  369.7 34.2 %copy-start.17 = (bf16[2,128,16,128]{3,2,1,0:T(8,128)(2,1)S(1)}, bf16[2,128,16,128]{3,2,1,0:T(8,128)(2,1)}, u32[]{:S(2)}) copy-start(bf16[2,128,16,128]{3,2,1,0:T(8,128)(2,1)} %get-tuple-element.139) | copy-start | bytes 3145732
  403.9 30.4 %collective-permute-start.16 = (bf16[2,128,16,128]{3,2,1,0:T(8,128)(2,1)S(1)}, bf16[2,128,16,128]{3,2,1,0:T(8,128)(2,1)S(1)}, u32[]{:S(2)}, u32[]{:S(2)}) collective-permute-start(bf16[2,128,16,128]{3,2,1,0:T(8,128)(2,1)S(1)} %copy-done.17), channel_id=1, source_target_pairs={{0,1},{1,0},{2,3},{3,2},{4,5},{5,4},{6,7},{7,6}} | collective-permute-start | bytes 3145736 | tf_op jit(solution)/shard_map/ppermute | solution.py:589
  418.7 15.6 %copy-start.18 = (bf16[128,16,128]{2,1,0:T(8,128)(2,1)S(1)}, bf16[128,16,128]{2,1,0:T(8,128)(2,1)}, u32[]{:S(2)}) copy-start(bf16[128,16,128]{2,1,0:T(8,128)(2,1)} %get-tuple-element.140) | copy-start | bytes 1572868
  433.7 60.4 %collective-permute-start.15 = (bf16[128,32,512]{2,1,0:T(8,128)(2,1)}, bf16[128,32,512]{2,1,0:T(8,128)(2,1)}, u32[]{:S(2)}, u32[]{:S(2)}) collective-permute-start(bf16[128,32,512]{2,1,0:T(8,128)(2,1)} %get-tuple-element.132.b_own1.refs_2_), channel_id=1, source_target_pairs={{0,1},{1,0},{2,3},{3,2},{4,5},{5,4},{6,7},{7,6}} | collective-permute-start | bytes 12582920 | tf_op jit(solution)/shard_map/ppermute | solution.py:589
  434.3 59.8 %copy-start = (bf16[2,128,16,128]{3,2,1,0:T(8,128)(2,1)}, bf16[2,128,16,128]{3,2,1,0:T(8,128)(2,1)S(1)}, u32[]{:S(2)}) copy-start(bf16[2,128,16,128]{3,2,1,0:T(8,128)(2,1)S(1)} %collective-permute-done.16.refs_1_.refs_9_) | copy-start | bytes 3145732
  434.3 62.3 %collective-permute-start.14 = (bf16[128,32,512]{2,1,0:T(8,128)(2,1)}, bf16[128,32,512]{2,1,0:T(8,128)(2,1)}, u32[]{:S(2)}, u32[]{:S(2)}) collective-permute-start(bf16[128,32,512]{2,1,0:T(8,128)(2,1)} %get-tuple-element.131.b_own0.refs_1_), channel_id=1, source_target_pairs={{0,1},{1,0},{2,3},{3,2},{4,5},{5,4},{6,7},{7,6}} | collective-permute-start | bytes 12582920 | tf_op jit(solution)/shard_map/ppermute | solution.py:589
  434.3 14.8 %collective-permute-start.17 = (bf16[128,16,128]{2,1,0:T(8,128)(2,1)S(1)}, bf16[128,16,128]{2,1,0:T(8,128)(2,1)S(1)}, u32[]{:S(2)}, u32[]{:S(2)}) collective-permute-start(bf16[128,16,128]{2,1,0:T(8,128)(2,1)S(1)} %copy-done.18), channel_id=1, source_target_pairs={{0,2},{1,3},{2,0},{3,1},{4,6},{5,7},{6,4},{7,5}} | collective-permute-start | bytes 1572872 | tf_op jit(solution)/shard_map/ppermute | solution.py:589
  436.0 23.3 %collective-permute-start.18 = (bf16[128,16,128]{2,1,0:T(8,128)(2,1)}, bf16[128,16,128]{2,1,0:T(8,128)(2,1)S(1)}, u32[]{:S(2)}, u32[]{:S(2)}) collective-permute-start(bf16[128,16,128]{2,1,0:T(8,128)(2,1)} %get-tuple-element.141), channel_id=1, source_target_pairs={{0,3},{1,2},{2,1},{3,0},{4,7},{5,6},{6,5},{7,4}} | collective-permute-start | bytes 1572872 | tf_op jit(solution)/shard_map/ppermute | solution.py:589
  449.1 45.0 %copy-start.4 = (bf16[128,16,128]{2,1,0:T(8,128)(2,1)}, bf16[128,16,128]{2,1,0:T(8,128)(2,1)S(1)}, u32[]{:S(2)}) copy-start(bf16[128,16,128]{2,1,0:T(8,128)(2,1)S(1)} %collective-permute-done.17.refs_2_) | copy-start | bytes 1572868
  449.1 13.1 %collective-permute-start.25 = (bf16[128,16,128]{2,1,0:T(8,128)(2,1)}, bf16[128,16,128]{2,1,0:T(8,128)(2,1)S(1)}, u32[]{:S(2)}, u32[]{:S(2)}) collective-permute-start(bf16[128,16,128]{2,1,0:T(8,128)(2,1)} %get-tuple-element.148), channel_id=1, source_target_pairs={{0,4},{1,5},{2,6},{3,7},{4,0},{5,1},{6,2},{7,3}} | collective-permute-start | bytes 1572872 | tf_op jit(solution)/shard_map/ppermute | solution.py:589
  459.3 34.8 %copy-start.5 = (bf16[128,16,128]{2,1,0:T(8,128)(2,1)}, bf16[128,16,128]{2,1,0:T(8,128)(2,1)S(1)}, u32[]{:S(2)}) copy-start(bf16[128,16,128]{2,1,0:T(8,128)(2,1)S(1)} %collective-permute-done.18.refs_3_) | copy-start | bytes 1572868
  459.3 14.1 %collective-permute-start.26 = (bf16[128,16,128]{2,1,0:T(8,128)(2,1)}, bf16[128,16,128]{2,1,0:T(8,128)(2,1)S(1)}, u32[]{:S(2)}, u32[]{:S(2)}) collective-permute-start(bf16[128,16,128]{2,1,0:T(8,128)(2,1)} %get-tuple-element.149), channel_id=1, source_target_pairs={{0,5},{1,4},{2,7},{3,6},{4,1},{5,0},{6,3},{7,2}} | collective-permute-start | bytes 1572872 | tf_op jit(solution)/shard_map/ppermute | solution.py:589
  462.3 31.9 %copy-start.6 = (bf16[128,16,128]{2,1,0:T(8,128)(2,1)}, bf16[128,16,128]{2,1,0:T(8,128)(2,1)S(1)}, u32[]{:S(2)}) copy-start(bf16[128,16,128]{2,1,0:T(8,128)(2,1)S(1)} %collective-permute-done.25.refs_12_) | copy-start | bytes 1572868
  462.3 77.8 %collective-permute-start.30 = (bf16[128,32,512]{2,1,0:T(8,128)(2,1)}, bf16[128,32,512]{2,1,0:T(8,128)(2,1)}, u32[]{:S(2)}, u32[]{:S(2)}) collective-permute-start(bf16[128,32,512]{2,1,0:T(8,128)(2,1)} %get-tuple-element.152.refs_22_), channel_id=1, source_target_pairs={{0,1},{1,0},{2,3},{3,2},{4,5},{5,4},{6,7},{7,6}} | collective-permute-start | bytes 12582920 | tf_op jit(solution)/shard_map/ppermute | solution.py:589
  473.4 20.7 %copy-start.7 = (bf16[128,16,128]{2,1,0:T(8,128)(2,1)}, bf16[128,16,128]{2,1,0:T(8,128)(2,1)S(1)}, u32[]{:S(2)}) copy-start(bf16[128,16,128]{2,1,0:T(8,128)(2,1)S(1)} %collective-permute-done.26.refs_13_) | copy-start | bytes 1572868
  473.4 70.8 %collective-permute-start.31 = (bf16[128,32,512]{2,1,0:T(8,128)(2,1)}, bf16[128,32,512]{2,1,0:T(8,128)(2,1)}, u32[]{:S(2)}, u32[]{:S(2)}) collective-permute-start(bf16[128,32,512]{2,1,0:T(8,128)(2,1)} %get-tuple-element.153.refs_26_), channel_id=1, source_target_pairs={{0,1},{1,0},{2,3},{3,2},{4,5},{5,4},{6,7},{7,6}} | collective-permute-start | bytes 12582920 | tf_op jit(solution)/shard_map/ppermute | solution.py:589
  473.8 86.7 %collective-permute-start.29 = (bf16[128,32,512]{2,1,0:T(8,128)(2,1)}, bf16[128,32,512]{2,1,0:T(8,128)(2,1)}, u32[]{:S(2)}, u32[]{:S(2)}) collective-permute-start(bf16[128,32,512]{2,1,0:T(8,128)(2,1)} %get-tuple-element.151.refs_20_), channel_id=1, source_target_pairs={{0,1},{1,0},{2,3},{3,2},{4,5},{5,4},{6,7},{7,6}} | collective-permute-start | bytes 12582920 | tf_op jit(solution)/shard_map/ppermute | solution.py:589
  494.2 47.5 %collective-permute-start.21 = (bf16[2,128,16,128]{3,2,1,0:T(8,128)(2,1)}, bf16[2,128,16,128]{3,2,1,0:T(8,128)(2,1)S(1)}, u32[]{:S(2)}, u32[]{:S(2)}) collective-permute-start(bf16[2,128,16,128]{3,2,1,0:T(8,128)(2,1)} %get-tuple-element.144), channel_id=1, source_target_pairs={{0,6},{1,7},{2,4},{3,5},{4,2},{5,3},{6,0},{7,1}} | collective-permute-start | bytes 3145736 | tf_op jit(solution)/shard_map/ppermute | solution.py:589
  496.5 46.1 %collective-permute-start.22 = (bf16[2,128,16,128]{3,2,1,0:T(8,128)(2,1)}, bf16[2,128,16,128]{3,2,1,0:T(8,128)(2,1)S(1)}, u32[]{:S(2)}, u32[]{:S(2)}) collective-permute-start(bf16[2,128,16,128]{3,2,1,0:T(8,128)(2,1)} %get-tuple-element.145), channel_id=1, source_target_pairs={{0,7},{1,6},{2,5},{3,4},{4,3},{5,2},{6,1},{7,0}} | collective-permute-start | bytes 3145736 | tf_op jit(solution)/shard_map/ppermute | solution.py:589
  540.1 20.5 %collective-permute-start.19 = (bf16[128,16,128]{2,1,0:T(8,128)(2,1)}, bf16[128,16,128]{2,1,0:T(8,128)(2,1)S(1)}, u32[]{:S(2)}, u32[]{:S(2)}) collective-permute-start(bf16[128,16,128]{2,1,0:T(8,128)(2,1)} %get-tuple-element.142), channel_id=1, source_target_pairs={{0,4},{1,5},{2,6},{3,7},{4,0},{5,1},{6,2},{7,3}} | collective-permute-start | bytes 1572872 | tf_op jit(solution)/shard_map/ppermute | solution.py:589
  541.6 18.9 %copy-start.1 = (bf16[2,128,16,128]{3,2,1,0:T(8,128)(2,1)}, bf16[2,128,16,128]{3,2,1,0:T(8,128)(2,1)S(1)}, u32[]{:S(2)}) copy-start(bf16[2,128,16,128]{3,2,1,0:T(8,128)(2,1)S(1)} %collective-permute-done.21.refs_6_.refs_14_) | copy-start | bytes 3145732
  541.6 23.6 %collective-permute-start.20 = (bf16[128,16,128]{2,1,0:T(8,128)(2,1)}, bf16[128,16,128]{2,1,0:T(8,128)(2,1)S(1)}, u32[]{:S(2)}, u32[]{:S(2)}) collective-permute-start(bf16[128,16,128]{2,1,0:T(8,128)(2,1)} %get-tuple-element.143), channel_id=1, source_target_pairs={{0,5},{1,4},{2,7},{3,6},{4,1},{5,0},{6,3},{7,2}} | collective-permute-start | bytes 1572872 | tf_op jit(solution)/shard_map/ppermute | solution.py:589
  542.6 17.9 %copy-start.2 = (bf16[2,128,16,128]{3,2,1,0:T(8,128)(2,1)}, bf16[2,128,16,128]{3,2,1,0:T(8,128)(2,1)S(1)}, u32[]{:S(2)}) copy-start(bf16[2,128,16,128]{3,2,1,0:T(8,128)(2,1)S(1)} %collective-permute-done.22.refs_7_.refs_15_) | copy-start | bytes 3145732
  542.7 22.5 %collective-permute-start.23 = (bf16[128,16,128]{2,1,0:T(8,128)(2,1)}, bf16[128,16,128]{2,1,0:T(8,128)(2,1)S(1)}, u32[]{:S(2)}, u32[]{:S(2)}) collective-permute-start(bf16[128,16,128]{2,1,0:T(8,128)(2,1)} %get-tuple-element.146), channel_id=1, source_target_pairs={{0,2},{1,3},{2,0},{3,1},{4,6},{5,7},{6,4},{7,5}} | collective-permute-start | bytes 1572872 | tf_op jit(solution)/shard_map/ppermute | solution.py:589
  544.2 23.6 %collective-permute-start.24 = (bf16[128,16,128]{2,1,0:T(8,128)(2,1)}, bf16[128,16,128]{2,1,0:T(8,128)(2,1)}, u32[]{:S(2)}, u32[]{:S(2)}) collective-permute-start(bf16[128,16,128]{2,1,0:T(8,128)(2,1)} %get-tuple-element.147), channel_id=1, source_target_pairs={{0,3},{1,2},{2,1},{3,0},{4,7},{5,6},{6,5},{7,4}} | collective-permute-start | bytes 1572872 | tf_op jit(solution)/shard_map/ppermute | solution.py:589
  567.9 27.8 %copy-start.13 = (bf16[128]{0:T(256)(128)(2,1)S(1)}, bf16[128]{0:T(256)(128)(2,1)}, u32[]{:S(2)}) copy-start(bf16[128]{0:T(256)(128)(2,1)} %param.20) | copy-start | bytes 772
  567.9 28.6 %copy-start.14 = (bf16[128]{0:T(256)(128)(2,1)S(1)}, bf16[128]{0:T(256)(128)(2,1)}, u32[]{:S(2)}) copy-start(bf16[128]{0:T(256)(128)(2,1)} %param.21) | copy-start | bytes 772
  (9 other events, 37.5 us)

commit v5 on v4

--- a/solution.py
+++ b/solution.py
@@ -475,8 +475,8 @@
 
 
 def sum_kernel(*refs):
-    accs, wout_refs, osc_refs, bg_refs, w_ref = refs[:7], refs[7:11], refs[11:14], refs[14:17], refs[17]
-    total, src, recv, mine, send1, recv1, send2, recv2 = refs[18:]
+    accs, acc_out, w_ref = refs[:7], refs[7], refs[8]
+    total, src, recv, mine, send1, recv1, send2, recv2 = refs[9:]
     me = lax.axis_index('dap')
 
     def peer(step):
@@ -487,10 +487,10 @@
         pl.semaphore_signal(barrier, inc=1, device_id=peer(step), device_id_type=pl.DeviceIdType.MESH)
     for blk in range(5):
         src[C * blk:C * (blk + 1)] = w_ref[C * blk:C * (blk + 1)].T
-    src[5 * C:VECS] = sum(ref[...] for ref in wout_refs[1:]) + wout_refs[0][...]
+    src[5 * C:VECS] = acc_out[...]
     rows = []
-    for ref, more in zip(accs, ((), (), (), osc_refs, (), (), bg_refs)):
-        rows += [ref[n] for n in range(4)] if len(ref.shape) > 2 else [sum((other[...] for other in more), ref[...])]
+    for ref in accs:
+        rows += [ref[n] for n in range(4)] if len(ref.shape) > 2 else [ref[...]]
     rows = [jnp.sum(val.T, axis=0, keepdims=True) for val in rows]
     src[VECS:] = jnp.concatenate(rows + [jnp.zeros((8 * SHARD - VECS - len(rows), C), F32)], axis=0)
     pl.semaphore_wait(barrier, 7)
@@ -537,8 +537,7 @@
     return [pl.BlockSpec(memory_space=pltpu.VMEM)] * count
 
 
-def sum_call(accs, wouts, acc_w):
-    args = [*accs, *wouts, acc_w]
+def sum_call(*args):
     total = pl.pallas_call(
         sum_kernel,
         in_specs=vmem_specs(len(args)),
@@ -629,9 +628,8 @@
                   [a_at[chunk_of[s & 6, h], h, s & 1] for h in range(2) for s in range(8)])
     d_z, acc_w, acc_bin, acc_isc, acc_ioff = in_call(ids, z_loc, dy_loc, mask_t, d_a[0], d_b, dg_chunks, w_t[:4 * C], *wide_in, w_cat)
 
-    wouts, oscs, bgs = zip(*sums)
-    accs = (acc_isc, acc_ioff, acc_bin, oscs[0], acc_ooff, acc_bout, bgs[0])
-    d_win, d_wgate, d_wout, *vecs = sum_call(accs, wouts + oscs[1:] + bgs[1:], acc_w)
+    acc_out, acc_osc, acc_bg = (sum(parts[1:], parts[0]) for parts in zip(*sums))
+    d_win, d_wgate, d_wout, *vecs = sum_call(acc_isc, acc_ioff, acc_bin, acc_osc, acc_ooff, acc_bout, acc_bg, acc_out, acc_w)
     d_bin, d_isc, d_ioff, d_osc, d_ooff, d_bout, d_bg = (vec.reshape(vec.size) for vec in vecs)
     return d_z, d_isc, d_ioff, d_win, d_bin, d_osc, d_ooff, d_wout, d_bout, d_wgate, d_bg
 

time: 667 us -> 686 us (1.028)
  waiting for transfers between devices: 237 us -> 253 us
    ppermute x34, waiting for transfers between devices: 237 us -> 253 us  [move(): return lax.ppermute(val, 'dap', [(d, d ^ flips) for d in range(8)])]
  transfers between devices with their start and end apart: 34 -> 34, of which waited for: 14 -> 14; matrix products, arithmetic and copies ran while one was open for 1% -> 2% of each run, Pallas kernels for 34% -> 33%
where the time goes in v5:
time: 686 us; the launch traced here: 685 us
  Pallas kernels  378 us (55%)
  waiting for transfers between devices  253 us (37%)
  starting transfers between devices  26.9 us (4%)
  local copies, waits for them, and re-layouts  18.7 us (3%)
  other arithmetic  7.84 us (1%)
    ppermute x34, waiting for transfers between devices, move(): return lax.ppermute(val, 'dap', [(d, d ^ flips) for d in range(8)])  253 us
    pallas_call x4, Pallas kernels, out_call(): pl.pallas_call(out_kernel, grid_spec=pltpu.PrefetchScalarGridSpec(num_sca...  97.6 us
    pallas_call x6, Pallas kernels, gated_call(): pl.pallas_call(functools.partial(gated_kernel, half_id), grid_spec=pltpu....  89.4 us
    pallas_call x3, Pallas kernels, da_call(): pl.pallas_call(functools.partial(da_kernel, len(do_chunks)), grid=(C // C...  54.9 us
    pallas_call x1, Pallas kernels, in_call(): pl.pallas_call(in_kernel, grid_spec=pltpu.PrefetchScalarGridSpec(num_scal...  51.9 us
    pallas_call x1, Pallas kernels, own_call(): pl.pallas_call(own_kernel, grid_spec=pltpu.PrefetchScalarGridSpec(num_sca...  39 us
    pallas_call x1, Pallas kernels, db_call(): pl.pallas_call(db_kernel, grid=(C // CK,), in_specs=[do_spec(*piece) for...  27.8 us
    ppermute x34, starting transfers between devices, move(): return lax.ppermute(val, 'dap', [(d, d ^ flips) for d in range(8)])  26.9 us
  transfers between devices with their start and end apart: 34, of which 14 were waited for; matrix products, arithmetic and copies ran while one was open for 2% of the time, Pallas kernels for 33%

profile of v5, /device:TPU:0, one launch (start us, length us, event | category | flops | bytes accessed | tf_op | source)
XLA Modules:
  0.0 685.0 jit_solution(15932056074463650325)
XLA Ops:
  2.0 1.5 convert_element_type.17.m_ref
  8.1 1.4 broadcast_in_dim.15.scale_ref
  9.5 1.4 broadcast_in_dim.16.offset_ref
  10.9 39.0 %own_rows.1 = (bf16[128,64,512]{2,1,0:T(8,128)(2,1)}, bf16[128,64,512]{2,1,0:T(8,128)(2,1)}, bf16[64,128,512]{2,1,0:T(8,128)(2,1)}, bf16[64,128,512]{2,1,0:T(8,1...) custom-call(s32[17]{0:T(128)} %stack.71.ids_ref, ...), custom_call_target="tpu_custom_call" | custom-call | flops 8589934592 | bytes 67108864 | tf_op jit(solution)/shard_map/own_rows/pallas_call | solution.py:193
  50.8 6.0 fusion.23
  56.8 2.5 collective-permute-start.1
  59.3 1.5 collective-permute-start.3
  65.4 24.0 %out_chain.4 = (bf16[128,64,128]{2,1,0:T(8,128)(2,1)}, bf16[64,128,128]{2,1,0:T(8,128)(2,1)}, bf16[2,128,16,128]{3,2,1,0:T(8,128)(2,1)}, bf16[2,128,16,128]{3,2,...) custom-call(s32[17]{0:T(128)} %get-tuple-element.112.ids_ref, ...), custom_call_target="tpu_custom_call" | custom-call | flops 8589934592 | bytes 67108864 | tf_op jit(solution)/shard_map/out_chain/pallas_call | solution.py:313
  89.3 62.8 %collective-permute-done.2.m_ref = bf16[64,512]{1,0:T(8,128)(2,1)S(1)} collective-permute-done((bf16[64,512]{1,0:T(8,128)(2,1)S(1)}, bf16[64,512]{1,0:T(8,128)(2,1)S(1)}, u32[]{:S(2)}, u32[]{:S(2)}) %collective-permute-start.2) | collective-permute-done | bytes 65568 | tf_op jit(solution)/shard_map/ppermute | solution.py:588
  152.7 14.8 %gated_rows.6 = (bf16[128,32,512]{2,1,0:T(8,128)(2,1)}, bf16[128,32,512]{2,1,0:T(8,128)(2,1)}, s32[17]{0:T(128)}) custom-call(s32[17]{0:T(128)} %get-tuple-element.118.ids_ref, bf16[32,512,128]{2,1,0:T(8,128)(2,1)} %collective-permute-done.1.z_ref, bf16[64,512]{1,0:T(8,128)(2,1)} %copy-done.29, bf16[512,144]{1,0:T(8,128)(2,1)} %copy.27.w_ref, ...), custom_call_target="tpu_custom_call" | custom-call | flops 8589934592 | bytes 67108864 | tf_op jit(solution)/shard_map/gated_rows/pallas_call | solution.py:132
  168.2 14.9 %gated_rows.7 = (bf16[128,32,512]{2,1,0:T(8,128)(2,1)}, bf16[128,32,512]{2,1,0:T(8,128)(2,1)}, s32[17]{0:T(128)}) custom-call(s32[17]{0:T(128)} %get-tuple-element.119.ids_ref, bf16[32,512,128]{2,1,0:T(8,128)(2,1)} %collective-permute-done.3.z_ref, bf16[64,512]{1,0:T(8,128)(2,1)} %copy-done.30, bf16[512,144]{1,0:T(8,128)(2,1)} %copy.27.w_ref, ...), custom_call_target="tpu_custom_call" | custom-call | flops 8589934592 | bytes 67108864 | tf_op jit(solution)/shard_map/gated_rows/pallas_call | solution.py:132
  183.5 1.8 collective-permute-start.7
  185.3 1.5 collective-permute-start.9
  187.0 3.5 collective-permute-done.6.b_par1.refs_9_
  190.5 1.7 collective-permute-start.13
  192.2 4.3 collective-permute-done.5.b_par0.refs_8_
  196.7 24.4 %out_chain.5 = (bf16[128,64,128]{2,1,0:T(8,128)(2,1)}, bf16[64,128,128]{2,1,0:T(8,128)(2,1)}, bf16[128,16,128]{2,1,0:T(8,128)(2,1)}, bf16[128,16,128]{2,1,0:T(8,...) custom-call(s32[17]{0:T(128)} %get-tuple-element.120.ids_ref, ...), custom_call_target="tpu_custom_call" | custom-call | flops 8589934592 | bytes 67108864 | tf_op jit(solution)/shard_map/out_chain/pallas_call | solution.py:313
  221.1 59.0 %collective-permute-done.8.m_ref = bf16[64,512]{1,0:T(8,128)(2,1)S(1)} collective-permute-done((bf16[64,512]{1,0:T(8,128)(2,1)S(1)}, bf16[64,512]{1,0:T(8,128)(2,1)S(1)}, u32[]{:S(2)}, u32[]{:S(2)}) %collective-permute-start.8) | collective-permute-done | bytes 65568 | tf_op jit(solution)/shard_map/ppermute | solution.py:588
  280.7 15.1 %gated_rows.8 = (bf16[128,32,512]{2,1,0:T(8,128)(2,1)}, bf16[128,32,512]{2,1,0:T(8,128)(2,1)}, s32[17]{0:T(128)}) custom-call(s32[17]{0:T(128)} %get-tuple-element.123.ids_ref, bf16[32,512,128]{2,1,0:T(8,128)(2,1)} %collective-permute-done.7.z_ref, bf16[64,512]{1,0:T(8,128)(2,1)} %copy-done.31, bf16[512,144]{1,0:T(8,128)(2,1)} %copy.27.w_ref, ...), custom_call_target="tpu_custom_call" | custom-call | flops 8589934592 | bytes 67108864 | tf_op jit(solution)/shard_map/gated_rows/pallas_call | solution.py:132
  295.8 14.8 %gated_rows.9 = (bf16[128,32,512]{2,1,0:T(8,128)(2,1)}, bf16[128,32,512]{2,1,0:T(8,128)(2,1)}, s32[17]{0:T(128)}) custom-call(s32[17]{0:T(128)} %get-tuple-element.124.ids_ref, bf16[32,512,128]{2,1,0:T(8,128)(2,1)} %collective-permute-done.9.z_ref, bf16[64,512]{1,0:T(8,128)(2,1)} %copy-done.31, bf16[512,144]{1,0:T(8,128)(2,1)} %copy.27.w_ref, ...), custom_call_target="tpu_custom_call" | custom-call | flops 8589934592 | bytes 67108864 | tf_op jit(solution)/shard_map/gated_rows/pallas_call | solution.py:132
  311.1 1.8 collective-permute-start.12
  312.9 56.2 %collective-permute-done.13.z_ref = bf16[32,512,128]{2,1,0:T(8,128)(2,1)} collective-permute-done((bf16[32,512,128]{2,1,0:T(8,128)(2,1)}, bf16[32,512,128]{2,1,0:T(8,128)(2,1)}, u32[]{:S(2)}, u32[]{:S(2)}) %collective-permute-start.13) | collective-permute-done | bytes 4194336 | tf_op jit(solution)/shard_map/ppermute | solution.py:588
  369.7 24.6 %out_chain.6 = (bf16[128,64,128]{2,1,0:T(8,128)(2,1)}, bf16[64,128,128]{2,1,0:T(8,128)(2,1)}, bf16[2,128,16,128]{3,2,1,0:T(8,128)(2,1)}, bf16[2,128,16,128]{3,2,...) custom-call(s32[17]{0:T(128)} %get-tuple-element.125.ids_ref, ...), custom_call_target="tpu_custom_call" | custom-call | flops 8589934592 | bytes 67108864 | tf_op jit(solution)/shard_map/out_chain/pallas_call | solution.py:313
  394.2 9.8 %collective-permute-done.12.z_ref = bf16[32,512,128]{2,1,0:T(8,128)(2,1)} collective-permute-done((bf16[32,512,128]{2,1,0:T(8,128)(2,1)}, bf16[32,512,128]{2,1,0:T(8,128)(2,1)}, u32[]{:S(2)}, u32[]{:S(2)}) %collective-permute-start.12) | collective-permute-done | bytes 4194336 | tf_op jit(solution)/shard_map/ppermute | solution.py:588
  404.0 14.8 %gated_rows.10 = (bf16[128,32,512]{2,1,0:T(8,128)(2,1)}, bf16[128,32,512]{2,1,0:T(8,128)(2,1)}, s32[17]{0:T(128)}) custom-call(s32[17]{0:T(128)} %get-tuple-element.128.ids_ref, bf16[32,512,128]{2,1,0:T(8,128)(2,1)} %collective-permute-done.12.z_ref, bf16[64,512]{1,0:T(8,128)(2,1)} %copy-done.30, bf16[512,144]{1,0:T(8,128)(2,1)} %copy.27.w_ref, ...), custom_call_target="tpu_custom_call" | custom-call | flops 8589934592 | bytes 67108864 | tf_op jit(solution)/shard_map/gated_rows/pallas_call | solution.py:132
  418.8 15.0 %gated_rows.11 = (bf16[128,32,512]{2,1,0:T(8,128)(2,1)}, bf16[128,32,512]{2,1,0:T(8,128)(2,1)}, s32[17]{0:T(128)}) custom-call(s32[17]{0:T(128)} %get-tuple-element.129.ids_ref, bf16[32,512,128]{2,1,0:T(8,128)(2,1)} %collective-permute-done.13.z_ref, bf16[64,512]{1,0:T(8,128)(2,1)} %copy-done.29, bf16[512,144]{1,0:T(8,128)(2,1)} %copy.27.w_ref, ...), custom_call_target="tpu_custom_call" | custom-call | flops 8589934592 | bytes 67108864 | tf_op jit(solution)/shard_map/gated_rows/pallas_call | solution.py:132
  434.4 1.7 collective-permute-start.17
  436.2 13.0 %collective-permute-done.17.refs_2_ = bf16[128,16,128]{2,1,0:T(8,128)(2,1)S(1)} collective-permute-done((bf16[128,16,128]{2,1,0:T(8,128)(2,1)S(1)}, bf16[128,16,128]{2,1,0:T(8,128)(2,1)S(1)}, u32[]{:S(2)}, u32[]{:S(2)}) %collective-permute-start.17) | collective-permute-done | bytes 524320 | tf_op jit(solution)/shard_map/ppermute | solution.py:588
  449.2 1.7 collective-permute-start.25
  450.9 8.5 %collective-permute-done.18.refs_3_ = bf16[128,16,128]{2,1,0:T(8,128)(2,1)S(1)} collective-permute-done((bf16[128,16,128]{2,1,0:T(8,128)(2,1)}, bf16[128,16,128]{2,1,0:T(8,128)(2,1)S(1)}, u32[]{:S(2)}, u32[]{:S(2)}) %collective-permute-start.18) | collective-permute-done | bytes 524320 | tf_op jit(solution)/shard_map/ppermute | solution.py:588
  459.4 2.0 collective-permute-start.26
  462.3 11.2 %collective-permute-done.26.refs_13_ = bf16[128,16,128]{2,1,0:T(8,128)(2,1)S(1)} collective-permute-done((bf16[128,16,128]{2,1,0:T(8,128)(2,1)}, bf16[128,16,128]{2,1,0:T(8,128)(2,1)S(1)}, u32[]{:S(2)}, u32[]{:S(2)}) %collective-permute-start.26) | collective-permute-done | bytes 524320 | tf_op jit(solution)/shard_map/ppermute | solution.py:588
  474.0 20.2 %grad_a.3.refs_5_ = f32[128,64,512]{2,1,0:T(8,128)} custom-call(bf16[128,64,128]{2,1,0:T(8,128)(2,1)} %get-tuple-element.136.refs_0_, bf16[128,64,128]{2,1,0:T(8,128)(2,1)} %get-tuple-element.137.refs_1_, bf16[128,64,512]{2,1,0:T(8,128)(2,1)} %get-tuple-element.114.b_own0.b_own1.refs_2_.refs_3_, ...), custom_call_target="tpu_custom_call" | custom-call | flops 8589934592 | bytes 67108864 | tf_op jit(solution)/shard_map/grad_a/pallas_call | solution.py:347
  494.2 18.6 %grad_a.4.refs_5_ = f32[128,64,512]{2,1,0:T(8,128)} custom-call(bf16[128,64,128]{2,1,0:T(8,128)(2,1)} %get-tuple-element.135.refs_0_, bf16[128,32,512]{2,1,0:T(8,128)(2,1)} %get-tuple-element.126.b_own0.refs_1_, bf16[128,32,512]{2,1,0:T(8,128)(2,1)} %get-tuple-element.127.b_own1.refs_2_, bf16[128,32,512]{2,1,0:T(8,128)(2,1)} %collective-permute-done.10.b_par0.refs_3_, ...), custom_call_target="tpu_custom_call" | custom-call | flops 8589934592 | bytes 67108864 | tf_op jit(solution)/shard_map/grad_a/pallas_call | solution.py:347
  512.8 2.4 collective-permute-start.21
  515.6 24.7 %out_chain.7 = (bf16[128,64,128]{2,1,0:T(8,128)(2,1)}, bf16[64,128,128]{2,1,0:T(8,128)(2,1)}, bf16[128,16,128]{2,1,0:T(8,128)(2,1)}, bf16[128,16,128]{2,1,0:T(8,...) custom-call(s32[17]{0:T(128)} %get-tuple-element.130.ids_ref, ...), custom_call_target="tpu_custom_call" | custom-call | flops 8589934592 | bytes 67108864 | tf_op jit(solution)/shard_map/out_chain/pallas_call | solution.py:313
  540.3 1.5 add_add_fusion.2.refs_3_
  541.8 1.5 add_add_fusion
  543.3 1.5 collective-permute-start.19
  545.1 16.2 %collective-permute-done.22.refs_7_.refs_15_ = bf16[2,128,16,128]{3,2,1,0:T(8,128)(2,1)S(1)} collective-permute-done((bf16[2,128,16,128]{3,2,1,0:T(8,128)(2,1)}, bf16[2,128,16,128]{3,2,1,0:T(8,128)(2,1)S(1)}, u32[]{:S(2)}, u32[]{:S(2)}) %collective-permute-start.22) | collective-permute-done | bytes 1048608 | tf_op jit(solution)/shard_map/ppermute | solution.py:588
  561.2 1.5 collective-permute-start.23
  563.0 16.1 %grad_a.5.da_ref = bf16[128,64,512]{2,1,0:T(8,128)(2,1)} custom-call(bf16[128,64,128]{2,1,0:T(8,128)(2,1)} %get-tuple-element.134.refs_0_, bf16[128,32,512]{2,1,0:T(8,128)(2,1)} %get-tuple-element.131.b_own0.refs_1_, bf16[128,32,512]{2,1,0:T(8,128)(2,1)} %get-tuple-element.132.b_own1.refs_2_, bf16[128,32,512]{2,1,0:T(8,128)(2,1)} %collective-permute-done.14.b_par0.refs_3_, ...), custom_call_target="tpu_custom_call" | custom-call | flops 8589934592 | bytes 67108864 | tf_op jit(solution)/shard_map/grad_a/pallas_call | solution.py:347
  579.2 5.0 collective-permute-done.20.refs_5_
  584.1 2.3 collective-permute-done.24.refs_11_
  586.5 27.8 %grad_b.1.db_ref = bf16[128,64,512]{2,1,0:T(8,128)(2,1)} custom-call(bf16[2,128,16,128]{3,2,1,0:T(8,128)(2,1)} %get-tuple-element.138.refs_0_.refs_8_, bf16[2,128,16,128]{3,2,1,0:T(8,128)(2,1)} %copy-done, bf16[128,16,128]{2,1,0:T(8,128)(2,1)} %copy-done.4, bf16[128,16,128]{2,1,0:T(8,128)(2,1)} %copy-done.5, bf16[128,16,128]{2,1,0:T(8,128)(2,1)} %copy-done.8, ...), custom_call_target="tpu_custom_call" | custom-call | flops 8589934592 | bytes 67108864 | tf_op jit(solution)/shard_map/grad_b/pallas_call | solution.py:380
  615.9 51.9 %in_backward.1 = (bf16[64,512,128]{2,1,0:T(8,128)(2,1)}, f32[640,128]{1,0:T(8,128)}, f32[4,128,128]{2,1,0:T(8,128)}, f32[128,128]{1,0:T(8,128)}, f32[128,128]{1,0:T(8,128)}) custom-call(s32[17]{0:T(128)} %get-tuple-element.133.ids_ref, bf16[64,512,128]{2,1,0:T(8,128)(2,1)} %z_ref.3, bf16[64,512,128]{2,1,0:T(8,128)(2,1)} %dy_ref.3, ...), custom_call_target="tpu_custom_call" | custom-call | flops 8589934592 | bytes 67108864 | tf_op jit(solution)/shard_map/in_backward/pallas_call | solution.py:454
  667.8 15.4 %sum_grads.1.total = bf16[896,128]{1,0:T(8,128)(2,1)} custom-call(f32[128,128]{1,0:T(8,128)} %get-tuple-element.161.refs_0_, f32[128,128]{1,0:T(8,128)} %get-tuple-element.162.refs_1_, f32[4,128,128]{2,1,0:T(8,128)} %get-tuple-element.163.refs_2_, f32[128,128]{1,0:T(8,128)} %add_add_fusion.2.refs_3_, f32[128,128]{1,0:T(8,128)} %get-tuple-element.168.refs_4_, ...), custom_call_target="tpu_custom_call" | custom-call | flops 8589934592 | bytes 67108864 | tf_op jit(solution)/shard_map/sum_grads/pallas_call | solution.py:541
  683.2 1.7 split_grads.1
  (131 shorter events, 19.7 us)
Async XLA Ops:
  50.0 14.0 %collective-permute-start = (bf16[128,64,512]{2,1,0:T(8,128)(2,1)}, bf16[128,64,512]{2,1,0:T(8,128)(2,1)}, u32[]{:S(2)}, u32[]{:S(2)}) collective-permute-start(bf16[128,64,512]{2,1,0:T(8,128)(2,1)} %get-tuple-element.114.b_own0.b_own1.refs_2_.refs_3_), channel_id=1, source_target_pairs={{0,1},{1,0},{2,3},{3,2},{4,5},{5,4},{6,7},{7,6}} | collective-permute-start | bytes 25165832 | tf_op jit(solution)/shard_map/ppermute | solution.py:588
  56.8 95.3 %collective-permute-start.1 = (bf16[32,512,128]{2,1,0:T(8,128)(2,1)}, bf16[32,512,128]{2,1,0:T(8,128)(2,1)}, u32[]{:S(2)}, u32[]{:S(2)}) collective-permute-start(bf16[32,512,128]{2,1,0:T(8,128)(2,1)} %get-tuple-element.190), channel_id=1, source_target_pairs={{0,2},{1,3},{2,0},{3,1},{4,6},{5,7},{6,4},{7,5}} | collective-permute-start | bytes 12582920 | tf_op jit(solution)/shard_map/ppermute | solution.py:588
  59.3 108.3 %collective-permute-start.3 = (bf16[32,512,128]{2,1,0:T(8,128)(2,1)}, bf16[32,512,128]{2,1,0:T(8,128)(2,1)}, u32[]{:S(2)}, u32[]{:S(2)}) collective-permute-start(bf16[32,512,128]{2,1,0:T(8,128)(2,1)} %get-tuple-element.189), channel_id=1, source_target_pairs={{0,4},{1,5},{2,6},{3,7},{4,0},{5,1},{6,2},{7,3}} | collective-permute-start | bytes 12582920 | tf_op jit(solution)/shard_map/ppermute | solution.py:588
  60.8 106.7 %collective-permute-start.4 = (bf16[64,512]{1,0:T(8,128)(2,1)S(1)}, bf16[64,512]{1,0:T(8,128)(2,1)S(1)}, u32[]{:S(2)}, u32[]{:S(2)}) collective-permute-start(bf16[64,512]{1,0:T(8,128)(2,1)S(1)} %copy-done.11), channel_id=1, source_target_pairs={{0,4},{1,5},{2,6},{3,7},{4,0},{5,1},{6,2},{7,3}} | collective-permute-start | bytes 196616 | tf_op jit(solution)/shard_map/ppermute | solution.py:588
  61.3 90.8 %collective-permute-start.2 = (bf16[64,512]{1,0:T(8,128)(2,1)S(1)}, bf16[64,512]{1,0:T(8,128)(2,1)S(1)}, u32[]{:S(2)}, u32[]{:S(2)}) collective-permute-start(bf16[64,512]{1,0:T(8,128)(2,1)S(1)} %copy-done.11), channel_id=1, source_target_pairs={{0,2},{1,3},{2,0},{3,1},{4,6},{5,7},{6,4},{7,5}} | collective-permute-start | bytes 196616 | tf_op jit(solution)/shard_map/ppermute | solution.py:588
  183.0 7.5 %collective-permute-start.6 = (bf16[128,32,512]{2,1,0:T(8,128)(2,1)}, bf16[128,32,512]{2,1,0:T(8,128)(2,1)}, u32[]{:S(2)}, u32[]{:S(2)}) collective-permute-start(bf16[128,32,512]{2,1,0:T(8,128)(2,1)} %get-tuple-element.122.b_own1.refs_7_), channel_id=1, source_target_pairs={{0,1},{1,0},{2,3},{3,2},{4,5},{5,4},{6,7},{7,6}} | collective-permute-start | bytes 12582920 | tf_op jit(solution)/shard_map/ppermute | solution.py:588
  183.0 13.5 %collective-permute-start.5 = (bf16[128,32,512]{2,1,0:T(8,128)(2,1)}, bf16[128,32,512]{2,1,0:T(8,128)(2,1)}, u32[]{:S(2)}, u32[]{:S(2)}) collective-permute-start(bf16[128,32,512]{2,1,0:T(8,128)(2,1)} %get-tuple-element.121.b_own0.refs_6_), channel_id=1, source_target_pairs={{0,1},{1,0},{2,3},{3,2},{4,5},{5,4},{6,7},{7,6}} | collective-permute-start | bytes 12582920 | tf_op jit(solution)/shard_map/ppermute | solution.py:588
  183.5 96.5 %collective-permute-start.7 = (bf16[32,512,128]{2,1,0:T(8,128)(2,1)}, bf16[32,512,128]{2,1,0:T(8,128)(2,1)}, u32[]{:S(2)}, u32[]{:S(2)}) collective-permute-start(bf16[32,512,128]{2,1,0:T(8,128)(2,1)} %collective-permute-done.1.z_ref), channel_id=1, source_target_pairs={{0,4},{1,5},{2,6},{3,7},{4,0},{5,1},{6,2},{7,3}} | collective-permute-start | bytes 12582920 | tf_op jit(solution)/shard_map/ppermute | solution.py:588
  185.3 110.5 %collective-permute-start.9 = (bf16[32,512,128]{2,1,0:T(8,128)(2,1)}, bf16[32,512,128]{2,1,0:T(8,128)(2,1)}, u32[]{:S(2)}, u32[]{:S(2)}) collective-permute-start(bf16[32,512,128]{2,1,0:T(8,128)(2,1)} %collective-permute-done.3.z_ref), channel_id=1, source_target_pairs={{0,2},{1,3},{2,0},{3,1},{4,6},{5,7},{6,4},{7,5}} | collective-permute-start | bytes 12582920 | tf_op jit(solution)/shard_map/ppermute | solution.py:588
  186.8 93.3 %collective-permute-start.8 = (bf16[64,512]{1,0:T(8,128)(2,1)S(1)}, bf16[64,512]{1,0:T(8,128)(2,1)S(1)}, u32[]{:S(2)}, u32[]{:S(2)}) collective-permute-start(bf16[64,512]{1,0:T(8,128)(2,1)S(1)} %copy-done.11), channel_id=1, source_target_pairs={{0,6},{1,7},{2,4},{3,5},{4,2},{5,3},{6,0},{7,1}} | collective-permute-start | bytes 196616 | tf_op jit(solution)/shard_map/ppermute | solution.py:588
  190.5 178.6 %collective-permute-start.13 = (bf16[32,512,128]{2,1,0:T(8,128)(2,1)}, bf16[32,512,128]{2,1,0:T(8,128)(2,1)}, u32[]{:S(2)}, u32[]{:S(2)}) collective-permute-start(bf16[32,512,128]{2,1,0:T(8,128)(2,1)} %get-tuple-element.189), channel_id=1, source_target_pairs={{0,2},{1,3},{2,0},{3,1},{4,6},{5,7},{6,4},{7,5}} | collective-permute-start | bytes 12582920 | tf_op jit(solution)/shard_map/ppermute | solution.py:588
  196.5 237.2 %collective-permute-start.27 = (bf16[128,64,512]{2,1,0:T(8,128)(2,1)}, bf16[128,64,512]{2,1,0:T(8,128)(2,1)}, u32[]{:S(2)}, u32[]{:S(2)}) collective-permute-start(bf16[128,64,512]{2,1,0:T(8,128)(2,1)} %get-tuple-element.113.a_ref.refs_16_.refs_24_), channel_id=1, source_target_pairs={{0,1},{1,0},{2,3},{3,2},{4,5},{5,4},{6,7},{7,6}} | collective-permute-start | bytes 25165832 | tf_op jit(solution)/shard_map/ppermute | solution.py:588
  310.6 58.5 %collective-permute-start.11 = (bf16[128,32,512]{2,1,0:T(8,128)(2,1)}, bf16[128,32,512]{2,1,0:T(8,128)(2,1)}, u32[]{:S(2)}, u32[]{:S(2)}) collective-permute-start(bf16[128,32,512]{2,1,0:T(8,128)(2,1)} %get-tuple-element.127.b_own1.refs_2_), channel_id=1, source_target_pairs={{0,1},{1,0},{2,3},{3,2},{4,5},{5,4},{6,7},{7,6}} | collective-permute-start | bytes 12582920 | tf_op jit(solution)/shard_map/ppermute | solution.py:588
  310.6 59.0 %collective-permute-start.10 = (bf16[128,32,512]{2,1,0:T(8,128)(2,1)}, bf16[128,32,512]{2,1,0:T(8,128)(2,1)}, u32[]{:S(2)}, u32[]{:S(2)}) collective-permute-start(bf16[128,32,512]{2,1,0:T(8,128)(2,1)} %get-tuple-element.126.b_own0.refs_1_), channel_id=1, source_target_pairs={{0,1},{1,0},{2,3},{3,2},{4,5},{5,4},{6,7},{7,6}} | collective-permute-start | bytes 12582920 | tf_op jit(solution)/shard_map/ppermute | solution.py:588
  311.1 92.9 %collective-permute-start.12 = (bf16[32,512,128]{2,1,0:T(8,128)(2,1)}, bf16[32,512,128]{2,1,0:T(8,128)(2,1)}, u32[]{:S(2)}, u32[]{:S(2)}) collective-permute-start(bf16[32,512,128]{2,1,0:T(8,128)(2,1)} %get-tuple-element.190), channel_id=1, source_target_pairs={{0,4},{1,5},{2,6},{3,7},{4,0},{5,1},{6,2},{7,3}} | collective-permute-start | bytes 12582920 | tf_op jit(solution)/shard_map/ppermute | solution.py:588
  369.1 65.3 %collective-permute-start.32 = (bf16[128,32,512]{2,1,0:T(8,128)(2,1)}, bf16[128,32,512]{2,1,0:T(8,128)(2,1)}, u32[]{:S(2)}, u32[]{:S(2)}) collective-permute-start(bf16[128,32,512]{2,1,0:T(8,128)(2,1)} %get-tuple-element.154.refs_28_), channel_id=1, source_target_pairs={{0,1},{1,0},{2,3},{3,2},{4,5},{5,4},{6,7},{7,6}} | collective-permute-start | bytes 12582920 | tf_op jit(solution)/shard_map/ppermute | solution.py:588
  369.1 66.9 %collective-permute-start.28 = (bf16[128,32,512]{2,1,0:T(8,128)(2,1)}, bf16[128,32,512]{2,1,0:T(8,128)(2,1)}, u32[]{:S(2)}, u32[]{:S(2)}) collective-permute-start(bf16[128,32,512]{2,1,0:T(8,128)(2,1)} %get-tuple-element.150.refs_18_), channel_id=1, source_target_pairs={{0,1},{1,0},{2,3},{3,2},{4,5},{5,4},{6,7},{7,6}} | collective-permute-start | bytes 12582920 | tf_op jit(solution)/shard_map/ppermute | solution.py:588
  369.6 104.2 %collective-permute-start.33 = (bf16[128,32,512]{2,1,0:T(8,128)(2,1)}, bf16[128,32,512]{2,1,0:T(8,128)(2,1)}, u32[]{:S(2)}, u32[]{:S(2)}) collective-permute-start(bf16[128,32,512]{2,1,0:T(8,128)(2,1)} %get-tuple-element.155.refs_30_), channel_id=1, source_target_pairs={{0,1},{1,0},{2,3},{3,2},{4,5},{5,4},{6,7},{7,6}} | collective-permute-start | bytes 12582920 | tf_op jit(solution)/shard_map/ppermute | solution.py:588
  369.7 34.3 %copy-start.26 = (bf16[2,128,16,128]{3,2,1,0:T(8,128)(2,1)S(1)}, bf16[2,128,16,128]{3,2,1,0:T(8,128)(2,1)}, u32[]{:S(2)}) copy-start(bf16[2,128,16,128]{3,2,1,0:T(8,128)(2,1)} %get-tuple-element.139) | copy-start | bytes 3145732
  404.0 30.3 %collective-permute-start.16 = (bf16[2,128,16,128]{3,2,1,0:T(8,128)(2,1)S(1)}, bf16[2,128,16,128]{3,2,1,0:T(8,128)(2,1)S(1)}, u32[]{:S(2)}, u32[]{:S(2)}) collective-permute-start(bf16[2,128,16,128]{3,2,1,0:T(8,128)(2,1)S(1)} %copy-done.26), channel_id=1, source_target_pairs={{0,1},{1,0},{2,3},{3,2},{4,5},{5,4},{6,7},{7,6}} | collective-permute-start | bytes 3145736 | tf_op jit(solution)/shard_map/ppermute | solution.py:588
  433.8 79.1 %collective-permute-start.15 = (bf16[128,32,512]{2,1,0:T(8,128)(2,1)}, bf16[128,32,512]{2,1,0:T(8,128)(2,1)}, u32[]{:S(2)}, u32[]{:S(2)}) collective-permute-start(bf16[128,32,512]{2,1,0:T(8,128)(2,1)} %get-tuple-element.132.b_own1.refs_2_), channel_id=1, source_target_pairs={{0,1},{1,0},{2,3},{3,2},{4,5},{5,4},{6,7},{7,6}} | collective-permute-start | bytes 12582920 | tf_op jit(solution)/shard_map/ppermute | solution.py:588
  434.3 59.8 %copy-start = (bf16[2,128,16,128]{3,2,1,0:T(8,128)(2,1)}, bf16[2,128,16,128]{3,2,1,0:T(8,128)(2,1)S(1)}, u32[]{:S(2)}) copy-start(bf16[2,128,16,128]{3,2,1,0:T(8,128)(2,1)S(1)} %collective-permute-done.16.refs_1_.refs_9_) | copy-start | bytes 3145732
  434.3 80.9 %collective-permute-start.14 = (bf16[128,32,512]{2,1,0:T(8,128)(2,1)}, bf16[128,32,512]{2,1,0:T(8,128)(2,1)}, u32[]{:S(2)}, u32[]{:S(2)}) collective-permute-start(bf16[128,32,512]{2,1,0:T(8,128)(2,1)} %get-tuple-element.131.b_own0.refs_1_), channel_id=1, source_target_pairs={{0,1},{1,0},{2,3},{3,2},{4,5},{5,4},{6,7},{7,6}} | collective-permute-start | bytes 12582920 | tf_op jit(solution)/shard_map/ppermute | solution.py:588
  434.4 14.8 %collective-permute-start.17 = (bf16[128,16,128]{2,1,0:T(8,128)(2,1)S(1)}, bf16[128,16,128]{2,1,0:T(8,128)(2,1)S(1)}, u32[]{:S(2)}, u32[]{:S(2)}) collective-permute-start(bf16[128,16,128]{2,1,0:T(8,128)(2,1)S(1)} %copy-done.28), channel_id=1, source_target_pairs={{0,2},{1,3},{2,0},{3,1},{4,6},{5,7},{6,4},{7,5}} | collective-permute-start | bytes 1572872 | tf_op jit(solution)/shard_map/ppermute | solution.py:588
  436.0 23.4 %collective-permute-start.18 = (bf16[128,16,128]{2,1,0:T(8,128)(2,1)}, bf16[128,16,128]{2,1,0:T(8,128)(2,1)S(1)}, u32[]{:S(2)}, u32[]{:S(2)}) collective-permute-start(bf16[128,16,128]{2,1,0:T(8,128)(2,1)} %get-tuple-element.141), channel_id=1, source_target_pairs={{0,3},{1,2},{2,1},{3,0},{4,7},{5,6},{6,5},{7,4}} | collective-permute-start | bytes 1572872 | tf_op jit(solution)/shard_map/ppermute | solution.py:588
  449.2 45.0 %copy-start.4 = (bf16[128,16,128]{2,1,0:T(8,128)(2,1)}, bf16[128,16,128]{2,1,0:T(8,128)(2,1)S(1)}, u32[]{:S(2)}) copy-start(bf16[128,16,128]{2,1,0:T(8,128)(2,1)S(1)} %collective-permute-done.17.refs_2_) | copy-start | bytes 1572868
  449.2 13.1 %collective-permute-start.25 = (bf16[128,16,128]{2,1,0:T(8,128)(2,1)}, bf16[128,16,128]{2,1,0:T(8,128)(2,1)S(1)}, u32[]{:S(2)}, u32[]{:S(2)}) collective-permute-start(bf16[128,16,128]{2,1,0:T(8,128)(2,1)} %get-tuple-element.148), channel_id=1, source_target_pairs={{0,4},{1,5},{2,6},{3,7},{4,0},{5,1},{6,2},{7,3}} | collective-permute-start | bytes 1572872 | tf_op jit(solution)/shard_map/ppermute | solution.py:588
  459.4 34.8 %copy-start.5 = (bf16[128,16,128]{2,1,0:T(8,128)(2,1)}, bf16[128,16,128]{2,1,0:T(8,128)(2,1)S(1)}, u32[]{:S(2)}) copy-start(bf16[128,16,128]{2,1,0:T(8,128)(2,1)S(1)} %collective-permute-done.18.refs_3_) | copy-start | bytes 1572868
  459.4 14.1 %collective-permute-start.26 = (bf16[128,16,128]{2,1,0:T(8,128)(2,1)}, bf16[128,16,128]{2,1,0:T(8,128)(2,1)S(1)}, u32[]{:S(2)}, u32[]{:S(2)}) collective-permute-start(bf16[128,16,128]{2,1,0:T(8,128)(2,1)} %get-tuple-element.149), channel_id=1, source_target_pairs={{0,5},{1,4},{2,7},{3,6},{4,1},{5,0},{6,3},{7,2}} | collective-permute-start | bytes 1572872 | tf_op jit(solution)/shard_map/ppermute | solution.py:588
  462.3 31.9 %copy-start.6 = (bf16[128,16,128]{2,1,0:T(8,128)(2,1)}, bf16[128,16,128]{2,1,0:T(8,128)(2,1)S(1)}, u32[]{:S(2)}) copy-start(bf16[128,16,128]{2,1,0:T(8,128)(2,1)S(1)} %collective-permute-done.25.refs_12_) | copy-start | bytes 1572868
  462.3 81.0 %collective-permute-start.30 = (bf16[128,32,512]{2,1,0:T(8,128)(2,1)}, bf16[128,32,512]{2,1,0:T(8,128)(2,1)}, u32[]{:S(2)}, u32[]{:S(2)}) collective-permute-start(bf16[128,32,512]{2,1,0:T(8,128)(2,1)} %get-tuple-element.152.refs_22_), channel_id=1, source_target_pairs={{0,1},{1,0},{2,3},{3,2},{4,5},{5,4},{6,7},{7,6}} | collective-permute-start | bytes 12582920 | tf_op jit(solution)/shard_map/ppermute | solution.py:588
  473.5 89.3 %collective-permute-start.31 = (bf16[128,32,512]{2,1,0:T(8,128)(2,1)}, bf16[128,32,512]{2,1,0:T(8,128)(2,1)}, u32[]{:S(2)}, u32[]{:S(2)}) collective-permute-start(bf16[128,32,512]{2,1,0:T(8,128)(2,1)} %get-tuple-element.153.refs_26_), channel_id=1, source_target_pairs={{0,1},{1,0},{2,3},{3,2},{4,5},{5,4},{6,7},{7,6}} | collective-permute-start | bytes 12582920 | tf_op jit(solution)/shard_map/ppermute | solution.py:588
  473.9 105.3 %collective-permute-start.29 = (bf16[128,32,512]{2,1,0:T(8,128)(2,1)}, bf16[128,32,512]{2,1,0:T(8,128)(2,1)}, u32[]{:S(2)}, u32[]{:S(2)}) collective-permute-start(bf16[128,32,512]{2,1,0:T(8,128)(2,1)} %get-tuple-element.151.refs_20_), channel_id=1, source_target_pairs={{0,1},{1,0},{2,3},{3,2},{4,5},{5,4},{6,7},{7,6}} | collective-permute-start | bytes 12582920 | tf_op jit(solution)/shard_map/ppermute | solution.py:588
  512.8 32.0 %collective-permute-start.21 = (bf16[2,128,16,128]{3,2,1,0:T(8,128)(2,1)S(1)}, bf16[2,128,16,128]{3,2,1,0:T(8,128)(2,1)S(1)}, u32[]{:S(2)}, u32[]{:S(2)}) collective-permute-start(bf16[2,128,16,128]{3,2,1,0:T(8,128)(2,1)S(1)} %copy-done.27), channel_id=1, source_target_pairs={{0,6},{1,7},{2,4},{3,5},{4,2},{5,3},{6,0},{7,1}} | collective-permute-start | bytes 3145736 | tf_op jit(solution)/shard_map/ppermute | solution.py:588
  515.2 46.0 %collective-permute-start.22 = (bf16[2,128,16,128]{3,2,1,0:T(8,128)(2,1)}, bf16[2,128,16,128]{3,2,1,0:T(8,128)(2,1)S(1)}, u32[]{:S(2)}, u32[]{:S(2)}) collective-permute-start(bf16[2,128,16,128]{3,2,1,0:T(8,128)(2,1)} %get-tuple-element.145), channel_id=1, source_target_pairs={{0,7},{1,6},{2,5},{3,4},{4,3},{5,2},{6,1},{7,0}} | collective-permute-start | bytes 3145736 | tf_op jit(solution)/shard_map/ppermute | solution.py:588
  515.5 26.2 %copy-start.12 = (f32[128,128]{1,0:T(8,128)S(1)}, f32[128,128]{1,0:T(8,128)}, u32[]{:S(2)}) copy-start(f32[128,128]{1,0:T(8,128)} %get-tuple-element.174) | copy-start | bytes 196612
  515.5 26.2 %copy-start.13 = (f32[128,128]{1,0:T(8,128)S(1)}, f32[128,128]{1,0:T(8,128)}, u32[]{:S(2)}) copy-start(f32[128,128]{1,0:T(8,128)} %get-tuple-element.170) | copy-start | bytes 196612
  515.5 26.2 %copy-start.15 = (f32[128,128]{1,0:T(8,128)S(1)}, f32[128,128]{1,0:T(8,128)}, u32[]{:S(2)}) copy-start(f32[128,128]{1,0:T(8,128)} %get-tuple-element.175) | copy-start | bytes 196612
  515.6 26.2 %copy-start.16 = (f32[128,128]{1,0:T(8,128)S(1)}, f32[128,128]{1,0:T(8,128)}, u32[]{:S(2)}) copy-start(f32[128,128]{1,0:T(8,128)} %get-tuple-element.171) | copy-start | bytes 196612
  515.6 26.2 %copy-start.18 = (f32[128,128]{1,0:T(8,128)S(1)}, f32[128,128]{1,0:T(8,128)}, u32[]{:S(2)}) copy-start(f32[128,128]{1,0:T(8,128)} %get-tuple-element.176) | copy-start | bytes 196612
  515.6 26.2 %copy-start.19 = (f32[128,128]{1,0:T(8,128)S(1)}, f32[128,128]{1,0:T(8,128)}, u32[]{:S(2)}) copy-start(f32[128,128]{1,0:T(8,128)} %get-tuple-element.172) | copy-start | bytes 196612
  543.3 35.8 %collective-permute-start.19 = (bf16[128,16,128]{2,1,0:T(8,128)(2,1)}, bf16[128,16,128]{2,1,0:T(8,128)(2,1)S(1)}, u32[]{:S(2)}, u32[]{:S(2)}) collective-permute-start(bf16[128,16,128]{2,1,0:T(8,128)(2,1)} %get-tuple-element.142), channel_id=1, source_target_pairs={{0,4},{1,5},{2,6},{3,7},{4,0},{5,1},{6,2},{7,3}} | collective-permute-start | bytes 1572872 | tf_op jit(solution)/shard_map/ppermute | solution.py:588
  544.9 34.3 %copy-start.1 = (bf16[2,128,16,128]{3,2,1,0:T(8,128)(2,1)}, bf16[2,128,16,128]{3,2,1,0:T(8,128)(2,1)S(1)}, u32[]{:S(2)}) copy-start(bf16[2,128,16,128]{3,2,1,0:T(8,128)(2,1)S(1)} %collective-permute-done.21.refs_6_.refs_14_) | copy-start | bytes 3145732
  544.9 39.3 %collective-permute-start.20 = (bf16[128,16,128]{2,1,0:T(8,128)(2,1)}, bf16[128,16,128]{2,1,0:T(8,128)(2,1)S(1)}, u32[]{:S(2)}, u32[]{:S(2)}) collective-permute-start(bf16[128,16,128]{2,1,0:T(8,128)(2,1)} %get-tuple-element.143), channel_id=1, source_target_pairs={{0,5},{1,4},{2,7},{3,6},{4,1},{5,0},{6,3},{7,2}} | collective-permute-start | bytes 1572872 | tf_op jit(solution)/shard_map/ppermute | solution.py:588
  561.2 22.9 %collective-permute-start.23 = (bf16[128,16,128]{2,1,0:T(8,128)(2,1)}, bf16[128,16,128]{2,1,0:T(8,128)(2,1)S(1)}, u32[]{:S(2)}, u32[]{:S(2)}) collective-permute-start(bf16[128,16,128]{2,1,0:T(8,128)(2,1)} %get-tuple-element.146), channel_id=1, source_target_pairs={{0,2},{1,3},{2,0},{3,1},{4,6},{5,7},{6,4},{7,5}} | collective-permute-start | bytes 1572872 | tf_op jit(solution)/shard_map/ppermute | solution.py:588
  562.8 23.6 %collective-permute-start.24 = (bf16[128,16,128]{2,1,0:T(8,128)(2,1)}, bf16[128,16,128]{2,1,0:T(8,128)(2,1)}, u32[]{:S(2)}, u32[]{:S(2)}) collective-permute-start(bf16[128,16,128]{2,1,0:T(8,128)(2,1)} %get-tuple-element.147), channel_id=1, source_target_pairs={{0,3},{1,2},{2,1},{3,0},{4,7},{5,6},{6,5},{7,4}} | collective-permute-start | bytes 1572872 | tf_op jit(solution)/shard_map/ppermute | solution.py:588
  586.4 27.8 %copy-start.22 = (bf16[128]{0:T(256)(128)(2,1)S(1)}, bf16[128]{0:T(256)(128)(2,1)}, u32[]{:S(2)}) copy-start(bf16[128]{0:T(256)(128)(2,1)} %param.20) | copy-start | bytes 772
  586.4 28.7 %copy-start.23 = (bf16[128]{0:T(256)(128)(2,1)S(1)}, bf16[128]{0:T(256)(128)(2,1)}, u32[]{:S(2)}) copy-start(bf16[128]{0:T(256)(128)(2,1)} %param.21) | copy-start | bytes 772
  (19 other events, 224.1 us)
